TPU v7x, 256 devices: a whole 4x4x8 slice. The times are simulated.
256 devices in a mesh: unit: 4 (over y_lo, core), ep: 4 (over z_lo), fsdp: 16 (over z_hi, y_hi, x).
Axes of the slice: x: 4, y: 4 (y_hi: 2, y_lo: 2; y = y_hi * 2 + y_lo), z: 8 (z_hi: 2, z_lo: 4; z = z_hi * 4 + z_lo), core: 2. Of those that a mesh axis runs over, the one named last changes fastest.
Arguments:
- w_down: float32 [256, 1024, 2048], P(('unit', 'ep'), None, 'fsdp'), parts along dimension 0, may hold values from -0.25 to 0.25
- router_weight: float32 [8192, 64], P(('unit', 'fsdp'), 'ep'), parts along dimension 0, may hold values from -0.125 to 0.125
- router_gain: float32 [8192], P(('unit', 'fsdp')), parts along dimension 0, may hold values from 0.25 to 1.75
Outputs:
- serve_down: bfloat16 [256, 1024, 2048], P(('unit', 'ep'), 'fsdp'), parts along dimension 0
- scale_down: float32 [256, 1024], P(('unit', 'ep'), 'fsdp'), parts along dimension 0
- serve_router: bfloat16 [8192, 64], P('unit'), parts along dimension 0
There are 4 independent parts, one for each index of `unit`. A program takes and returns all parts, laid end to end along the dimension named above; each array names one. Nothing has to cross between parts.
All inputs are finite; a program needn't handle non-finite values. Where the computation divides by a largest or mean magnitude, that divisor is 1e-20 or more.
Results may differ from a plain program's by a relative error of at most 0.001.
Values may be sent and summed in bfloat16 or wider, within the bound.
No kernel may reach another device: no remote copies, remote signals or barrier semaphores. Data moves between devices by JAX's collectives and lax.ppermute only.
A program may use at most 64 MiB of HBM per device.

v0:
```python
import jax
import jax.numpy as jnp
from jax import lax
from jax.sharding import PartitionSpec as P

D_MODEL = 2048


def copy_for_each(shard, axis):
    length = lax.axis_size(axis)
    return lax.all_to_all(
        jnp.broadcast_to(shard[None], (length, *shard.shape)), axis, 0, 0, tiled=True
    )


def taken_together(shard, axis):
    return copy_for_each(shard, axis).sum(axis=0)


def cut_along(shard, dim, length):
    before, after = (shard.shape[:dim], shard.shape[dim + 1 :])
    return jnp.moveaxis(shard.reshape(*before, length, -1, *after), dim, 0)


def edges_of(length, count):
    unit = 8 if length >= 8 * count else 1
    return [length // unit * k // count * unit for k in range(1, count)]


def laid_out(tiles, dim):
    tiles = jnp.moveaxis(tiles, 0, dim)
    lengths = tiles.shape
    return tiles.reshape(*lengths[:dim], lengths[dim] * lengths[dim + 1], *lengths[dim + 2 :])


def exchange_in_pieces(shard, axis, pieces, split_dim, concat_dim):
    tiles = cut_along(shard, split_dim, lax.axis_size(axis))
    widest = max(range(1, max(2, tiles.ndim - 1)), key=lambda d: tiles.shape[d])
    outs = []
    for section in jnp.split(tiles, edges_of(tiles.shape[widest], pieces), axis=widest):
        if section.size:
            outs.append(lax.all_to_all(section, axis, split_axis=0, concat_axis=0, tiled=True))
    return laid_out(jnp.concatenate(outs, axis=widest), concat_dim)


def gathered_copies(shard, axis, dim):
    return laid_out(copy_for_each(shard, axis), dim)


def on_device(w_down, router_weight, router_gain):
    total_down = taken_together(jnp.sum(jnp.abs(w_down), axis=2), "fsdp")
    scale_down = total_down / D_MODEL
    narrow_down = (w_down / jnp.expand_dims(scale_down, 2)).astype(jnp.bfloat16)
    serve_down = exchange_in_pieces(narrow_down, "fsdp", 2, 1, 2)
    scale_down = lax.dynamic_slice_in_dim(
        scale_down, lax.axis_index("fsdp") * serve_down.shape[1], serve_down.shape[1], axis=1
    )
    part_router = (router_weight * router_gain[:, None]).astype(jnp.bfloat16)
    row_router = gathered_copies(part_router, "fsdp", 0)
    serve_router = gathered_copies(row_router, "ep", 1)
    return (serve_down, scale_down, serve_router)


def solution(mesh):
    return jax.shard_map(
        on_device,
        mesh=mesh,
        in_specs=(P(("unit", "ep"), None, "fsdp"), P(("unit", "fsdp"), "ep"), P(("unit", "fsdp"))),
        out_specs=(P(("unit", "ep"), "fsdp", None), P(("unit", "ep"), "fsdp"), P("unit", None)),
        check_vma=False,
    )
```

profile of v0, /device:TPU:34, one launch (start us, length us, event | category | flops | bytes accessed | tf_op | source)
XLA Modules:
  0.0 198.6 jit_solution(401176799986804132)
XLA Ops:
  0.6 0.7 multiply_convert_fusion
  1.3 0.6 broadcast_in_dim.9
  2.0 13.2 %all-to-all-start.3 = ((bf16[16,128,16]{1,2,0:T(8,128)(2,1)}), bf16[16,128,16]{1,2,0:T(8,128)(2,1)S(1)}, u32[]{:S(2)}, u32[]{:S(2)}) async-start(bf16[16,128,16]{1,2,0:T(8,128)(2,1)} %broadcast_in_dim.9), calls=%async_computation.3 | async-start | bytes 131072 | tf_op jit(solution)/shard_map/all_to_all | solution.py:11
  15.2 5.6 %abs_reduce_fusion = f32[16,1024]{1,0:T(8,128)S(1)} fusion(f32[16,1024,128]{2,1,0:T(8,128)} %param.3), kind=kLoop, calls=%fused_computation.1 | loop fusion | flops 4177920 | bytes 8454144 | tf_op jit(solution)/shard_map/reduce_sum | solution.py:51
  20.8 5.8 %all-to-all-done.3 = bf16[16,128,16]{1,2,0:T(8,128)(2,1)S(1)} async-done(((bf16[16,128,16]{1,2,0:T(8,128)(2,1)}), bf16[16,128,16]{1,2,0:T(8,128)(2,1)S(1)}, u32[]{:S(2)}, u32[]{:S(2)}) %all-to-all-start.3) | async-done | bytes 65568 | tf_op jit(solution)/shard_map/all_to_all | solution.py:11
  26.6 1.1 broadcast_in_dim.8
  27.6 6.3 %all-to-all-start = ((f32[16,16,1024]{2,1,0:T(8,128)}), f32[16,16,1024]{2,1,0:T(8,128)S(1)}, u32[]{:S(2)}, u32[]{:S(2)}) async-start(f32[16,16,1024]{2,1,0:T(8,128)} %broadcast_in_dim.8), calls=%async_computation | async-start | bytes 2097152 | tf_op jit(solution)/shard_map/all_to_all | solution.py:11
  33.9 31.5 %all-to-all-done = f32[16,16,1024]{2,1,0:T(8,128)S(1)} async-done(((f32[16,16,1024]{2,1,0:T(8,128)}), f32[16,16,1024]{2,1,0:T(8,128)S(1)}, u32[]{:S(2)}, u32[]{:S(2)}) %all-to-all-start) | async-done | bytes 1048608 | tf_op jit(solution)/shard_map/all_to_all | solution.py:11
  65.5 0.7 broadcast_in_dim.11
  66.2 3.7 %all-to-all-start.4 = ((bf16[4,2048,16]{1,2,0:T(8,128)(2,1)}), bf16[4,2048,16]{1,2,0:T(8,128)(2,1)S(1)}, u32[]{:S(2)}, u32[]{:S(2)}) async-start(bf16[4,2048,16]{1,2,0:T(8,128)(2,1)} %broadcast_in_dim.11), calls=%async_computation.4 | async-start | bytes 524288 | tf_op jit(solution)/shard_map/all_to_all | solution.py:11
  69.9 0.1 reduce_sum.19
  70.0 5.3 %divide_convert_fusion = bf16[16,1024,128]{2,1,0:T(8,128)(2,1)S(1)} fusion(f32[16,1024,128]{2,1,0:T(8,128)} %param.3, f32[16,1024]{1,0:T(8,128)S(1)} %broadcast_multiply_fusion), kind=kLoop, calls=%fused_computation | loop fusion | flops 4194304 | bytes 12648448 | tf_op jit(solution)/shard_map/convert_element_type | solution.py:53
  75.3 2.1 %fusion = (bf16[16,16,32,128]{3,2,0,1:T(8,128)(2,1)S(1)}, bf16[16,16,32,128]{3,2,0,1:T(8,128)(2,1)}) fusion(bf16[16,16,64,128]{3,2,0,1:T(8,128)(2,1)S(1)} %bitcast.17), kind=kLoop, calls=%fused_computation.8 | loop fusion | bytes 8388608 | tf_op jit(solution)/shard_map/split | solution.py:40
  77.3 1.8 copy.11
  79.2 0.0 all-to-all-done.4
  79.2 5.0 %all-to-all-start.1 = ((bf16[16,16,32,128]{3,2,1,0:T(8,128)(2,1)}), bf16[16,16,32,128]{3,2,1,0:T(8,128)(2,1)S(1)}, u32[]{:S(2)}, u32[]{:S(2)}) async-start(bf16[16,16,32,128]{3,2,1,0:T(8,128)(2,1)} %copy.11), calls=%async_computation.1 | async-start | bytes 4194304 | tf_op jit(solution)/shard_map/all_to_all | solution.py:42
  84.1 3.5 %copy.12 = bf16[16,16,32,128]{3,2,1,0:T(8,128)(2,1)} copy(bf16[16,16,32,128]{3,2,0,1:T(8,128)(2,1)} %get-tuple-element.4) | data formatting | bytes 4194304 | tf_op jit(solution)/shard_map/split | solution.py:40
  87.6 50.1 %all-to-all-done.1 = bf16[16,16,32,128]{3,2,1,0:T(8,128)(2,1)S(1)} async-done(((bf16[16,16,32,128]{3,2,1,0:T(8,128)(2,1)}), bf16[16,16,32,128]{3,2,1,0:T(8,128)(2,1)S(1)}, u32[]{:S(2)}, u32[]{:S(2)}) %all-to-all-start.1) | async-done | bytes 2097184 | tf_op jit(solution)/shard_map/all_to_all | solution.py:42
  137.8 4.9 %all-to-all-start.2 = ((bf16[16,16,32,128]{3,2,1,0:T(8,128)(2,1)}), bf16[16,16,32,128]{3,2,1,0:T(8,128)(2,1)}, u32[]{:S(2)}, u32[]{:S(2)}) async-start(bf16[16,16,32,128]{3,2,1,0:T(8,128)(2,1)} %copy.12), calls=%async_computation.2 | async-start | bytes 4194304 | tf_op jit(solution)/shard_map/all_to_all | solution.py:42
  142.7 0.7 constant_dynamic-slice_fusion
  143.3 51.0 %all-to-all-done.2 = bf16[16,16,32,128]{3,2,1,0:T(8,128)(2,1)} async-done(((bf16[16,16,32,128]{3,2,1,0:T(8,128)(2,1)}), bf16[16,16,32,128]{3,2,1,0:T(8,128)(2,1)}, u32[]{:S(2)}, u32[]{:S(2)}) %all-to-all-start.2) | async-done | bytes 2097184 | tf_op jit(solution)/shard_map/all_to_all | solution.py:42
  194.3 3.6 %copy_bitcast_fusion = bf16[16,64,2048]{2,1,0:T(8,128)(2,1)} fusion(bf16[16,16,32,128]{3,2,1,0:T(8,128)(2,1)} %all-to-all-done.2, bf16[16,16,32,128]{3,2,1,0:T(8,128)(2,1)S(1)} %all-to-all-done.1), kind=kLoop, calls=%fused_computation.2 | loop fusion | flops 8388608 | bytes 8388608 | tf_op jit(solution)/shard_map/reshape | solution.py:33
  197.9 0.7 copy.20
  (2 shorter events, 0.0 us)
Async XLA Ops:
  2.0 24.6 %all-to-all-start.3 = ((bf16[16,128,16]{1,2,0:T(8,128)(2,1)}), bf16[16,128,16]{1,2,0:T(8,128)(2,1)S(1)}, u32[]{:S(2)}, u32[]{:S(2)}) async-start(bf16[16,128,16]{1,2,0:T(8,128)(2,1)} %broadcast_in_dim.9), calls=%async_computation.3 | async-start | bytes 131072 | tf_op jit(solution)/shard_map/all_to_all | solution.py:11
  27.6 37.8 %all-to-all-start = ((f32[16,16,1024]{2,1,0:T(8,128)}), f32[16,16,1024]{2,1,0:T(8,128)S(1)}, u32[]{:S(2)}, u32[]{:S(2)}) async-start(f32[16,16,1024]{2,1,0:T(8,128)} %broadcast_in_dim.8), calls=%async_computation | async-start | bytes 2097152 | tf_op jit(solution)/shard_map/all_to_all | solution.py:11
  66.2 13.0 %all-to-all-start.4 = ((bf16[4,2048,16]{1,2,0:T(8,128)(2,1)}), bf16[4,2048,16]{1,2,0:T(8,128)(2,1)S(1)}, u32[]{:S(2)}, u32[]{:S(2)}) async-start(bf16[4,2048,16]{1,2,0:T(8,128)(2,1)} %broadcast_in_dim.11), calls=%async_computation.4 | async-start | bytes 524288 | tf_op jit(solution)/shard_map/all_to_all | solution.py:11
  79.2 58.6 %all-to-all-start.1 = ((bf16[16,16,32,128]{3,2,1,0:T(8,128)(2,1)}), bf16[16,16,32,128]{3,2,1,0:T(8,128)(2,1)S(1)}, u32[]{:S(2)}, u32[]{:S(2)}) async-start(bf16[16,16,32,128]{3,2,1,0:T(8,128)(2,1)} %copy.11), calls=%async_computation.1 | async-start | bytes 4194304 | tf_op jit(solution)/shard_map/all_to_all | solution.py:42
  137.8 56.6 %all-to-all-start.2 = ((bf16[16,16,32,128]{3,2,1,0:T(8,128)(2,1)}), bf16[16,16,32,128]{3,2,1,0:T(8,128)(2,1)}, u32[]{:S(2)}, u32[]{:S(2)}) async-start(bf16[16,16,32,128]{3,2,1,0:T(8,128)(2,1)} %copy.12), calls=%async_computation.2 | async-start | bytes 4194304 | tf_op jit(solution)/shard_map/all_to_all | solution.py:42
where the time goes:
time: 199 us
  waiting for transfers between devices  138 us (69%)
  starting transfers between devices  33.1 us (17%)
  other arithmetic  15.2 us (8%)
  local copies, waits for them, and re-layouts  11.2 us (6%)
    all_to_all x2, waiting for transfers between devices, exchange_in_pieces(): lax.all_to_all(section, axis, split_axis=0, concat_axis=0, tiled=True)  101 us
    all_to_all x3, waiting for transfers between devices, copy_for_each(): lax.all_to_all(jnp.broadcast_to(shard[None], (length, *shard.shape)), axi...  37.3 us
    all_to_all x3, starting transfers between devices, copy_for_each(): lax.all_to_all(jnp.broadcast_to(shard[None], (length, *shard.shape)), axi...  23.2 us
    all_to_all x2, starting transfers between devices, exchange_in_pieces(): lax.all_to_all(section, axis, split_axis=0, concat_axis=0, tiled=True)  9.89 us
    split x3, local copies, waits for them, and re-layouts, exchange_in_pieces(): jnp.split(tiles, edges_of(tiles.shape[widest], pieces), axis=widest)  7.38 us
    reduce_sum x1, other arithmetic, on_device(): total_down = taken_together(jnp.sum(jnp.abs(w_down), axis=2), 'fsdp')  5.61 us
    convert_element_type x1, other arithmetic, on_device(): narrow_down = (w_down / jnp.expand_dims(scale_down, 2)).astype(jnp.bfloat16)  5.26 us
  transfers between devices with their start and end apart: 5, of which 4 were waited for; matrix products, arithmetic and copies ran while one was open for 10% of the time, Pallas kernels for 0%

commit v1 on v0

v1 whole, which is shorter than its diff:
```python
import functools

import jax
import jax.numpy as jnp
from jax import lax
from jax.experimental import pallas as pl
from jax.experimental.pallas import tpu as pltpu
from jax.sharding import PartitionSpec as P

D_MODEL = 2048
EXPERTS = 16
ROWS = 64
LANES = 128
HALF = 512
PLANES = [list(range(8)), list(range(8, 16))]

E, F1, F2, L = (0, 2), (2, 6), (8, 4), (12, 4)
OWN = (2, 14)


def swap(shard, k, axis="fsdp"):
    return lax.ppermute(shard, axis, [(i, i ^ k) for i in range(lax.axis_size(axis))])


def in_plane(shard):
    return lax.all_to_all(shard, "fsdp", 0, 0, axis_index_groups=PLANES, tiled=True)


def tie(value, *others):
    return lax.optimization_barrier((value, *others))[0]


def spread_kernel(other, scaled, z_ref, w_ref, *refs):
    out_ref = refs[-1]
    high = (z_ref[0] ^ other) == 1
    for i in range(w_ref.shape[0]):
        if scaled:
            tile = refs[0][i]
            tile = jnp.where(high, jnp.concatenate([tile[4:8], tile[0:4]], 0), tile)
            inverse = (D_MODEL / tile).T
        for j in range(4):
            block = w_ref[i, j * LANES : (j + 1) * LANES, :]
            if scaled:
                block = block * inverse[:, j : j + 1]
            block = block.astype(out_ref.dtype)
            out_ref[2 * j, i] = block[:ROWS]
            out_ref[2 * j + 1, i] = block[ROWS:]


def spread(w, sums, z, which, other, step):
    first, count = which
    scaled = sums is not None
    kind = jnp.bfloat16 if scaled else jnp.float32
    assert first % step == 0 and count % step == 0
    at = first // step
    in_specs = [pl.BlockSpec((step, HALF, LANES), lambda e, z: (at + e, z[0] ^ other, 0))]
    args = [w]
    if scaled:
        in_specs.append(pl.BlockSpec((step, 8, LANES), lambda e, z: (at + e, 0, 0)))
        args.append(sums)
    return pl.pallas_call(
        functools.partial(spread_kernel, other, scaled),
        grid_spec=pltpu.PrefetchScalarGridSpec(
            num_scalar_prefetch=1,
            grid=(count // step,),
            in_specs=in_specs,
            out_specs=pl.BlockSpec((8, step, ROWS, LANES), lambda e, z: (0, e, 0, 0)),
        ),
        out_shape=jax.ShapeDtypeStruct((8, count, ROWS, LANES), kind),
        name="spread",
        cost_estimate=pl.CostEstimate(
            flops=count * 1_000_000, bytes_accessed=count * 393_216, transcendentals=0
        ),
    )(z, *args)


def join_kernel(scaled, z_ref, in_ref, *refs):
    out_ref = refs[-1]
    for i in range(out_ref.shape[0]):
        for g in range(8):
            block = in_ref[g, i]
            if scaled:
                block = block * refs[0][i]
            out_ref[i, :, g * LANES : (g + 1) * LANES] = block.astype(jnp.bfloat16)


def join(out, came, inverse, z, which, other, step):
    first, count = which
    assert first % step == 0 and count % step == 0
    at = first // step
    in_specs = [pl.BlockSpec((8, step, ROWS, LANES), lambda e, z: (0, e, 0, 0))]
    args = [came]
    if inverse is not None:
        in_specs.append(pl.BlockSpec((step, ROWS, LANES), lambda e, z: (e, 0, 0)))
        args.append(inverse)
    alias = {}
    if out is not None:
        in_specs.append(pl.BlockSpec(memory_space=pl.ANY))
        args.append(out)
        alias = {len(args): 0}
    return pl.pallas_call(
        functools.partial(join_kernel, inverse is not None),
        grid_spec=pltpu.PrefetchScalarGridSpec(
            num_scalar_prefetch=1,
            grid=(count // step,),
            in_specs=in_specs,
            out_specs=pl.BlockSpec((step, ROWS, 1024), lambda e, z: (at + e, 0, z[0] ^ other)),
        ),
        out_shape=jax.ShapeDtypeStruct((EXPERTS, ROWS, D_MODEL), jnp.bfloat16),
        input_output_aliases=alias,
        name="join",
        cost_estimate=pl.CostEstimate(
            flops=count * 1_000_000, bytes_accessed=count * 262_144, transcendentals=0
        ),
    )(z, *args)


def on_device(w_down, router_weight, router_gain):
    index = lax.axis_index("fsdp").astype(jnp.int32)
    z = (index // 8).reshape(1)

    raw = spread(w_down, None, z, E, 1, 2)
    came_e = swap(raw, 8)
    own_e = spread(w_down, None, z, E, 0, 2)
    sums = jnp.sum(jnp.abs(w_down), axis=2).reshape(EXPERTS, 8, LANES)
    for k in (1, 2, 4):
        sums = sums + swap(sums, k)
    came = swap(sums, 8)

    part = (router_weight * router_gain[:, None]).astype(jnp.bfloat16).T
    part = tie(part, sums)
    part = lax.all_to_all(jnp.broadcast_to(part[None], (4, 16, LANES)), "ep", 0, 0, tiled=True)
    part = part.reshape(ROWS, LANES)
    sums = sums + came

    oth_f1 = spread(w_down, sums, z, F1, 1, 2)
    came_f1 = swap(oth_f1, 8)
    oth_l = spread(w_down, sums, z, L, 1, 2)
    oth_f2 = spread(w_down, sums, z, F2, 1, 2)
    came_f2 = swap(oth_f2, 8)
    plane_l = in_plane(oth_l)
    own = spread(w_down, sums, z, OWN, 0, 2)
    other_part = swap(part, 8)
    came_l = swap(plane_l, 8)
    own = in_plane(own)
    own_e = in_plane(tie(own_e, oth_f2))
    came_e = in_plane(came_e)

    scale = lax.dynamic_slice_in_dim(sums.reshape(EXPERTS, 16, ROWS), index, 1, 1)[:, 0] / D_MODEL
    inverse = jnp.broadcast_to((1.0 / scale[:2])[:, :, None], (2, ROWS, LANES))

    came_f1 = in_plane(came_f1)
    both = jnp.broadcast_to(jnp.stack([part, other_part])[None], (8, 2, ROWS, LANES))
    both = in_plane(both)
    came_f2 = in_plane(came_f2)

    out = join(None, own_e, inverse, z, E, 0, 2)
    out = join(out, own, None, z, OWN, 0, 2)
    out = join(out, came_e, inverse, z, E, 1, 2)
    out = join(out, came_f1, None, z, F1, 1, 2)
    out = join(out, came_f2, None, z, F2, 1, 4)
    out = join(out, came_l, None, z, L, 1, 4)

    halves = both.transpose(1, 2, 0, 3).reshape(2, ROWS, 1024)
    halves = jnp.where(z[0] == 0, halves, halves[::-1])
    router = jnp.concatenate([halves[0], halves[1]], 1).T
    return (out, scale, router)


def solution(mesh):
    return jax.shard_map(
        on_device,
        mesh=mesh,
        in_specs=(P(("unit", "ep"), None, "fsdp"), P(("unit", "fsdp"), "ep"), P(("unit", "fsdp"))),
        out_specs=(P(("unit", "ep"), "fsdp", None), P(("unit", "ep"), "fsdp"), P("unit", None)),
        check_vma=False,
    )
```

time: 199 us -> 202 us (1.015)
  the two profiles are of different devices: /device:TPU:34 before, /device:TPU:1 now
where the time goes in v1:
time: 202 us; the launch traced here: 201 us
  waiting for transfers between devices  66.8 us (33%)
  starting transfers between devices  64.5 us (32%)
  Pallas kernels  34.1 us (17%)
  blocking collectives  22.7 us (11%)
  other arithmetic  7.65 us (4%)
  local copies, waits for them, and re-layouts  3.95 us (2%)
    ppermute x9, waiting for transfers between devices, swap(): lax.ppermute(shard, axis, [(i, i ^ k) for i in range(lax.axis_size(axis))])  58.7 us
    all_to_all x6, starting transfers between devices, in_plane(): lax.all_to_all(shard, 'fsdp', 0, 0, axis_index_groups=PLANES, tiled=True)  36.3 us
    ppermute x9, starting transfers between devices, swap(): lax.ppermute(shard, axis, [(i, i ^ k) for i in range(lax.axis_size(axis))])  28.2 us
    pallas_call x6, Pallas kernels, spread(): pl.pallas_call(functools.partial(spread_kernel, other, scaled), grid_spec...  18.6 us
    pallas_call x6, Pallas kernels, join(): pl.pallas_call(functools.partial(join_kernel, inverse is not None), grid_...  15.5 us
    all_to_all x1, blocking collectives, in_plane(): lax.all_to_all(shard, 'fsdp', 0, 0, axis_index_groups=PLANES, tiled=True)  12.8 us
    all_to_all x1, blocking collectives, on_device(): lax.all_to_all(jnp.broadcast_to(part[None], (4, 16, LANES)), 'ep', 0, 0,...  9.93 us
    all_to_all x6, waiting for transfers between devices, in_plane(): lax.all_to_all(shard, 'fsdp', 0, 0, axis_index_groups=PLANES, tiled=True)  8.11 us
  transfers between devices with their start and end apart: 15, of which 11 were waited for; matrix products, arithmetic and copies ran while one was open for 2% of the time, Pallas kernels for 16%

profile of v1, /device:TPU:1, one launch (start us, length us, event | category | flops | bytes accessed | tf_op | source)
XLA Modules:
  0.0 200.5 jit_solution(3103704850884916011)
XLA Ops:
  0.7 5.6 %abs_reduce_fusion = f32[16,1024]{1,0:T(8,128)S(1)} fusion(f32[16,1024,128]{2,1,0:T(8,128)} %w_ref.11), kind=kLoop, calls=%fused_computation | loop fusion | flops 4177920 | bytes 8454144 | tf_op jit(solution)/shard_map/reduce_sum | solution.py:125
  6.3 2.1 %collective-permute-start = (f32[16,8,128]{2,1,0:T(8,128)S(1)}, f32[16,8,128]{2,1,0:T(8,128)S(1)}, u32[]{:S(2)}, u32[]{:S(2)}) collective-permute-start(f32[16,8,128]{2,1,0:T(8,128)S(1)} %bitcast.27), channel_id=1, source_target_pairs={{0,1},{1,0},{2,3},{3,2},{4,5},{5,4},{6,7},{7,6},{8,9},{9,8},{10,11... | collective-permute-start | bytes 196616 | tf_op jit(solution)/shard_map/ppermute | solution.py:22
  10.1 3.1 %collective-permute-start.1 = (f32[16,8,128]{2,1,0:T(8,128)S(1)}, f32[16,8,128]{2,1,0:T(8,128)S(1)}, u32[]{:S(2)}, u32[]{:S(2)}) collective-permute-start(f32[16,8,128]{2,1,0:T(8,128)S(1)} %bitcast_add_fusion), channel_id=1, source_target_pairs={{0,2},{1,3},{2,0},{3,1},{4,6},{5,7},{6,4},{7,5},{8,10},{9,11},{10,... | collective-permute-start | bytes 196616 | tf_op jit(solution)/shard_map/ppermute | solution.py:22
  14.8 3.2 %collective-permute-start.2 = (f32[16,8,128]{2,1,0:T(8,128)S(1)}, f32[16,8,128]{2,1,0:T(8,128)S(1)}, u32[]{:S(2)}, u32[]{:S(2)}) collective-permute-start(f32[16,8,128]{2,1,0:T(8,128)S(1)} %add.17), channel_id=1, source_target_pairs={{0,4},{1,5},{2,6},{3,7},{4,0},{5,1},{6,2},{7,3},{8,12},{9,13},{10,... | collective-permute-start | bytes 196616 | tf_op jit(solution)/shard_map/ppermute | solution.py:22
  19.7 9.9 %all_to_all.40 = bf16[4,16,128]{2,1,0:T(8,128)(2,1)S(1)} all-to-all(bf16[4,16,128]{2,1,0:T(8,128)(2,1)S(1)} %broadcast_in_dim.7), channel_id=1, replica_groups=mesh['unit'=4,'ep'=4,'fsdp'=16] {'ep'}, dimensions={0} | all-to-all | bytes 32768 | tf_op jit(solution)/shard_map/all_to_all | solution.py:132
  29.7 4.2 %collective-permute-start.8 = (bf16[64,128]{1,0:T(8,128)(2,1)S(1)}, bf16[64,128]{1,0:T(8,128)(2,1)S(1)}, u32[]{:S(2)}, u32[]{:S(2)}) collective-permute-start(bf16[64,128]{1,0:T(8,128)(2,1)S(1)} %bitcast.28), channel_id=1, source_target_pairs={{0,8},{1,9},{2,10},{3,11},{4,12},{5,13},{6,14},{7,15},{8,0},{9,1},... | collective-permute-start | bytes 49160 | tf_op jit(solution)/shard_map/ppermute | solution.py:22
  33.9 2.3 %collective-permute-done.8 = bf16[64,128]{1,0:T(8,128)(2,1)S(1)} collective-permute-done((bf16[64,128]{1,0:T(8,128)(2,1)S(1)}, bf16[64,128]{1,0:T(8,128)(2,1)S(1)}, u32[]{:S(2)}, u32[]{:S(2)}) %collective-permute-start.8) | collective-permute-done | bytes 16416 | tf_op jit(solution)/shard_map/ppermute | solution.py:22
  36.9 6.7 %all-to-all-start.7 = ((bf16[8,2,64,128]{3,2,1,0:T(8,128)(2,1)}), bf16[8,2,64,128]{3,2,1,0:T(8,128)(2,1)S(1)}, u32[]{:S(2)}, u32[]{:S(2)}) async-start(bf16[8,2,64,128]{3,2,1,0:T(8,128)(2,1)} %broadcast_in_dim.8), calls=%async_computation.7 | async-start | bytes 524288 | tf_op jit(solution)/shard_map/all_to_all | solution.py:26
  43.6 4.2 %collective-permute-start.3 = (f32[16,8,128]{2,1,0:T(8,128)S(1)}, f32[16,8,128]{2,1,0:T(8,128)S(1)}, u32[]{:S(2)}, u32[]{:S(2)}) collective-permute-start(f32[16,8,128]{2,1,0:T(8,128)S(1)} %add.18), channel_id=1, source_target_pairs={{0,8},{1,9},{2,10},{3,11},{4,12},{5,13},{6,14},{7,15},{8,0},{9,1},... | collective-permute-start | bytes 196616 | tf_op jit(solution)/shard_map/ppermute | solution.py:22
  47.8 1.9 spread.11
  51.2 2.4 %spread.7 = bf16[8,4,64,128]{3,2,1,0:T(8,128)(2,1)} custom-call(s32[1]{0:T(128)} %bitcast.z_ref, f32[16,1024,128]{2,1,0:T(8,128)} %w_ref.11, f32[16,8,128]{2,1,0:T(8,128)} %add.19.refs_0_), custom_call_target="tpu_custom_call" | custom-call | flops 4000000 | bytes 1572864 | tf_op jit(solution)/shard_map/spread/pallas_call | solution.py:61
  53.6 6.6 %all-to-all-start.5 = ((f32[8,2,64,128]{3,2,1,0:T(8,128)}), f32[8,2,64,128]{3,2,1,0:T(8,128)S(1)}, u32[]{:S(2)}, u32[]{:S(2)}) async-start(f32[8,2,64,128]{3,2,1,0:T(8,128)} %spread.11), calls=%async_computation.5 | async-start | bytes 1048576 | tf_op jit(solution)/shard_map/all_to_all | solution.py:26
  60.3 1.9 spread.9
  62.1 4.2 %collective-permute-start.7 = (f32[8,2,64,128]{3,2,1,0:T(8,128)}, f32[8,2,64,128]{3,2,1,0:T(8,128)S(1)}, u32[]{:S(2)}, u32[]{:S(2)}) collective-permute-start(f32[8,2,64,128]{3,2,1,0:T(8,128)} %spread.9), channel_id=1, source_target_pairs={{0,8},{1,9},{2,10},{3,11},{4,12},{5,13},{6,14},{7,15},{8,0},{9,1},... | collective-permute-start | bytes 1572872 | tf_op jit(solution)/shard_map/ppermute | solution.py:22
  66.3 2.4 %spread.6 = bf16[8,4,64,128]{3,2,1,0:T(8,128)(2,1)} custom-call(s32[1]{0:T(128)} %bitcast.z_ref, f32[16,1024,128]{2,1,0:T(8,128)} %w_ref.11, f32[16,8,128]{2,1,0:T(8,128)} %add.19.refs_0_), custom_call_target="tpu_custom_call" | custom-call | flops 4000000 | bytes 1572864 | tf_op jit(solution)/shard_map/spread/pallas_call | solution.py:61
  69.3 6.1 %all-to-all-start = ((bf16[8,4,64,128]{3,2,1,0:T(8,128)(2,1)}), bf16[8,4,64,128]{3,2,1,0:T(8,128)(2,1)S(1)}, u32[]{:S(2)}, u32[]{:S(2)}) async-start(bf16[8,4,64,128]{3,2,1,0:T(8,128)(2,1)} %spread.6), calls=%async_computation | async-start | bytes 1048576 | tf_op jit(solution)/shard_map/all_to_all | solution.py:26
  75.4 3.5 %spread.8 = bf16[8,6,64,128]{3,2,1,0:T(8,128)(2,1)} custom-call(s32[1]{0:T(128)} %bitcast.z_ref, f32[16,1024,128]{2,1,0:T(8,128)} %w_ref.11, f32[16,8,128]{2,1,0:T(8,128)} %add.19.refs_0_), custom_call_target="tpu_custom_call" | custom-call | flops 6000000 | bytes 2359296 | tf_op jit(solution)/shard_map/spread/pallas_call | solution.py:61
  81.2 3.4 %all-to-all-done = bf16[8,4,64,128]{3,2,1,0:T(8,128)(2,1)S(1)} async-done(((bf16[8,4,64,128]{3,2,1,0:T(8,128)(2,1)}), bf16[8,4,64,128]{3,2,1,0:T(8,128)(2,1)S(1)}, u32[]{:S(2)}, u32[]{:S(2)}) %all-to-all-start) | async-done | bytes 524320 | tf_op jit(solution)/shard_map/all_to_all | solution.py:26
  84.6 12.8 %all_to_all.41.in_ref = f32[8,2,64,128]{3,2,1,0:T(8,128)} all-to-all(f32[8,2,64,128]{3,2,1,0:T(8,128)S(1)} %collective-permute-done.7), channel_id=1, replica_groups={{0,1,2,3,4,5,6,7},{8,9,10,11,12,13,14,15},{16,17,18,19,20,21,22,23},{24..., dimensions={0} | all-to-all | bytes 1048576 | tf_op jit(solution)/shard_map/all_to_all | solution.py:26
  97.3 25.2 %collective-permute-done.6 = bf16[8,6,64,128]{3,2,1,0:T(8,128)(2,1)} collective-permute-done((bf16[8,6,64,128]{3,2,1,0:T(8,128)(2,1)}, bf16[8,6,64,128]{3,2,1,0:T(8,128)(2,1)}, u32[]{:S(2)}, u32[]{:S(2)}) %collective-permute-start.6) | collective-permute-done | bytes 786464 | tf_op jit(solution)/shard_map/ppermute | solution.py:22
  122.6 6.8 %all-to-all-start.2 = ((bf16[8,6,64,128]{3,2,1,0:T(8,128)(2,1)}), bf16[8,6,64,128]{3,2,1,0:T(8,128)(2,1)S(1)}, u32[]{:S(2)}, u32[]{:S(2)}) async-start(bf16[8,6,64,128]{3,2,1,0:T(8,128)(2,1)} %collective-permute-done.6), calls=%async_computation.2 | async-start | bytes 1572864 | tf_op jit(solution)/shard_map/all_to_all | solution.py:26
  129.4 6.6 %spread.10 = bf16[8,14,64,128]{3,2,1,0:T(8,128)(2,1)} custom-call(s32[1]{0:T(128)} %bitcast.z_ref, f32[16,1024,128]{2,1,0:T(8,128)} %w_ref.11, f32[16,8,128]{2,1,0:T(8,128)} %add.19.refs_0_), custom_call_target="tpu_custom_call" | custom-call | flops 14000000 | bytes 5505024 | tf_op jit(solution)/shard_map/spread/pallas_call | solution.py:61
  136.0 4.2 %all-to-all-done.2.in_ref = bf16[8,6,64,128]{3,2,1,0:T(8,128)(2,1)S(1)} async-done(((bf16[8,6,64,128]{3,2,1,0:T(8,128)(2,1)}), bf16[8,6,64,128]{3,2,1,0:T(8,128)(2,1)S(1)}, u32[]{:S(2)}, u32[]{:S(2)}) %all-to-all-start.2) | async-done | bytes 786464 | tf_op jit(solution)/shard_map/all_to_all | solution.py:26
  140.1 3.6 %all-to-all-start.4 = ((bf16[8,14,64,128]{3,2,1,0:T(8,128)(2,1)}), bf16[8,14,64,128]{3,2,1,0:T(8,128)(2,1)S(1)}, u32[]{:S(2)}, u32[]{:S(2)}) async-start(bf16[8,14,64,128]{3,2,1,0:T(8,128)(2,1)} %spread.10), calls=%async_computation.4 | async-start | bytes 3670016 | tf_op jit(solution)/shard_map/all_to_all | solution.py:26
  144.5 2.0 collective-permute-start.5
  147.9 3.5 %collective-permute-start.4 = (bf16[8,4,64,128]{3,2,1,0:T(8,128)(2,1)}, bf16[8,4,64,128]{3,2,1,0:T(8,128)(2,1)}, u32[]{:S(2)}, u32[]{:S(2)}) collective-permute-start(bf16[8,4,64,128]{3,2,1,0:T(8,128)(2,1)} %copy-done.6), channel_id=1, source_target_pairs={{0,8},{1,9},{2,10},{3,11},{4,12},{5,13},{6,14},{7,15},{8,0},{9,1},... | collective-permute-start | bytes 1572872 | tf_op jit(solution)/shard_map/ppermute | solution.py:22
  151.5 24.7 %collective-permute-done.5 = bf16[8,4,64,128]{3,2,1,0:T(8,128)(2,1)} collective-permute-done((bf16[8,4,64,128]{3,2,1,0:T(8,128)(2,1)S(1)}, bf16[8,4,64,128]{3,2,1,0:T(8,128)(2,1)}, u32[]{:S(2)}, u32[]{:S(2)}) %collective-permute-start.5) | collective-permute-done | bytes 524320 | tf_op jit(solution)/shard_map/ppermute | solution.py:22
  176.2 6.6 %all-to-all-start.1 = ((bf16[8,4,64,128]{3,2,1,0:T(8,128)(2,1)}), bf16[8,4,64,128]{3,2,1,0:T(8,128)(2,1)S(1)}, u32[]{:S(2)}, u32[]{:S(2)}) async-start(bf16[8,4,64,128]{3,2,1,0:T(8,128)(2,1)} %collective-permute-done.5), calls=%async_computation.1 | async-start | bytes 1048576 | tf_op jit(solution)/shard_map/all_to_all | solution.py:26
  186.0 5.2 %join.7.refs_1_ = bf16[16,64,2048]{2,1,0:T(8,128)(2,1)} custom-call(s32[1]{0:T(128)} %bitcast.z_ref, bf16[8,14,64,128]{3,2,1,0:T(8,128)(2,1)} %copy-done, bf16[16,64,2048]{2,1,0:T(8,128)(2,1)} %join.6.refs_0_), custom_call_target="tpu_custom_call", output_to_operand_aliasing={{}: (2, {})} | custom-call | flops 14000000 | bytes 3670016 | tf_op jit(solution)/shard_map/join/pallas_call | solution.py:101
  193.0 2.9 %join.9.refs_0_ = bf16[16,64,2048]{2,1,0:T(8,128)(2,1)} custom-call(s32[1]{0:T(128)} %bitcast.z_ref, bf16[8,6,64,128]{3,2,1,0:T(8,128)(2,1)} %copy-done.1, bf16[16,64,2048]{2,1,0:T(8,128)(2,1)} %join.8.refs_0_), custom_call_target="tpu_custom_call", output_to_operand_aliasing={{}: (2, {})} | custom-call | flops 6000000 | bytes 1572864 | tf_op jit(solution)/shard_map/join/pallas_call | solution.py:101
  196.7 1.9 join.10.refs_0_
  198.6 1.9 join.11
  (49 shorter events, 18.4 us)
Async XLA Ops:
  0.6 17.4 %copy-start.7 = (f32[128,16]{0,1:T(8,128)S(1)}, f32[128,16]{0,1:T(8,128)}, u32[]{:S(2)}) copy-start(f32[128,16]{0,1:T(8,128)} %param.4) | copy-start | bytes 24580
  0.6 17.4 %copy-start.8 = (f32[128]{0:T(128)S(1)}, f32[128]{0:T(128)}, u32[]{:S(2)}) copy-start(f32[128]{0:T(128)} %param.5) | copy-start | bytes 1540
  6.3 3.8 %collective-permute-start = (f32[16,8,128]{2,1,0:T(8,128)S(1)}, f32[16,8,128]{2,1,0:T(8,128)S(1)}, u32[]{:S(2)}, u32[]{:S(2)}) collective-permute-start(f32[16,8,128]{2,1,0:T(8,128)S(1)} %bitcast.27), channel_id=1, source_target_pairs={{0,1},{1,0},{2,3},{3,2},{4,5},{5,4},{6,7},{7,6},{8,9},{9,8},{10,11... | collective-permute-start | bytes 196616 | tf_op jit(solution)/shard_map/ppermute | solution.py:22
  10.1 4.7 %collective-permute-start.1 = (f32[16,8,128]{2,1,0:T(8,128)S(1)}, f32[16,8,128]{2,1,0:T(8,128)S(1)}, u32[]{:S(2)}, u32[]{:S(2)}) collective-permute-start(f32[16,8,128]{2,1,0:T(8,128)S(1)} %bitcast_add_fusion), channel_id=1, source_target_pairs={{0,2},{1,3},{2,0},{3,1},{4,6},{5,7},{6,4},{7,5},{8,10},{9,11},{10,... | collective-permute-start | bytes 196616 | tf_op jit(solution)/shard_map/ppermute | solution.py:22
  14.8 4.9 %collective-permute-start.2 = (f32[16,8,128]{2,1,0:T(8,128)S(1)}, f32[16,8,128]{2,1,0:T(8,128)S(1)}, u32[]{:S(2)}, u32[]{:S(2)}) collective-permute-start(f32[16,8,128]{2,1,0:T(8,128)S(1)} %add.17), channel_id=1, source_target_pairs={{0,4},{1,5},{2,6},{3,7},{4,0},{5,1},{6,2},{7,3},{8,12},{9,13},{10,... | collective-permute-start | bytes 196616 | tf_op jit(solution)/shard_map/ppermute | solution.py:22
  29.7 6.5 %collective-permute-start.8 = (bf16[64,128]{1,0:T(8,128)(2,1)S(1)}, bf16[64,128]{1,0:T(8,128)(2,1)S(1)}, u32[]{:S(2)}, u32[]{:S(2)}) collective-permute-start(bf16[64,128]{1,0:T(8,128)(2,1)S(1)} %bitcast.28), channel_id=1, source_target_pairs={{0,8},{1,9},{2,10},{3,11},{4,12},{5,13},{6,14},{7,15},{8,0},{9,1},... | collective-permute-start | bytes 49160 | tf_op jit(solution)/shard_map/ppermute | solution.py:22
  36.9 16.7 %all-to-all-start.7 = ((bf16[8,2,64,128]{3,2,1,0:T(8,128)(2,1)}), bf16[8,2,64,128]{3,2,1,0:T(8,128)(2,1)S(1)}, u32[]{:S(2)}, u32[]{:S(2)}) async-start(bf16[8,2,64,128]{3,2,1,0:T(8,128)(2,1)} %broadcast_in_dim.8), calls=%async_computation.7 | async-start | bytes 524288 | tf_op jit(solution)/shard_map/all_to_all | solution.py:26
  43.6 7.0 %collective-permute-start.3 = (f32[16,8,128]{2,1,0:T(8,128)S(1)}, f32[16,8,128]{2,1,0:T(8,128)S(1)}, u32[]{:S(2)}, u32[]{:S(2)}) collective-permute-start(f32[16,8,128]{2,1,0:T(8,128)S(1)} %add.18), channel_id=1, source_target_pairs={{0,8},{1,9},{2,10},{3,11},{4,12},{5,13},{6,14},{7,15},{8,0},{9,1},... | collective-permute-start | bytes 196616 | tf_op jit(solution)/shard_map/ppermute | solution.py:22
  53.6 15.7 %all-to-all-start.5 = ((f32[8,2,64,128]{3,2,1,0:T(8,128)}), f32[8,2,64,128]{3,2,1,0:T(8,128)S(1)}, u32[]{:S(2)}, u32[]{:S(2)}) async-start(f32[8,2,64,128]{3,2,1,0:T(8,128)} %spread.11), calls=%async_computation.5 | async-start | bytes 1048576 | tf_op jit(solution)/shard_map/all_to_all | solution.py:26
  62.1 19.1 %collective-permute-start.7 = (f32[8,2,64,128]{3,2,1,0:T(8,128)}, f32[8,2,64,128]{3,2,1,0:T(8,128)S(1)}, u32[]{:S(2)}, u32[]{:S(2)}) collective-permute-start(f32[8,2,64,128]{3,2,1,0:T(8,128)} %spread.9), channel_id=1, source_target_pairs={{0,8},{1,9},{2,10},{3,11},{4,12},{5,13},{6,14},{7,15},{8,0},{9,1},... | collective-permute-start | bytes 1572872 | tf_op jit(solution)/shard_map/ppermute | solution.py:22
  69.3 9.6 %copy-start.3 = (f32[8,2,64,128]{3,2,1,0:T(8,128)}, f32[8,2,64,128]{3,2,1,0:T(8,128)S(1)}, u32[]{:S(2)}) copy-start(f32[8,2,64,128]{3,2,1,0:T(8,128)S(1)} %all-to-all-done.5.in_ref) | copy-start | bytes 1572868
  69.3 15.2 %all-to-all-start = ((bf16[8,4,64,128]{3,2,1,0:T(8,128)(2,1)}), bf16[8,4,64,128]{3,2,1,0:T(8,128)(2,1)S(1)}, u32[]{:S(2)}, u32[]{:S(2)}) async-start(bf16[8,4,64,128]{3,2,1,0:T(8,128)(2,1)} %spread.6), calls=%async_computation | async-start | bytes 1048576 | tf_op jit(solution)/shard_map/all_to_all | solution.py:26
  78.9 43.7 %collective-permute-start.6 = (bf16[8,6,64,128]{3,2,1,0:T(8,128)(2,1)}, bf16[8,6,64,128]{3,2,1,0:T(8,128)(2,1)}, u32[]{:S(2)}, u32[]{:S(2)}) collective-permute-start(bf16[8,6,64,128]{3,2,1,0:T(8,128)(2,1)} %spread.8), channel_id=1, source_target_pairs={{0,8},{1,9},{2,10},{3,11},{4,12},{5,13},{6,14},{7,15},{8,0},{9,1},... | collective-permute-start | bytes 2359304 | tf_op jit(solution)/shard_map/ppermute | solution.py:22
  84.5 38.0 %copy-start.6 = (bf16[8,4,64,128]{3,2,1,0:T(8,128)(2,1)}, bf16[8,4,64,128]{3,2,1,0:T(8,128)(2,1)S(1)}, u32[]{:S(2)}) copy-start(bf16[8,4,64,128]{3,2,1,0:T(8,128)(2,1)S(1)} %all-to-all-done) | copy-start | bytes 1572868
  122.6 17.6 %all-to-all-start.2 = ((bf16[8,6,64,128]{3,2,1,0:T(8,128)(2,1)}), bf16[8,6,64,128]{3,2,1,0:T(8,128)(2,1)S(1)}, u32[]{:S(2)}, u32[]{:S(2)}) async-start(bf16[8,6,64,128]{3,2,1,0:T(8,128)(2,1)} %collective-permute-done.6), calls=%async_computation.2 | async-start | bytes 1572864 | tf_op jit(solution)/shard_map/all_to_all | solution.py:26
  129.4 14.4 %copy-start.2 = (f32[16,8,128]{2,1,0:T(8,128)S(1)}, f32[16,8,128]{2,1,0:T(8,128)}, u32[]{:S(2)}) copy-start(f32[16,8,128]{2,1,0:T(8,128)} %add.19.refs_0_) | copy-start | bytes 196612
  129.4 15.1 %copy-start.5 = (bf16[8,4,64,128]{3,2,1,0:T(8,128)(2,1)S(1)}, bf16[8,4,64,128]{3,2,1,0:T(8,128)(2,1)}, u32[]{:S(2)}) copy-start(bf16[8,4,64,128]{3,2,1,0:T(8,128)(2,1)} %spread.7) | copy-start | bytes 1572868
  140.1 45.9 %copy-start.1 = (bf16[8,6,64,128]{3,2,1,0:T(8,128)(2,1)}, bf16[8,6,64,128]{3,2,1,0:T(8,128)(2,1)S(1)}, u32[]{:S(2)}) copy-start(bf16[8,6,64,128]{3,2,1,0:T(8,128)(2,1)S(1)} %all-to-all-done.2.in_ref) | copy-start | bytes 2359300
  140.1 36.0 %all-to-all-start.4 = ((bf16[8,14,64,128]{3,2,1,0:T(8,128)(2,1)}), bf16[8,14,64,128]{3,2,1,0:T(8,128)(2,1)S(1)}, u32[]{:S(2)}, u32[]{:S(2)}) async-start(bf16[8,14,64,128]{3,2,1,0:T(8,128)(2,1)} %spread.10), calls=%async_computation.4 | async-start | bytes 3670016 | tf_op jit(solution)/shard_map/all_to_all | solution.py:26
  144.5 31.7 %collective-permute-start.5 = (bf16[8,4,64,128]{3,2,1,0:T(8,128)(2,1)S(1)}, bf16[8,4,64,128]{3,2,1,0:T(8,128)(2,1)}, u32[]{:S(2)}, u32[]{:S(2)}) collective-permute-start(bf16[8,4,64,128]{3,2,1,0:T(8,128)(2,1)S(1)} %copy-done.5), channel_id=1, source_target_pairs={{0,8},{1,9},{2,10},{3,11},{4,12},{5,13},{6,14},{7,15},{8,0},{9,1},... | collective-permute-start | bytes 1572872 | tf_op jit(solution)/shard_map/ppermute | solution.py:22
  147.9 50.7 %collective-permute-start.4 = (bf16[8,4,64,128]{3,2,1,0:T(8,128)(2,1)}, bf16[8,4,64,128]{3,2,1,0:T(8,128)(2,1)}, u32[]{:S(2)}, u32[]{:S(2)}) collective-permute-start(bf16[8,4,64,128]{3,2,1,0:T(8,128)(2,1)} %copy-done.6), channel_id=1, source_target_pairs={{0,8},{1,9},{2,10},{3,11},{4,12},{5,13},{6,14},{7,15},{8,0},{9,1},... | collective-permute-start | bytes 1572872 | tf_op jit(solution)/shard_map/ppermute | solution.py:22
  176.2 9.8 %copy-start = (bf16[8,14,64,128]{3,2,1,0:T(8,128)(2,1)}, bf16[8,14,64,128]{3,2,1,0:T(8,128)(2,1)S(1)}, u32[]{:S(2)}) copy-start(bf16[8,14,64,128]{3,2,1,0:T(8,128)(2,1)S(1)} %all-to-all-done.4.in_ref) | copy-start | bytes 5505028
  176.2 19.7 %all-to-all-start.1 = ((bf16[8,4,64,128]{3,2,1,0:T(8,128)(2,1)}), bf16[8,4,64,128]{3,2,1,0:T(8,128)(2,1)S(1)}, u32[]{:S(2)}, u32[]{:S(2)}) async-start(bf16[8,4,64,128]{3,2,1,0:T(8,128)(2,1)} %collective-permute-done.5), calls=%async_computation.1 | async-start | bytes 1048576 | tf_op jit(solution)/shard_map/all_to_all | solution.py:26
  195.9 0.8 copy-start.4

commit v2 on v1

v2 whole, which is shorter than its diff:
```python
import functools

import jax
import jax.numpy as jnp
from jax import lax
from jax.experimental import pallas as pl
from jax.experimental.pallas import tpu as pltpu
from jax.sharding import PartitionSpec as P

D_MODEL = 2048
EXPERTS = 16
ROWS = 64
LANES = 128
HALF = 512

F, L, E = (0, 7), (7, 7), (14, 2)
A, B = (0, 10), (10, 6)


def swap(shard, k):
    return lax.ppermute(shard, "fsdp", [(i, i ^ k) for i in range(lax.axis_size("fsdp"))])


def relative(s, m):
    s = jnp.where((m & 8) != 0, jnp.concatenate([s[4:8], s[0:4]], 0), s)
    s = jnp.where((m & 4) != 0, jnp.concatenate([s[2:4], s[0:2], s[6:8], s[4:6]], 0), s)
    odd = [s[i ^ 1 : (i ^ 1) + 1] for i in range(8)]
    s = jnp.where((m & 2) != 0, jnp.concatenate(odd, 0), s)
    return jnp.where((m & 1) != 0, jnp.concatenate([s[:, ROWS:], s[:, :ROWS]], 1), s)


def spread_kernel(other, scaled, me_ref, w_ref, *refs):
    m = me_ref[0] ^ (8 * other)
    outs = refs[1:] if scaled else refs
    for i in range(w_ref.shape[0]):
        if scaled:
            inverse = (D_MODEL / relative(refs[0][i], m)).T
        for r in range(8):
            at = pl.multiple_of(((m & 7) ^ r) * ROWS, ROWS)
            block = w_ref[i, pl.ds(at, ROWS), :]
            if scaled:
                h = (r & 1) * ROWS
                block = block * inverse[h : h + ROWS, r >> 1 : (r >> 1) + 1]
            y, x = r >> 2, r & 3
            if len(outs) == w_ref.shape[0] and not scaled:
                outs[i][2 * x + y, 0] = block.astype(outs[i].dtype)
            elif len(outs) == 4:
                outs[x][y, i] = block.astype(outs[x].dtype)
            else:
                outs[0][2 * x + y, i] = block.astype(outs[0].dtype)


def spread(w, sums, me, which, other, arrays, step):
    first, count = which
    scaled = sums is not None
    kind = jnp.bfloat16 if scaled else jnp.float32
    assert count % step == 0
    blocks = 8 // arrays
    in_specs = [
        pl.BlockSpec(
            (pl.Element(step), pl.Element(HALF), pl.Element(LANES)),
            lambda e, m: (first + e * step, ((m[0] >> 3) ^ other) * HALF, 0),
        )
    ]
    args = [w]
    if scaled:
        in_specs.append(
            pl.BlockSpec(
                (pl.Element(step), pl.Element(8), pl.Element(LANES)),
                lambda e, m: (first + e * step, 0, 0),
            )
        )
        args.append(sums)
    return pl.pallas_call(
        functools.partial(spread_kernel, other, scaled),
        grid_spec=pltpu.PrefetchScalarGridSpec(
            num_scalar_prefetch=1,
            grid=(count // step,),
            in_specs=in_specs,
            out_specs=[pl.BlockSpec((blocks, step, ROWS, LANES), lambda e, m: (0, e, 0, 0))]
            * arrays,
        ),
        out_shape=[jax.ShapeDtypeStruct((blocks, count, ROWS, LANES), kind)] * arrays,
        name="spread",
        cost_estimate=pl.CostEstimate(
            flops=count * 1_000_000, bytes_accessed=count * 393_216, transcendentals=0
        ),
    )(me, *args)


def own_kernel(me_ref, w_ref, s_ref, router_ref, *refs):
    m = me_ref[0]
    raws, outs = refs[:-2], refs[-2:]
    count = w_ref.shape[0]
    for i in range(count):
        inverse = (D_MODEL / relative(s_ref[i], m)).T
        for r in range(8):
            at = pl.multiple_of(((m & 7) ^ r) * ROWS, ROWS)
            column = inverse[(r & 1) * ROWS : (r & 1) * ROWS + ROWS, r >> 1 : (r >> 1) + 1]
            outs[r >> 2][r & 3, i] = (w_ref[i, pl.ds(at, ROWS), :] * column).astype(jnp.bfloat16)
            raw = i - (count - len(raws))
            if raw >= 0:
                block = raws[raw][2 * (r & 3) + (r >> 2), 0] * column
                outs[r >> 2][r & 3, count + 2 + raw] = block.astype(jnp.bfloat16)
    for out in outs:
        for x in range(4):
            for z in range(2):
                out[x, count + z] = router_ref[z]


def spread_own(w, sums, router, raws, me, which):
    first, count = which
    slots = count + 2 + len(raws)

    def whole(*shape):
        return pl.BlockSpec(shape, lambda e, m: (0,) * len(shape))

    return pl.pallas_call(
        own_kernel,
        grid_spec=pltpu.PrefetchScalarGridSpec(
            num_scalar_prefetch=1,
            grid=(1,),
            in_specs=[
                pl.BlockSpec(
                    (pl.Element(count), pl.Element(HALF), pl.Element(LANES)),
                    lambda e, m: (first, (m[0] >> 3) * HALF, 0),
                ),
                pl.BlockSpec(
                    (pl.Element(count), pl.Element(8), pl.Element(LANES)),
                    lambda e, m: (first, 0, 0),
                ),
                whole(2, ROWS, LANES),
            ]
            + [whole(8, 1, ROWS, LANES)] * len(raws),
            out_specs=[whole(4, slots, ROWS, LANES)] * 2,
        ),
        out_shape=[jax.ShapeDtypeStruct((4, slots, ROWS, LANES), jnp.bfloat16)] * 2,
        name="spread_own",
        cost_estimate=pl.CostEstimate(
            flops=slots * 1_000_000, bytes_accessed=slots * 393_216, transcendentals=0
        ),
    )(me, w, sums, router, *raws)


def spread_raw(w, me, which):
    first, count = which
    return pl.pallas_call(
        functools.partial(spread_kernel, 1, False),
        grid_spec=pltpu.PrefetchScalarGridSpec(
            num_scalar_prefetch=1,
            grid=(1,),
            in_specs=[
                pl.BlockSpec(
                    (pl.Element(count), pl.Element(HALF), pl.Element(LANES)),
                    lambda e, m: (first, ((m[0] >> 3) ^ 1) * HALF, 0),
                )
            ],
            out_specs=[pl.BlockSpec((8, 1, ROWS, LANES), lambda e, m: (0, 0, 0, 0))] * count,
        ),
        out_shape=[jax.ShapeDtypeStruct((8, 1, ROWS, LANES), jnp.float32)] * count,
        name="spread_raw",
        cost_estimate=pl.CostEstimate(
            flops=count * 1_000_000, bytes_accessed=count * 524_288, transcendentals=0
        ),
    )(me, w)


def join_kernel(where, me_ref, *refs):
    me = me_ref[0]
    out_ref = refs[-1]
    for i in range(out_ref.shape[0]):
        for ref, places in zip(refs, where):
            for place, r in places:
                at = pl.multiple_of(((me & 7) ^ r) * LANES, LANES)
                out_ref[i, :, pl.ds(at, LANES)] = ref[place, i]


def join(out, pieces, me, which, other, step, slot=0):
    first, count = which
    assert count % step == 0 and slot % step == 0
    base = slot // step
    in_specs, args, where = [], [], []
    for array, taken, rs in pieces:
        in_specs.append(pl.BlockSpec((taken, step, ROWS, LANES), lambda e, m: (0, base + e, 0, 0)))
        args.append(array)
        where.append([(i, r) for i, r in enumerate(rs)])
    alias = {}
    if out is not None:
        in_specs.append(pl.BlockSpec(memory_space=pl.ANY))
        args.append(out)
        alias = {len(args): 0}
    return pl.pallas_call(
        functools.partial(join_kernel, where),
        grid_spec=pltpu.PrefetchScalarGridSpec(
            num_scalar_prefetch=1,
            grid=(count // step,),
            in_specs=in_specs,
            out_specs=pl.BlockSpec(
                (pl.Element(step), pl.Element(ROWS), pl.Element(1024)),
                lambda e, m: (first + e * step, 0, ((m[0] >> 3) ^ other) * 1024),
            ),
        ),
        out_shape=jax.ShapeDtypeStruct((EXPERTS, ROWS, D_MODEL), jnp.bfloat16),
        input_output_aliases=alias,
        name="join",
        cost_estimate=pl.CostEstimate(
            flops=count * 1_000_000, bytes_accessed=count * 262_144, transcendentals=0
        ),
    )(me, *args)


def plane(arrays):
    have = [arrays[0]] + [swap(arrays[k], k) for k in (1, 2, 3)]
    over_y = swap(jnp.concatenate([a[1:2] for a in have], 0), 4)
    return have, over_y


def plane_y(arrays):
    kept, sent = arrays
    over_y = swap(sent, 4)
    pieces = [(kept, 1, [0]), (over_y, 1, [4])]
    for k in (1, 2, 3):
        both = jnp.concatenate([kept[k : k + 1], over_y[k : k + 1]], 0)
        pieces.append((swap(both, k), 2, [k, 4 + k]))
    return pieces


def by_x(came):
    return [came[2 * k : 2 * k + 2] for k in range(4)]


def pieces_of(have, over_y):
    return [(have[k], 1, [k]) for k in range(4)] + [(over_y, 4, [4, 5, 6, 7])]


def router_kernel(where, me_ref, *refs):
    me = me_ref[0]
    for ref, places in zip(refs, where):
        for place, r in places:
            for z in range(2):
                at = pl.multiple_of((me ^ (8 * z + r)) * LANES, LANES)
                refs[-1][:, pl.ds(at, LANES)] = ref[place, z]


def router_join(pieces, me, slot):
    where = [list(enumerate(rs)) for _, _, rs in pieces]
    assert slot % 2 == 0
    return pl.pallas_call(
        functools.partial(router_kernel, where),
        grid_spec=pltpu.PrefetchScalarGridSpec(
            num_scalar_prefetch=1,
            grid=(1,),
            in_specs=[
                pl.BlockSpec((taken, 2, ROWS, LANES), lambda e, m: (0, slot // 2, 0, 0))
                for _, taken, _ in pieces
            ],
            out_specs=pl.BlockSpec((ROWS, D_MODEL), lambda e, m: (0, 0)),
        ),
        out_shape=jax.ShapeDtypeStruct((ROWS, D_MODEL), jnp.bfloat16),
        name="router",
        cost_estimate=pl.CostEstimate(flops=2_000_000, bytes_accessed=524_288, transcendentals=0),
    )(me, *[array for array, _, _ in pieces])


def on_device(w_down, router_weight, router_gain):
    index = lax.axis_index("fsdp").astype(jnp.int32)
    me = index.reshape(1)

    sums = jnp.sum(jnp.abs(w_down), axis=2).reshape(EXPERTS, 8, LANES)
    for k in (1, 2, 4, 8):
        sums = sums + swap(sums, k)

    part = (router_weight * router_gain[:, None]).astype(jnp.bfloat16).T
    part = lax.all_to_all(jnp.broadcast_to(part[None], (4, 16, LANES)), "ep", 0, 0, tiled=True)
    part = part.reshape(ROWS, LANES)
    router = jnp.stack([part, swap(part, 8)])

    raws = spread_raw(w_down, me, E)
    raws = [swap(raw, 8) for raw in raws]

    (oth_f,) = spread(w_down, sums, me, F, 1, 1, 7)
    came_f = swap(oth_f, 8)
    oth_l = spread(w_down, sums, me, L, 1, 4, 7)
    own_b = spread_own(w_down, sums, router, raws, me, B)
    own_a = spread(w_down, sums, me, A, 0, 4, 5)

    plane_l = plane(oth_l)
    last = jnp.concatenate([a[0:1] for a in plane_l[0]] + [plane_l[1]], 0)
    came_l = swap(last, 8)
    plane_b = plane_y(own_b)
    plane_a = plane(own_a)
    plane_f = plane(by_x(came_f))

    scale = lax.dynamic_slice_in_dim(sums.reshape(EXPERTS, 16, ROWS), index, 1, 1)[:, 0] / D_MODEL

    out = join(None, pieces_of(*plane_a), me, A, 0, 5)
    out = join(out, plane_b, me, B, 0, B[1])
    serve_router = router_join(plane_b, me, B[1]).T
    out = join(out, plane_b, me, E, 1, 2, B[1] + 2)
    out = join(out, pieces_of(*plane_f), me, F, 1, 7)
    out = join(out, [(came_l, 8, list(range(8)))], me, L, 1, 7)
    return (out, scale, serve_router)


def solution(mesh):
    return jax.shard_map(
        on_device,
        mesh=mesh,
        in_specs=(P(("unit", "ep"), None, "fsdp"), P(("unit", "fsdp"), "ep"), P(("unit", "fsdp"))),
        out_specs=(P(("unit", "ep"), "fsdp", None), P(("unit", "ep"), "fsdp"), P("unit", None)),
        check_vma=False,
    )
```

time: 202 us -> 191 us (0.946)
  the two profiles are of different devices: /device:TPU:1 before, /device:TPU:80 now
where the time goes in v2:
time: 191 us; the launch traced here: 190 us
  waiting for transfers between devices  72.9 us (38%)
  starting transfers between devices  66.2 us (35%)
  Pallas kernels  30.2 us (16%)
  local copies, waits for them, and re-layouts  10.4 us (5%)
  other arithmetic  9.39 us (5%)
    ppermute x25, waiting for transfers between devices, swap(): lax.ppermute(shard, 'fsdp', [(i, i ^ k) for i in range(lax.axis_size('fsd...  72.9 us
    ppermute x25, starting transfers between devices, swap(): lax.ppermute(shard, 'fsdp', [(i, i ^ k) for i in range(lax.axis_size('fsd...  61.5 us
    pallas_call x3, Pallas kernels, spread(): pl.pallas_call(functools.partial(spread_kernel, other, scaled), grid_spec...  11.9 us
    pallas_call x5, Pallas kernels, join(): pl.pallas_call(functools.partial(join_kernel, where), grid_spec=pltpu.Pre...  10.9 us
    reduce_sum x1, other arithmetic, on_device(): sums = jnp.sum(jnp.abs(w_down), axis=2).reshape(EXPERTS, 8, LANES)  5.62 us
    all_to_all x1, starting transfers between devices, on_device(): lax.all_to_all(jnp.broadcast_to(part[None], (4, 16, LANES)), 'ep', 0, 0,...  4.68 us
  transfers between devices with their start and end apart: 26, of which 12 were waited for; matrix products, arithmetic and copies ran while one was open for 7% of the time, Pallas kernels for 15%

profile of v2, /device:TPU:80, one launch (start us, length us, event | category | flops | bytes accessed | tf_op | source)
XLA Modules:
  0.0 190.1 jit_solution(3882962038314550519)
XLA Ops:
  0.7 5.6 %abs_reduce_fusion = f32[16,1024]{1,0:T(8,128)S(1)} fusion(f32[16,1024,128]{2,1,0:T(8,128)} %w_ref.9), kind=kLoop, calls=%fused_computation | loop fusion | flops 4177920 | bytes 8454144 | tf_op jit(solution)/shard_map/reduce_sum | solution.py:269
  7.9 2.8 %collective-permute-done = f32[16,8,128]{2,1,0:T(8,128)S(1)} collective-permute-done((f32[16,8,128]{2,1,0:T(8,128)S(1)}, f32[16,8,128]{2,1,0:T(8,128)S(1)}, u32[]{:S(2)}, u32[]{:S(2)}) %collective-permute-start) | collective-permute-done | bytes 65568 | tf_op jit(solution)/shard_map/ppermute | solution.py:21
  10.7 3.1 %collective-permute-start.1 = (f32[16,8,128]{2,1,0:T(8,128)S(1)}, f32[16,8,128]{2,1,0:T(8,128)S(1)}, u32[]{:S(2)}, u32[]{:S(2)}) collective-permute-start(f32[16,8,128]{2,1,0:T(8,128)S(1)} %bitcast_add_fusion), channel_id=1, source_target_pairs={{0,2},{1,3},{2,0},{3,1},{4,6},{5,7},{6,4},{7,5},{8,10},{9,11},{10,... | collective-permute-start | bytes 196616 | tf_op jit(solution)/shard_map/ppermute | solution.py:21
  13.8 2.7 %collective-permute-done.1 = f32[16,8,128]{2,1,0:T(8,128)S(1)} collective-permute-done((f32[16,8,128]{2,1,0:T(8,128)S(1)}, f32[16,8,128]{2,1,0:T(8,128)S(1)}, u32[]{:S(2)}, u32[]{:S(2)}) %collective-permute-start.1) | collective-permute-done | bytes 65568 | tf_op jit(solution)/shard_map/ppermute | solution.py:21
  17.0 5.4 %collective-permute-done.2 = f32[16,8,128]{2,1,0:T(8,128)S(1)} collective-permute-done((f32[16,8,128]{2,1,0:T(8,128)S(1)}, f32[16,8,128]{2,1,0:T(8,128)S(1)}, u32[]{:S(2)}, u32[]{:S(2)}) %collective-permute-start.2) | collective-permute-done | bytes 65568 | tf_op jit(solution)/shard_map/ppermute | solution.py:21
  22.4 5.5 %collective-permute-start.3 = (f32[16,8,128]{2,1,0:T(8,128)S(1)}, f32[16,8,128]{2,1,0:T(8,128)S(1)}, u32[]{:S(2)}, u32[]{:S(2)}) collective-permute-start(f32[16,8,128]{2,1,0:T(8,128)S(1)} %add.17), channel_id=1, source_target_pairs={{0,8},{1,9},{2,10},{3,11},{4,12},{5,13},{6,14},{7,15},{8,0},{9,1},... | collective-permute-start | bytes 196616 | tf_op jit(solution)/shard_map/ppermute | solution.py:21
  28.5 4.7 %all-to-all-start = ((bf16[4,16,128]{2,1,0:T(8,128)(2,1)}), bf16[4,16,128]{2,1,0:T(8,128)(2,1)S(1)}, u32[]{:S(2)}, u32[]{:S(2)}) async-start(bf16[4,16,128]{2,1,0:T(8,128)(2,1)} %broadcast_in_dim.2), calls=%async_computation | async-start | bytes 32768 | tf_op jit(solution)/shard_map/all_to_all | solution.py:274
  33.2 1.9 spread_raw.1
  36.5 4.5 %collective-permute-start.16 = (f32[8,1,64,128]{3,2,1,0:T(8,128)}, f32[8,1,64,128]{3,2,1,0:T(8,128)}, u32[]{:S(2)}, u32[]{:S(2)}) collective-permute-start(f32[8,1,64,128]{3,2,1,0:T(8,128)} %get-tuple-element.20), channel_id=1, source_target_pairs={{0,8},{1,9},{2,10},{3,11},{4,12},{5,13},{6,14},{7,15},{8,0},{9,1},... | collective-permute-start | bytes 786440 | tf_op jit(solution)/shard_map/ppermute | solution.py:21
  43.0 4.3 %spread.5 = (bf16[2,10,64,128]{3,2,1,0:T(8,128)(2,1)}, bf16[2,10,64,128]{3,2,1,0:T(8,128)(2,1)}, bf16[2,10,64,128]{3,2,1,0:T(8,128)(2,1)}, bf16[2,10,64,128]{3,2,1,0:T(8,128)(2,1)}) custom-call(s32[1]{0:T(128)} %bitcast.me_ref, f32[16,1024,128]{2,1,0:T(8,128)} %w_ref.9, f32[16,8,128]{2,1,0:T(8,128)} %add.18.refs_0_.s_ref), custom_call_target="tpu_custom_call" | custom-call | flops 10000000 | bytes 3932160 | tf_op jit(solution)/shard_map/spread/pallas_call | solution.py:74
  47.4 3.8 %spread.4 = bf16[8,7,64,128]{3,2,1,0:T(8,128)(2,1)} custom-call(s32[1]{0:T(128)} %bitcast.me_ref, f32[16,1024,128]{2,1,0:T(8,128)} %w_ref.9, f32[16,8,128]{2,1,0:T(8,128)} %add.18.refs_0_.s_ref), custom_call_target="tpu_custom_call" | custom-call | flops 7000000 | bytes 2752512 | tf_op jit(solution)/shard_map/spread/pallas_call | solution.py:74
  51.2 3.8 %spread.3 = (bf16[2,7,64,128]{3,2,1,0:T(8,128)(2,1)}, bf16[2,7,64,128]{3,2,1,0:T(8,128)(2,1)}, bf16[2,7,64,128]{3,2,1,0:T(8,128)(2,1)}, bf16[2,7,64,128]{3,2,1,0:T(8,128)(2,1)}) custom-call(s32[1]{0:T(128)} %bitcast.me_ref, f32[16,1024,128]{2,1,0:T(8,128)} %w_ref.9, f32[16,8,128]{2,1,0:T(8,128)} %add.18.refs_0_.s_ref), custom_call_target="tpu_custom_call" | custom-call | flops 7000000 | bytes 2752512 | tf_op jit(solution)/shard_map/spread/pallas_call | solution.py:74
  58.0 8.4 %collective-permute-done.4 = bf16[2,7,64,128]{3,2,1,0:T(8,128)(2,1)S(1)} collective-permute-done((bf16[2,7,64,128]{3,2,1,0:T(8,128)(2,1)}, bf16[2,7,64,128]{3,2,1,0:T(8,128)(2,1)S(1)}, u32[]{:S(2)}, u32[]{:S(2)}) %collective-permute-start.4) | collective-permute-done | bytes 229408 | tf_op jit(solution)/shard_map/ppermute | solution.py:21
  66.3 3.8 %collective-permute-start.5 = (bf16[2,7,64,128]{3,2,1,0:T(8,128)(2,1)}, bf16[2,7,64,128]{3,2,1,0:T(8,128)(2,1)S(1)}, u32[]{:S(2)}, u32[]{:S(2)}) collective-permute-start(bf16[2,7,64,128]{3,2,1,0:T(8,128)(2,1)} %get-tuple-element.17), channel_id=1, source_target_pairs={{0,2},{1,3},{2,0},{3,1},{4,6},{5,7},{6,4},{7,5},{8,10},{9,11},{10,... | collective-permute-start | bytes 688136 | tf_op jit(solution)/shard_map/ppermute | solution.py:21
  70.2 4.3 %collective-permute-done.5 = bf16[2,7,64,128]{3,2,1,0:T(8,128)(2,1)S(1)} collective-permute-done((bf16[2,7,64,128]{3,2,1,0:T(8,128)(2,1)}, bf16[2,7,64,128]{3,2,1,0:T(8,128)(2,1)S(1)}, u32[]{:S(2)}, u32[]{:S(2)}) %collective-permute-start.5) | collective-permute-done | bytes 229408 | tf_op jit(solution)/shard_map/ppermute | solution.py:21
  74.5 3.3 %collective-permute-start.6 = (bf16[2,7,64,128]{3,2,1,0:T(8,128)(2,1)}, bf16[2,7,64,128]{3,2,1,0:T(8,128)(2,1)S(1)}, u32[]{:S(2)}, u32[]{:S(2)}) collective-permute-start(bf16[2,7,64,128]{3,2,1,0:T(8,128)(2,1)} %get-tuple-element.18), channel_id=1, source_target_pairs={{0,3},{1,2},{2,1},{3,0},{4,7},{5,6},{6,5},{7,4},{8,11},{9,10},{10,... | collective-permute-start | bytes 688136 | tf_op jit(solution)/shard_map/ppermute | solution.py:21
  77.8 4.2 %collective-permute-done.6 = bf16[2,7,64,128]{3,2,1,0:T(8,128)(2,1)S(1)} collective-permute-done((bf16[2,7,64,128]{3,2,1,0:T(8,128)(2,1)}, bf16[2,7,64,128]{3,2,1,0:T(8,128)(2,1)S(1)}, u32[]{:S(2)}, u32[]{:S(2)}) %collective-permute-start.6) | collective-permute-done | bytes 229408 | tf_op jit(solution)/shard_map/ppermute | solution.py:21
  82.0 4.5 %collective-permute-start.9 = (bf16[8,7,64,128]{3,2,1,0:T(8,128)(2,1)S(1)}, bf16[8,7,64,128]{3,2,1,0:T(8,128)(2,1)S(1)}, u32[]{:S(2)}, u32[]{:S(2)}) collective-permute-start(bf16[8,7,64,128]{3,2,1,0:T(8,128)(2,1)S(1)} %copy-done.5), channel_id=1, source_target_pairs={{0,8},{1,9},{2,10},{3,11},{4,12},{5,13},{6,14},{7,15},{8,0},{9,1},... | collective-permute-start | bytes 2752520 | tf_op jit(solution)/shard_map/ppermute | solution.py:21
  88.3 5.8 %collective-permute-start.22 = (bf16[2,10,64,128]{3,2,1,0:T(8,128)(2,1)}, bf16[2,10,64,128]{3,2,1,0:T(8,128)(2,1)S(1)}, u32[]{:S(2)}, u32[]{:S(2)}) collective-permute-start(bf16[2,10,64,128]{3,2,1,0:T(8,128)(2,1)} %get-tuple-element.25), channel_id=1, source_target_pairs={{0,2},{1,3},{2,0},{3,1},{4,6},{5,7},{6,4},{7,5},{8,10},{9,11},{10,... | collective-permute-start | bytes 983048 | tf_op jit(solution)/shard_map/ppermute | solution.py:21
  96.5 3.8 %spread_own.1 = (bf16[4,10,64,128]{3,2,1,0:T(8,128)(2,1)}, bf16[4,10,64,128]{3,2,1,0:T(8,128)(2,1)}) custom-call(s32[1]{0:T(128)} %bitcast.me_ref, f32[16,1024,128]{2,1,0:T(8,128)} %w_ref.9, f32[16,8,128]{2,1,0:T(8,128)} %add.18.refs_0_.s_ref, bf16[2,64,128]{2,1,0:T(8,128)(2,1)} %pad_maximum_fusion.6.router_ref, ...), custom_call_target="tpu_custom_call" | custom-call | flops 10000000 | bytes 3932160 | tf_op jit(solution)/shard_map/spread_own/pallas_call | solution.py:118
  100.3 3.2 %collective-permute-start.17 = (bf16[4,10,64,128]{3,2,1,0:T(8,128)(2,1)}, bf16[4,10,64,128]{3,2,1,0:T(8,128)(2,1)S(1)}, u32[]{:S(2)}, u32[]{:S(2)}) collective-permute-start(bf16[4,10,64,128]{3,2,1,0:T(8,128)(2,1)} %get-tuple-element.22), channel_id=1, source_target_pairs={{0,4},{1,5},{2,6},{3,7},{4,0},{5,1},{6,2},{7,3},{8,12},{9,13},{10,... | collective-permute-start | bytes 1966088 | tf_op jit(solution)/shard_map/ppermute | solution.py:21
  107.0 2.3 %collective-permute-done.7 = bf16[4,7,64,128]{3,2,1,0:T(8,128)(2,1)} collective-permute-done((bf16[4,7,64,128]{3,2,1,0:T(8,128)(2,1)}, bf16[4,7,64,128]{3,2,1,0:T(8,128)(2,1)}, u32[]{:S(2)}, u32[]{:S(2)}) %collective-permute-start.7) | collective-permute-done | bytes 458784 | tf_op jit(solution)/shard_map/ppermute | solution.py:21
  111.2 19.7 %collective-permute-done.9 = bf16[8,7,64,128]{3,2,1,0:T(8,128)(2,1)S(1)} collective-permute-done((bf16[8,7,64,128]{3,2,1,0:T(8,128)(2,1)S(1)}, bf16[8,7,64,128]{3,2,1,0:T(8,128)(2,1)S(1)}, u32[]{:S(2)}, u32[]{:S(2)}) %collective-permute-start.9) | collective-permute-done | bytes 917536 | tf_op jit(solution)/shard_map/ppermute | solution.py:21
  133.4 12.5 %collective-permute-start.11 = (bf16[2,7,64,128]{3,2,1,0:T(8,128)(2,1)S(1)}, bf16[2,7,64,128]{3,2,1,0:T(8,128)(2,1)S(1)}, u32[]{:S(2)}, u32[]{:S(2)}) collective-permute-start(bf16[2,7,64,128]{3,2,1,0:T(8,128)(2,1)S(1)} %get-tuple-element.28), channel_id=1, source_target_pairs={{0,2},{1,3},{2,0},{3,1},{4,6},{5,7},{6,4},{7,5},{8,10},{9,11},{10,... | collective-permute-start | bytes 688136 | tf_op jit(solution)/shard_map/ppermute | solution.py:21
  146.2 11.0 %collective-permute-done.11.refs_2_ = bf16[2,7,64,128]{3,2,1,0:T(8,128)(2,1)S(1)} collective-permute-done((bf16[2,7,64,128]{3,2,1,0:T(8,128)(2,1)S(1)}, bf16[2,7,64,128]{3,2,1,0:T(8,128)(2,1)S(1)}, u32[]{:S(2)}, u32[]{:S(2)}) %collective-permute-start.11) | collective-permute-done | bytes 229408 | tf_op jit(solution)/shard_map/ppermute | solution.py:21
  159.0 5.8 %collective-permute-start.20 = (bf16[2,10,64,128]{3,2,1,0:T(8,128)(2,1)S(1)}, bf16[2,10,64,128]{3,2,1,0:T(8,128)(2,1)S(1)}, u32[]{:S(2)}, u32[]{:S(2)}) collective-permute-start(bf16[2,10,64,128]{3,2,1,0:T(8,128)(2,1)S(1)} %pad_maximum_fusion.5), channel_id=1, source_target_pairs={{0,3},{1,2},{2,1},{3,0},{4,7},{5,6},{6,5},{7,4},{8,11},{9,10},{10,... | collective-permute-start | bytes 983048 | tf_op jit(solution)/shard_map/ppermute | solution.py:21
  166.2 3.9 %collective-permute-done.19.refs_3_ = bf16[2,10,64,128]{3,2,1,0:T(8,128)(2,1)S(1)} collective-permute-done((bf16[2,10,64,128]{3,2,1,0:T(8,128)(2,1)S(1)}, bf16[2,10,64,128]{3,2,1,0:T(8,128)(2,1)S(1)}, u32[]{:S(2)}, u32[]{:S(2)}) %collective-permute-start.19) | collective-permute-done | bytes 327712 | tf_op jit(solution)/shard_map/ppermute | solution.py:21
  170.1 6.6 %collective-permute-done.20.refs_4_ = bf16[2,10,64,128]{3,2,1,0:T(8,128)(2,1)S(1)} collective-permute-done((bf16[2,10,64,128]{3,2,1,0:T(8,128)(2,1)S(1)}, bf16[2,10,64,128]{3,2,1,0:T(8,128)(2,1)S(1)}, u32[]{:S(2)}, u32[]{:S(2)}) %collective-permute-start.20) | collective-permute-done | bytes 327712 | tf_op jit(solution)/shard_map/ppermute | solution.py:21
  179.1 2.3 %join.5.refs_5_ = bf16[16,64,2048]{2,1,0:T(8,128)(2,1)} custom-call(s32[1]{0:T(128)} %bitcast.me_ref, bf16[2,10,64,128]{3,2,1,0:T(8,128)(2,1)} %get-tuple-element.23.refs_0_, bf16[2,10,64,128]{3,2,1,0:T(8,128)(2,1)} %copy-done.7, bf16[2,10,64,128]{3,2,1,0:T(8,128)(2,1)} %copy-done.8, bf16[2,10,64,128]{3,2,1,0:T(8,128)(2,1)} %collective-permute-done.23.refs_3_, ...), custom_call_target="tpu_custom_call" | custom-call | flops 10000000 | bytes 2621440 | tf_op jit(solution)/shard_map/join/pallas_call | solution.py:192
  181.5 2.3 %join.6.refs_5_ = bf16[16,64,2048]{2,1,0:T(8,128)(2,1)} custom-call(s32[1]{0:T(128)} %bitcast.me_ref, bf16[4,10,64,128]{3,2,1,0:T(8,128)(2,1)} %get-tuple-element.21.refs_0_, bf16[4,10,64,128]{3,2,1,0:T(8,128)(2,1)} %copy-done, bf16[2,10,64,128]{3,2,1,0:T(8,128)(2,1)} %copy-done.1, ...), custom_call_target="tpu_custom_call", output_to_operand_aliasing={{}: (6, {})} | custom-call | flops 6000000 | bytes 1572864 | tf_op jit(solution)/shard_map/join/pallas_call | solution.py:192
  185.4 2.3 %join.8.refs_1_ = bf16[16,64,2048]{2,1,0:T(8,128)(2,1)} custom-call(s32[1]{0:T(128)} %bitcast.me_ref, bf16[2,7,64,128]{3,2,1,0:T(8,128)(2,1)} %get-tuple-element.30.refs_0_, bf16[2,7,64,128]{3,2,1,0:T(8,128)(2,1)} %copy-done.10, bf16[2,7,64,128]{3,2,1,0:T(8,128)(2,1)} %copy-done.11, ...), custom_call_target="tpu_custom_call", output_to_operand_aliasing={{}: (6, {})} | custom-call | flops 7000000 | bytes 1835008 | tf_op jit(solution)/shard_map/join/pallas_call | solution.py:192
  187.8 2.3 %join.9 = bf16[16,64,2048]{2,1,0:T(8,128)(2,1)} custom-call(s32[1]{0:T(128)} %bitcast.me_ref, bf16[8,7,64,128]{3,2,1,0:T(8,128)(2,1)} %collective-permute-done.8.refs_0_, bf16[16,64,2048]{2,1,0:T(8,128)(2,1)} %join.8.refs_1_), custom_call_target="tpu_custom_call", output_to_operand_aliasing={{}: (2, {})} | custom-call | flops 7000000 | bytes 1835008 | tf_op jit(solution)/shard_map/join/pallas_call | solution.py:192
  (97 shorter events, 28.8 us)
Async XLA Ops:
  6.3 4.4 %collective-permute-start = (f32[16,8,128]{2,1,0:T(8,128)S(1)}, f32[16,8,128]{2,1,0:T(8,128)S(1)}, u32[]{:S(2)}, u32[]{:S(2)}) collective-permute-start(f32[16,8,128]{2,1,0:T(8,128)S(1)} %bitcast.14), channel_id=1, source_target_pairs={{0,1},{1,0},{2,3},{3,2},{4,5},{5,4},{6,7},{7,6},{8,9},{9,8},{10,11... | collective-permute-start | bytes 196616 | tf_op jit(solution)/shard_map/ppermute | solution.py:21
  10.7 5.9 %collective-permute-start.1 = (f32[16,8,128]{2,1,0:T(8,128)S(1)}, f32[16,8,128]{2,1,0:T(8,128)S(1)}, u32[]{:S(2)}, u32[]{:S(2)}) collective-permute-start(f32[16,8,128]{2,1,0:T(8,128)S(1)} %bitcast_add_fusion), channel_id=1, source_target_pairs={{0,2},{1,3},{2,0},{3,1},{4,6},{5,7},{6,4},{7,5},{8,10},{9,11},{10,... | collective-permute-start | bytes 196616 | tf_op jit(solution)/shard_map/ppermute | solution.py:21
  16.5 5.9 %collective-permute-start.2 = (f32[16,8,128]{2,1,0:T(8,128)S(1)}, f32[16,8,128]{2,1,0:T(8,128)S(1)}, u32[]{:S(2)}, u32[]{:S(2)}) collective-permute-start(f32[16,8,128]{2,1,0:T(8,128)S(1)} %add.16), channel_id=1, source_target_pairs={{0,4},{1,5},{2,6},{3,7},{4,0},{5,1},{6,2},{7,3},{8,12},{9,13},{10,... | collective-permute-start | bytes 196616 | tf_op jit(solution)/shard_map/ppermute | solution.py:21
  22.4 20.0 %collective-permute-start.3 = (f32[16,8,128]{2,1,0:T(8,128)S(1)}, f32[16,8,128]{2,1,0:T(8,128)S(1)}, u32[]{:S(2)}, u32[]{:S(2)}) collective-permute-start(f32[16,8,128]{2,1,0:T(8,128)S(1)} %add.17), channel_id=1, source_target_pairs={{0,8},{1,9},{2,10},{3,11},{4,12},{5,13},{6,14},{7,15},{8,0},{9,1},... | collective-permute-start | bytes 196616 | tf_op jit(solution)/shard_map/ppermute | solution.py:21
  28.5 12.5 %all-to-all-start = ((bf16[4,16,128]{2,1,0:T(8,128)(2,1)}), bf16[4,16,128]{2,1,0:T(8,128)(2,1)S(1)}, u32[]{:S(2)}, u32[]{:S(2)}) async-start(bf16[4,16,128]{2,1,0:T(8,128)(2,1)} %broadcast_in_dim.2), calls=%async_computation | async-start | bytes 32768 | tf_op jit(solution)/shard_map/all_to_all | solution.py:274
  35.1 59.0 %collective-permute-start.15 = (f32[8,1,64,128]{3,2,1,0:T(8,128)}, f32[8,1,64,128]{3,2,1,0:T(8,128)}, u32[]{:S(2)}, u32[]{:S(2)}) collective-permute-start(f32[8,1,64,128]{3,2,1,0:T(8,128)} %get-tuple-element.19), channel_id=1, source_target_pairs={{0,8},{1,9},{2,10},{3,11},{4,12},{5,13},{6,14},{7,15},{8,0},{9,1},... | collective-permute-start | bytes 786440 | tf_op jit(solution)/shard_map/ppermute | solution.py:21
  36.5 57.6 %collective-permute-start.16 = (f32[8,1,64,128]{3,2,1,0:T(8,128)}, f32[8,1,64,128]{3,2,1,0:T(8,128)}, u32[]{:S(2)}, u32[]{:S(2)}) collective-permute-start(f32[8,1,64,128]{3,2,1,0:T(8,128)} %get-tuple-element.20), channel_id=1, source_target_pairs={{0,8},{1,9},{2,10},{3,11},{4,12},{5,13},{6,14},{7,15},{8,0},{9,1},... | collective-permute-start | bytes 786440 | tf_op jit(solution)/shard_map/ppermute | solution.py:21
  41.0 47.3 %collective-permute-start.14 = (bf16[64,128]{1,0:T(8,128)(2,1)S(1)}, bf16[64,128]{1,0:T(8,128)(2,1)S(1)}, u32[]{:S(2)}, u32[]{:S(2)}) collective-permute-start(bf16[64,128]{1,0:T(8,128)(2,1)S(1)} %bitcast.16), channel_id=1, source_target_pairs={{0,8},{1,9},{2,10},{3,11},{4,12},{5,13},{6,14},{7,15},{8,0},{9,1},... | collective-permute-start | bytes 49160 | tf_op jit(solution)/shard_map/ppermute | solution.py:21
  51.2 43.9 %copy-start.4 = (f32[16,8,128]{2,1,0:T(8,128)S(1)}, f32[16,8,128]{2,1,0:T(8,128)}, u32[]{:S(2)}) copy-start(f32[16,8,128]{2,1,0:T(8,128)} %add.18.refs_0_.s_ref) | copy-start | bytes 196612
  51.2 44.7 %copy-start.6 = (bf16[2,10,64,128]{3,2,1,0:T(8,128)(2,1)S(1)}, bf16[2,10,64,128]{3,2,1,0:T(8,128)(2,1)}, u32[]{:S(2)}) copy-start(bf16[2,10,64,128]{3,2,1,0:T(8,128)(2,1)} %get-tuple-element.23.refs_0_) | copy-start | bytes 983044
  55.0 45.4 %collective-permute-start.21 = (bf16[2,10,64,128]{3,2,1,0:T(8,128)(2,1)}, bf16[2,10,64,128]{3,2,1,0:T(8,128)(2,1)S(1)}, u32[]{:S(2)}, u32[]{:S(2)}) collective-permute-start(bf16[2,10,64,128]{3,2,1,0:T(8,128)(2,1)} %get-tuple-element.24), channel_id=1, source_target_pairs={{0,1},{1,0},{2,3},{3,2},{4,5},{5,4},{6,7},{7,6},{8,9},{9,8},{10,11... | collective-permute-start | bytes 983048 | tf_op jit(solution)/shard_map/ppermute | solution.py:21
  56.4 9.9 %collective-permute-start.4 = (bf16[2,7,64,128]{3,2,1,0:T(8,128)(2,1)}, bf16[2,7,64,128]{3,2,1,0:T(8,128)(2,1)S(1)}, u32[]{:S(2)}, u32[]{:S(2)}) collective-permute-start(bf16[2,7,64,128]{3,2,1,0:T(8,128)(2,1)} %get-tuple-element.16), channel_id=1, source_target_pairs={{0,1},{1,0},{2,3},{3,2},{4,5},{5,4},{6,7},{7,6},{8,9},{9,8},{10,11... | collective-permute-start | bytes 688136 | tf_op jit(solution)/shard_map/ppermute | solution.py:21
  66.3 8.1 %collective-permute-start.5 = (bf16[2,7,64,128]{3,2,1,0:T(8,128)(2,1)}, bf16[2,7,64,128]{3,2,1,0:T(8,128)(2,1)S(1)}, u32[]{:S(2)}, u32[]{:S(2)}) collective-permute-start(bf16[2,7,64,128]{3,2,1,0:T(8,128)(2,1)} %get-tuple-element.17), channel_id=1, source_target_pairs={{0,2},{1,3},{2,0},{3,1},{4,6},{5,7},{6,4},{7,5},{8,10},{9,11},{10,... | collective-permute-start | bytes 688136 | tf_op jit(solution)/shard_map/ppermute | solution.py:21
  74.5 7.5 %collective-permute-start.6 = (bf16[2,7,64,128]{3,2,1,0:T(8,128)(2,1)}, bf16[2,7,64,128]{3,2,1,0:T(8,128)(2,1)S(1)}, u32[]{:S(2)}, u32[]{:S(2)}) collective-permute-start(bf16[2,7,64,128]{3,2,1,0:T(8,128)(2,1)} %get-tuple-element.18), channel_id=1, source_target_pairs={{0,3},{1,2},{2,1},{3,0},{4,7},{5,6},{6,5},{7,4},{8,11},{9,10},{10,... | collective-permute-start | bytes 688136 | tf_op jit(solution)/shard_map/ppermute | solution.py:21
  82.0 48.9 %collective-permute-start.9 = (bf16[8,7,64,128]{3,2,1,0:T(8,128)(2,1)S(1)}, bf16[8,7,64,128]{3,2,1,0:T(8,128)(2,1)S(1)}, u32[]{:S(2)}, u32[]{:S(2)}) collective-permute-start(bf16[8,7,64,128]{3,2,1,0:T(8,128)(2,1)S(1)} %copy-done.5), channel_id=1, source_target_pairs={{0,8},{1,9},{2,10},{3,11},{4,12},{5,13},{6,14},{7,15},{8,0},{9,1},... | collective-permute-start | bytes 2752520 | tf_op jit(solution)/shard_map/ppermute | solution.py:21
  88.3 16.4 %collective-permute-start.22 = (bf16[2,10,64,128]{3,2,1,0:T(8,128)(2,1)}, bf16[2,10,64,128]{3,2,1,0:T(8,128)(2,1)S(1)}, u32[]{:S(2)}, u32[]{:S(2)}) collective-permute-start(bf16[2,10,64,128]{3,2,1,0:T(8,128)(2,1)} %get-tuple-element.25), channel_id=1, source_target_pairs={{0,2},{1,3},{2,0},{3,1},{4,6},{5,7},{6,4},{7,5},{8,10},{9,11},{10,... | collective-permute-start | bytes 983048 | tf_op jit(solution)/shard_map/ppermute | solution.py:21
  94.1 10.7 %collective-permute-start.23 = (bf16[2,10,64,128]{3,2,1,0:T(8,128)(2,1)}, bf16[2,10,64,128]{3,2,1,0:T(8,128)(2,1)}, u32[]{:S(2)}, u32[]{:S(2)}) collective-permute-start(bf16[2,10,64,128]{3,2,1,0:T(8,128)(2,1)} %get-tuple-element.26), channel_id=1, source_target_pairs={{0,3},{1,2},{2,1},{3,0},{4,7},{5,6},{6,5},{7,4},{8,11},{9,10},{10,... | collective-permute-start | bytes 983048 | tf_op jit(solution)/shard_map/ppermute | solution.py:21
  94.1 15.3 %collective-permute-start.7 = (bf16[4,7,64,128]{3,2,1,0:T(8,128)(2,1)}, bf16[4,7,64,128]{3,2,1,0:T(8,128)(2,1)}, u32[]{:S(2)}, u32[]{:S(2)}) collective-permute-start(bf16[4,7,64,128]{3,2,1,0:T(8,128)(2,1)} %pad_maximum_fusion.1), channel_id=1, source_target_pairs={{0,4},{1,5},{2,6},{3,7},{4,0},{5,1},{6,2},{7,3},{8,12},{9,13},{10,... | collective-permute-start | bytes 1376264 | tf_op jit(solution)/shard_map/ppermute | solution.py:21
  100.3 45.8 %copy-start.7 = (bf16[2,10,64,128]{3,2,1,0:T(8,128)(2,1)}, bf16[2,10,64,128]{3,2,1,0:T(8,128)(2,1)S(1)}, u32[]{:S(2)}) copy-start(bf16[2,10,64,128]{3,2,1,0:T(8,128)(2,1)S(1)} %collective-permute-done.21.refs_1_) | copy-start | bytes 983044
  100.3 33.0 %collective-permute-start.17 = (bf16[4,10,64,128]{3,2,1,0:T(8,128)(2,1)}, bf16[4,10,64,128]{3,2,1,0:T(8,128)(2,1)S(1)}, u32[]{:S(2)}, u32[]{:S(2)}) collective-permute-start(bf16[4,10,64,128]{3,2,1,0:T(8,128)(2,1)} %get-tuple-element.22), channel_id=1, source_target_pairs={{0,4},{1,5},{2,6},{3,7},{4,0},{5,1},{6,2},{7,3},{8,12},{9,13},{10,... | collective-permute-start | bytes 1966088 | tf_op jit(solution)/shard_map/ppermute | solution.py:21
  104.7 41.2 %copy-start.8 = (bf16[2,10,64,128]{3,2,1,0:T(8,128)(2,1)}, bf16[2,10,64,128]{3,2,1,0:T(8,128)(2,1)S(1)}, u32[]{:S(2)}) copy-start(bf16[2,10,64,128]{3,2,1,0:T(8,128)(2,1)S(1)} %collective-permute-done.22.refs_2_) | copy-start | bytes 983044
  106.7 72.4 %collective-permute-start.24 = (bf16[4,10,64,128]{3,2,1,0:T(8,128)(2,1)}, bf16[4,10,64,128]{3,2,1,0:T(8,128)(2,1)}, u32[]{:S(2)}, u32[]{:S(2)}) collective-permute-start(bf16[4,10,64,128]{3,2,1,0:T(8,128)(2,1)} %pad_maximum_fusion), channel_id=1, source_target_pairs={{0,4},{1,5},{2,6},{3,7},{4,0},{5,1},{6,2},{7,3},{8,12},{9,13},{10,... | collective-permute-start | bytes 1966088 | tf_op jit(solution)/shard_map/ppermute | solution.py:21
  111.2 76.6 %collective-permute-start.8 = (bf16[8,7,64,128]{3,2,1,0:T(8,128)(2,1)}, bf16[8,7,64,128]{3,2,1,0:T(8,128)(2,1)}, u32[]{:S(2)}, u32[]{:S(2)}) collective-permute-start(bf16[8,7,64,128]{3,2,1,0:T(8,128)(2,1)} %constant_dynamic-update-slice_fusion), channel_id=1, source_target_pairs={{0,8},{1,9},{2,10},{3,11},{4,12},{5,13},{6,14},{7,15},{8,0},{9,1},... | collective-permute-start | bytes 2752520 | tf_op jit(solution)/shard_map/ppermute | solution.py:21
  131.7 14.3 %collective-permute-start.10 = (bf16[2,7,64,128]{3,2,1,0:T(8,128)(2,1)S(1)}, bf16[2,7,64,128]{3,2,1,0:T(8,128)(2,1)S(1)}, u32[]{:S(2)}, u32[]{:S(2)}) collective-permute-start(bf16[2,7,64,128]{3,2,1,0:T(8,128)(2,1)S(1)} %get-tuple-element.29), channel_id=1, source_target_pairs={{0,1},{1,0},{2,3},{3,2},{4,5},{5,4},{6,7},{7,6},{8,9},{9,8},{10,11... | collective-permute-start | bytes 688136 | tf_op jit(solution)/shard_map/ppermute | solution.py:21
  133.4 43.3 %copy-start = (bf16[4,10,64,128]{3,2,1,0:T(8,128)(2,1)}, bf16[4,10,64,128]{3,2,1,0:T(8,128)(2,1)S(1)}, u32[]{:S(2)}) copy-start(bf16[4,10,64,128]{3,2,1,0:T(8,128)(2,1)S(1)} %collective-permute-done.17.refs_1_) | copy-start | bytes 1966084
  133.4 23.8 %collective-permute-start.11 = (bf16[2,7,64,128]{3,2,1,0:T(8,128)(2,1)S(1)}, bf16[2,7,64,128]{3,2,1,0:T(8,128)(2,1)S(1)}, u32[]{:S(2)}, u32[]{:S(2)}) collective-permute-start(bf16[2,7,64,128]{3,2,1,0:T(8,128)(2,1)S(1)} %get-tuple-element.28), channel_id=1, source_target_pairs={{0,2},{1,3},{2,0},{3,1},{4,6},{5,7},{6,4},{7,5},{8,10},{9,11},{10,... | collective-permute-start | bytes 688136 | tf_op jit(solution)/shard_map/ppermute | solution.py:21
  145.9 12.9 %collective-permute-start.12 = (bf16[2,7,64,128]{3,2,1,0:T(8,128)(2,1)S(1)}, bf16[2,7,64,128]{3,2,1,0:T(8,128)(2,1)S(1)}, u32[]{:S(2)}, u32[]{:S(2)}) collective-permute-start(bf16[2,7,64,128]{3,2,1,0:T(8,128)(2,1)S(1)} %get-tuple-element.27), channel_id=1, source_target_pairs={{0,3},{1,2},{2,1},{3,0},{4,7},{5,6},{6,5},{7,4},{8,11},{9,10},{10,... | collective-permute-start | bytes 688136 | tf_op jit(solution)/shard_map/ppermute | solution.py:21
  145.9 35.5 %copy-start.10 = (bf16[2,7,64,128]{3,2,1,0:T(8,128)(2,1)}, bf16[2,7,64,128]{3,2,1,0:T(8,128)(2,1)S(1)}, u32[]{:S(2)}) copy-start(bf16[2,7,64,128]{3,2,1,0:T(8,128)(2,1)S(1)} %collective-permute-done.10.refs_1_) | copy-start | bytes 688132
  145.9 13.0 %collective-permute-start.18 = (bf16[2,10,64,128]{3,2,1,0:T(8,128)(2,1)S(1)}, bf16[2,10,64,128]{3,2,1,0:T(8,128)(2,1)S(1)}, u32[]{:S(2)}, u32[]{:S(2)}) collective-permute-start(bf16[2,10,64,128]{3,2,1,0:T(8,128)(2,1)S(1)} %pad_maximum_fusion.3), channel_id=1, source_target_pairs={{0,1},{1,0},{2,3},{3,2},{4,5},{5,4},{6,7},{7,6},{8,9},{9,8},{10,11... | collective-permute-start | bytes 983048 | tf_op jit(solution)/shard_map/ppermute | solution.py:21
  157.2 13.0 %collective-permute-start.19 = (bf16[2,10,64,128]{3,2,1,0:T(8,128)(2,1)S(1)}, bf16[2,10,64,128]{3,2,1,0:T(8,128)(2,1)S(1)}, u32[]{:S(2)}, u32[]{:S(2)}) collective-permute-start(bf16[2,10,64,128]{3,2,1,0:T(8,128)(2,1)S(1)} %pad_maximum_fusion.4), channel_id=1, source_target_pairs={{0,2},{1,3},{2,0},{3,1},{4,6},{5,7},{6,4},{7,5},{8,10},{9,11},{10,... | collective-permute-start | bytes 983048 | tf_op jit(solution)/shard_map/ppermute | solution.py:21
  158.8 26.6 %collective-permute-start.13 = (bf16[4,7,64,128]{3,2,1,0:T(8,128)(2,1)S(1)}, bf16[4,7,64,128]{3,2,1,0:T(8,128)(2,1)}, u32[]{:S(2)}, u32[]{:S(2)}) collective-permute-start(bf16[4,7,64,128]{3,2,1,0:T(8,128)(2,1)S(1)} %pad_maximum_fusion.2), channel_id=1, source_target_pairs={{0,4},{1,5},{2,6},{3,7},{4,0},{5,1},{6,2},{7,3},{8,12},{9,13},{10,... | collective-permute-start | bytes 1376264 | tf_op jit(solution)/shard_map/ppermute | solution.py:21
  159.0 17.7 %collective-permute-start.20 = (bf16[2,10,64,128]{3,2,1,0:T(8,128)(2,1)S(1)}, bf16[2,10,64,128]{3,2,1,0:T(8,128)(2,1)S(1)}, u32[]{:S(2)}, u32[]{:S(2)}) collective-permute-start(bf16[2,10,64,128]{3,2,1,0:T(8,128)(2,1)S(1)} %pad_maximum_fusion.5), channel_id=1, source_target_pairs={{0,3},{1,2},{2,1},{3,0},{4,7},{5,6},{6,5},{7,4},{8,11},{9,10},{10,... | collective-permute-start | bytes 983048 | tf_op jit(solution)/shard_map/ppermute | solution.py:21
  (10 other events, 167.6 us)

commit v3 on v2

--- a/solution.py
+++ b/solution.py
@@ -19,6 +19,10 @@
 
 def swap(shard, k):
     return lax.ppermute(shard, "fsdp", [(i, i ^ k) for i in range(lax.axis_size("fsdp"))])
+
+
+def pack(parts):
+    return jnp.concatenate([array[first:end] for array, first, end in parts], 0)
 
 
 def relative(s, m):
@@ -88,7 +92,7 @@
     )(me, *args)
 
 
-def own_kernel(me_ref, w_ref, s_ref, router_ref, *refs):
+def own_kernel(me_ref, w_ref, s_ref, near_ref, far_ref, *refs):
     m = me_ref[0]
     raws, outs = refs[:-2], refs[-2:]
     count = w_ref.shape[0]
@@ -104,8 +108,8 @@
                 outs[r >> 2][r & 3, count + 2 + raw] = block.astype(jnp.bfloat16)
     for out in outs:
         for x in range(4):
-            for z in range(2):
-                out[x, count + z] = router_ref[z]
+            out[x, count] = near_ref[...]
+            out[x, count + 1] = far_ref[...]
 
 
 def spread_own(w, sums, router, raws, me, which):
@@ -129,7 +133,8 @@
                     (pl.Element(count), pl.Element(8), pl.Element(LANES)),
                     lambda e, m: (first, 0, 0),
                 ),
-                whole(2, ROWS, LANES),
+                whole(ROWS, LANES),
+                whole(ROWS, LANES),
             ]
             + [whole(8, 1, ROWS, LANES)] * len(raws),
             out_specs=[whole(4, slots, ROWS, LANES)] * 2,
@@ -139,7 +144,7 @@
         cost_estimate=pl.CostEstimate(
             flops=slots * 1_000_000, bytes_accessed=slots * 393_216, transcendentals=0
         ),
-    )(me, w, sums, router, *raws)
+    )(me, w, sums, *router, *raws)
 
 
 def spread_raw(w, me, which):
@@ -211,8 +216,7 @@
 
 def plane(arrays):
     have = [arrays[0]] + [swap(arrays[k], k) for k in (1, 2, 3)]
-    over_y = swap(jnp.concatenate([a[1:2] for a in have], 0), 4)
-    return have, over_y
+    return have, swap(pack([(a, 1, 2) for a in have]), 4)
 
 
 def plane_y(arrays):
@@ -220,7 +224,7 @@
     over_y = swap(sent, 4)
     pieces = [(kept, 1, [0]), (over_y, 1, [4])]
     for k in (1, 2, 3):
-        both = jnp.concatenate([kept[k : k + 1], over_y[k : k + 1]], 0)
+        both = pack([(kept, k, k + 1), (over_y, k, k + 1)])
         pieces.append((swap(both, k), 2, [k, 4 + k]))
     return pieces
 
@@ -273,7 +277,7 @@
     part = (router_weight * router_gain[:, None]).astype(jnp.bfloat16).T
     part = lax.all_to_all(jnp.broadcast_to(part[None], (4, 16, LANES)), "ep", 0, 0, tiled=True)
     part = part.reshape(ROWS, LANES)
-    router = jnp.stack([part, swap(part, 8)])
+    router = (part, swap(part, 8))
 
     raws = spread_raw(w_down, me, E)
     raws = [swap(raw, 8) for raw in raws]
@@ -285,7 +289,7 @@
     own_a = spread(w_down, sums, me, A, 0, 4, 5)
 
     plane_l = plane(oth_l)
-    last = jnp.concatenate([a[0:1] for a in plane_l[0]] + [plane_l[1]], 0)
+    last = pack([(a, 0, 1) for a in plane_l[0]] + [(plane_l[1], 0, 4)])
     came_l = swap(last, 8)
     plane_b = plane_y(own_b)
     plane_a = plane(own_a)
@@ -293,8 +297,8 @@
 
     scale = lax.dynamic_slice_in_dim(sums.reshape(EXPERTS, 16, ROWS), index, 1, 1)[:, 0] / D_MODEL
 
-    out = join(None, pieces_of(*plane_a), me, A, 0, 5)
-    out = join(out, plane_b, me, B, 0, B[1])
+    out = join(None, plane_b, me, B, 0, B[1])
+    out = join(out, pieces_of(*plane_a), me, A, 0, 5)
     serve_router = router_join(plane_b, me, B[1]).T
     out = join(out, plane_b, me, E, 1, 2, B[1] + 2)
     out = join(out, pieces_of(*plane_f), me, F, 1, 7)

time: 191 us -> 181 us (0.948)
  the two profiles are of different devices: /device:TPU:80 before, /device:TPU:96 now
where the time goes in v3:
time: 181 us; the launch traced here: 180 us
  waiting for transfers between devices  69.1 us (38%)
  starting transfers between devices  59.9 us (33%)
  Pallas kernels  30.3 us (17%)
  local copies, waits for them, and re-layouts  11.1 us (6%)
  other arithmetic  8.86 us (5%)
    ppermute x25, waiting for transfers between devices, swap(): lax.ppermute(shard, 'fsdp', [(i, i ^ k) for i in range(lax.axis_size('fsd...  69.1 us
    ppermute x25, starting transfers between devices, swap(): lax.ppermute(shard, 'fsdp', [(i, i ^ k) for i in range(lax.axis_size('fsd...  54.8 us
    pallas_call x3, Pallas kernels, spread(): pl.pallas_call(functools.partial(spread_kernel, other, scaled), grid_spec...  12 us
    pallas_call x5, Pallas kernels, join(): pl.pallas_call(functools.partial(join_kernel, where), grid_spec=pltpu.Pre...  10.9 us
    reduce_sum x1, other arithmetic, on_device(): sums = jnp.sum(jnp.abs(w_down), axis=2).reshape(EXPERTS, 8, LANES)  5.62 us
    all_to_all x1, starting transfers between devices, on_device(): lax.all_to_all(jnp.broadcast_to(part[None], (4, 16, LANES)), 'ep', 0, 0,...  5.13 us
    slice x14, local copies, waits for them, and re-layouts, pack(): return jnp.concatenate([array[first:end] for array, first, end in parts], 0)  3.87 us
    pallas_call x1, Pallas kernels, spread_own(): pl.pallas_call(own_kernel, grid_spec=pltpu.PrefetchScalarGridSpec(num_sca...  3.84 us
  transfers between devices with their start and end apart: 26, of which 12 were waited for; matrix products, arithmetic and copies ran while one was open for 7% of the time, Pallas kernels for 16%

profile of v3, /device:TPU:96, one launch (start us, length us, event | category | flops | bytes accessed | tf_op | source)
XLA Modules:
  0.0 180.2 jit_solution(1406608155107536841)
XLA Ops:
  0.7 5.6 %abs_reduce_fusion = f32[16,1024]{1,0:T(8,128)S(1)} fusion(f32[16,1024,128]{2,1,0:T(8,128)} %w_ref.9), kind=kLoop, calls=%fused_computation | loop fusion | flops 4177920 | bytes 8454144 | tf_op jit(solution)/shard_map/reduce_sum | solution.py:273
  7.9 2.8 %collective-permute-done = f32[16,8,128]{2,1,0:T(8,128)S(1)} collective-permute-done((f32[16,8,128]{2,1,0:T(8,128)S(1)}, f32[16,8,128]{2,1,0:T(8,128)S(1)}, u32[]{:S(2)}, u32[]{:S(2)}) %collective-permute-start) | collective-permute-done | bytes 65568 | tf_op jit(solution)/shard_map/ppermute | solution.py:21
  10.7 3.1 %collective-permute-start.1 = (f32[16,8,128]{2,1,0:T(8,128)S(1)}, f32[16,8,128]{2,1,0:T(8,128)S(1)}, u32[]{:S(2)}, u32[]{:S(2)}) collective-permute-start(f32[16,8,128]{2,1,0:T(8,128)S(1)} %bitcast_add_fusion), channel_id=1, source_target_pairs={{0,2},{1,3},{2,0},{3,1},{4,6},{5,7},{6,4},{7,5},{8,10},{9,11},{10,... | collective-permute-start | bytes 196616 | tf_op jit(solution)/shard_map/ppermute | solution.py:21
  13.8 2.7 %collective-permute-done.1 = f32[16,8,128]{2,1,0:T(8,128)S(1)} collective-permute-done((f32[16,8,128]{2,1,0:T(8,128)S(1)}, f32[16,8,128]{2,1,0:T(8,128)S(1)}, u32[]{:S(2)}, u32[]{:S(2)}) %collective-permute-start.1) | collective-permute-done | bytes 65568 | tf_op jit(solution)/shard_map/ppermute | solution.py:21
  16.5 3.3 %collective-permute-start.2 = (f32[16,8,128]{2,1,0:T(8,128)S(1)}, f32[16,8,128]{2,1,0:T(8,128)S(1)}, u32[]{:S(2)}, u32[]{:S(2)}) collective-permute-start(f32[16,8,128]{2,1,0:T(8,128)S(1)} %add.16), channel_id=1, source_target_pairs={{0,4},{1,5},{2,6},{3,7},{4,0},{5,1},{6,2},{7,3},{8,12},{9,13},{10,... | collective-permute-start | bytes 196616 | tf_op jit(solution)/shard_map/ppermute | solution.py:21
  19.8 2.6 %collective-permute-done.2 = f32[16,8,128]{2,1,0:T(8,128)S(1)} collective-permute-done((f32[16,8,128]{2,1,0:T(8,128)S(1)}, f32[16,8,128]{2,1,0:T(8,128)S(1)}, u32[]{:S(2)}, u32[]{:S(2)}) %collective-permute-start.2) | collective-permute-done | bytes 65568 | tf_op jit(solution)/shard_map/ppermute | solution.py:21
  22.4 4.6 %collective-permute-start.3 = (f32[16,8,128]{2,1,0:T(8,128)S(1)}, f32[16,8,128]{2,1,0:T(8,128)S(1)}, u32[]{:S(2)}, u32[]{:S(2)}) collective-permute-start(f32[16,8,128]{2,1,0:T(8,128)S(1)} %add.17), channel_id=1, source_target_pairs={{0,8},{1,9},{2,10},{3,11},{4,12},{5,13},{6,14},{7,15},{8,0},{9,1},... | collective-permute-start | bytes 196616 | tf_op jit(solution)/shard_map/ppermute | solution.py:21
  27.6 5.1 %all-to-all-start = ((bf16[4,16,128]{2,1,0:T(8,128)(2,1)}), bf16[4,16,128]{2,1,0:T(8,128)(2,1)S(1)}, u32[]{:S(2)}, u32[]{:S(2)}) async-start(bf16[4,16,128]{2,1,0:T(8,128)(2,1)} %broadcast_in_dim.2), calls=%async_computation | async-start | bytes 32768 | tf_op jit(solution)/shard_map/all_to_all | solution.py:278
  32.7 1.9 %spread_raw.1 = (f32[8,1,64,128]{3,2,1,0:T(8,128)}, f32[8,1,64,128]{3,2,1,0:T(8,128)}) custom-call(s32[1]{0:T(128)} %bitcast.me_ref, f32[16,1024,128]{2,1,0:T(8,128)} %w_ref.9), custom_call_target="tpu_custom_call" | custom-call | flops 2000000 | bytes 1048576 | tf_op jit(solution)/shard_map/spread_raw/pallas_call | solution.py:152
  36.0 4.5 %collective-permute-start.16 = (f32[8,1,64,128]{3,2,1,0:T(8,128)}, f32[8,1,64,128]{3,2,1,0:T(8,128)}, u32[]{:S(2)}, u32[]{:S(2)}) collective-permute-start(f32[8,1,64,128]{3,2,1,0:T(8,128)} %get-tuple-element.20), channel_id=1, source_target_pairs={{0,8},{1,9},{2,10},{3,11},{4,12},{5,13},{6,14},{7,15},{8,0},{9,1},... | collective-permute-start | bytes 786440 | tf_op jit(solution)/shard_map/ppermute | solution.py:21
  42.6 4.3 %spread.5 = (bf16[2,10,64,128]{3,2,1,0:T(8,128)(2,1)}, bf16[2,10,64,128]{3,2,1,0:T(8,128)(2,1)}, bf16[2,10,64,128]{3,2,1,0:T(8,128)(2,1)}, bf16[2,10,64,128]{3,2,1,0:T(8,128)(2,1)}) custom-call(s32[1]{0:T(128)} %bitcast.me_ref, f32[16,1024,128]{2,1,0:T(8,128)} %w_ref.9, f32[16,8,128]{2,1,0:T(8,128)} %add.18.refs_0_.s_ref), custom_call_target="tpu_custom_call" | custom-call | flops 10000000 | bytes 3932160 | tf_op jit(solution)/shard_map/spread/pallas_call | solution.py:78
  46.9 3.8 %spread.4 = bf16[8,7,64,128]{3,2,1,0:T(8,128)(2,1)} custom-call(s32[1]{0:T(128)} %bitcast.me_ref, f32[16,1024,128]{2,1,0:T(8,128)} %w_ref.9, f32[16,8,128]{2,1,0:T(8,128)} %add.18.refs_0_.s_ref), custom_call_target="tpu_custom_call" | custom-call | flops 7000000 | bytes 2752512 | tf_op jit(solution)/shard_map/spread/pallas_call | solution.py:78
  50.7 3.8 %spread.3 = (bf16[2,7,64,128]{3,2,1,0:T(8,128)(2,1)}, bf16[2,7,64,128]{3,2,1,0:T(8,128)(2,1)}, bf16[2,7,64,128]{3,2,1,0:T(8,128)(2,1)}, bf16[2,7,64,128]{3,2,1,0:T(8,128)(2,1)}) custom-call(s32[1]{0:T(128)} %bitcast.me_ref, f32[16,1024,128]{2,1,0:T(8,128)} %w_ref.9, f32[16,8,128]{2,1,0:T(8,128)} %add.18.refs_0_.s_ref), custom_call_target="tpu_custom_call" | custom-call | flops 7000000 | bytes 2752512 | tf_op jit(solution)/shard_map/spread/pallas_call | solution.py:78
  57.6 8.4 %collective-permute-done.4 = bf16[2,7,64,128]{3,2,1,0:T(8,128)(2,1)S(1)} collective-permute-done((bf16[2,7,64,128]{3,2,1,0:T(8,128)(2,1)}, bf16[2,7,64,128]{3,2,1,0:T(8,128)(2,1)S(1)}, u32[]{:S(2)}, u32[]{:S(2)}) %collective-permute-start.4) | collective-permute-done | bytes 229408 | tf_op jit(solution)/shard_map/ppermute | solution.py:21
  66.0 3.8 %collective-permute-start.5 = (bf16[2,7,64,128]{3,2,1,0:T(8,128)(2,1)}, bf16[2,7,64,128]{3,2,1,0:T(8,128)(2,1)S(1)}, u32[]{:S(2)}, u32[]{:S(2)}) collective-permute-start(bf16[2,7,64,128]{3,2,1,0:T(8,128)(2,1)} %get-tuple-element.17), channel_id=1, source_target_pairs={{0,2},{1,3},{2,0},{3,1},{4,6},{5,7},{6,4},{7,5},{8,10},{9,11},{10,... | collective-permute-start | bytes 688136 | tf_op jit(solution)/shard_map/ppermute | solution.py:21
  69.8 4.3 %collective-permute-done.5 = bf16[2,7,64,128]{3,2,1,0:T(8,128)(2,1)S(1)} collective-permute-done((bf16[2,7,64,128]{3,2,1,0:T(8,128)(2,1)}, bf16[2,7,64,128]{3,2,1,0:T(8,128)(2,1)S(1)}, u32[]{:S(2)}, u32[]{:S(2)}) %collective-permute-start.5) | collective-permute-done | bytes 229408 | tf_op jit(solution)/shard_map/ppermute | solution.py:21
  74.1 3.3 %collective-permute-start.6 = (bf16[2,7,64,128]{3,2,1,0:T(8,128)(2,1)}, bf16[2,7,64,128]{3,2,1,0:T(8,128)(2,1)S(1)}, u32[]{:S(2)}, u32[]{:S(2)}) collective-permute-start(bf16[2,7,64,128]{3,2,1,0:T(8,128)(2,1)} %get-tuple-element.18), channel_id=1, source_target_pairs={{0,3},{1,2},{2,1},{3,0},{4,7},{5,6},{6,5},{7,4},{8,11},{9,10},{10,... | collective-permute-start | bytes 688136 | tf_op jit(solution)/shard_map/ppermute | solution.py:21
  77.4 4.2 %collective-permute-done.6 = bf16[2,7,64,128]{3,2,1,0:T(8,128)(2,1)S(1)} collective-permute-done((bf16[2,7,64,128]{3,2,1,0:T(8,128)(2,1)}, bf16[2,7,64,128]{3,2,1,0:T(8,128)(2,1)S(1)}, u32[]{:S(2)}, u32[]{:S(2)}) %collective-permute-start.6) | collective-permute-done | bytes 229408 | tf_op jit(solution)/shard_map/ppermute | solution.py:21
  81.6 4.5 %collective-permute-start.9 = (bf16[8,7,64,128]{3,2,1,0:T(8,128)(2,1)S(1)}, bf16[8,7,64,128]{3,2,1,0:T(8,128)(2,1)S(1)}, u32[]{:S(2)}, u32[]{:S(2)}) collective-permute-start(bf16[8,7,64,128]{3,2,1,0:T(8,128)(2,1)S(1)} %copy-done.5), channel_id=1, source_target_pairs={{0,8},{1,9},{2,10},{3,11},{4,12},{5,13},{6,14},{7,15},{8,0},{9,1},... | collective-permute-start | bytes 2752520 | tf_op jit(solution)/shard_map/ppermute | solution.py:21
  88.0 3.2 %collective-permute-start.7 = (bf16[4,7,64,128]{3,2,1,0:T(8,128)(2,1)}, bf16[4,7,64,128]{3,2,1,0:T(8,128)(2,1)}, u32[]{:S(2)}, u32[]{:S(2)}) collective-permute-start(bf16[4,7,64,128]{3,2,1,0:T(8,128)(2,1)} %pad_maximum_fusion.1), channel_id=1, source_target_pairs={{0,4},{1,5},{2,6},{3,7},{4,0},{5,1},{6,2},{7,3},{8,12},{9,13},{10,... | collective-permute-start | bytes 1376264 | tf_op jit(solution)/shard_map/ppermute | solution.py:21
  91.9 2.2 %collective-permute-start.22 = (bf16[2,10,64,128]{3,2,1,0:T(8,128)(2,1)}, bf16[2,10,64,128]{3,2,1,0:T(8,128)(2,1)S(1)}, u32[]{:S(2)}, u32[]{:S(2)}) collective-permute-start(bf16[2,10,64,128]{3,2,1,0:T(8,128)(2,1)} %get-tuple-element.25), channel_id=1, source_target_pairs={{0,2},{1,3},{2,0},{3,1},{4,6},{5,7},{6,4},{7,5},{8,10},{9,11},{10,... | collective-permute-start | bytes 983048 | tf_op jit(solution)/shard_map/ppermute | solution.py:21
  96.5 3.8 %spread_own.1 = (bf16[4,10,64,128]{3,2,1,0:T(8,128)(2,1)}, bf16[4,10,64,128]{3,2,1,0:T(8,128)(2,1)}) custom-call(s32[1]{0:T(128)} %bitcast.me_ref, f32[16,1024,128]{2,1,0:T(8,128)} %w_ref.9, f32[16,8,128]{2,1,0:T(8,128)} %add.18.refs_0_.s_ref, bf16[64,128]{1,0:T(8,128)(2,1)} %bitcast.15, bf16[64,128]{1,0:T(8,128)(2,1)} %copy-done.15, ...), custom_call_target="tpu_custom_call" | custom-call | flops 10000000 | bytes 3932160 | tf_op jit(solution)/shard_map/spread_own/pallas_call | solution.py:122
  102.0 2.3 %collective-permute-done.23.refs_3_ = bf16[2,10,64,128]{3,2,1,0:T(8,128)(2,1)} collective-permute-done((bf16[2,10,64,128]{3,2,1,0:T(8,128)(2,1)}, bf16[2,10,64,128]{3,2,1,0:T(8,128)(2,1)}, u32[]{:S(2)}, u32[]{:S(2)}) %collective-permute-start.23) | collective-permute-done | bytes 327712 | tf_op jit(solution)/shard_map/ppermute | solution.py:21
  110.4 27.7 %collective-permute-done.9 = bf16[8,7,64,128]{3,2,1,0:T(8,128)(2,1)S(1)} collective-permute-done((bf16[8,7,64,128]{3,2,1,0:T(8,128)(2,1)S(1)}, bf16[8,7,64,128]{3,2,1,0:T(8,128)(2,1)S(1)}, u32[]{:S(2)}, u32[]{:S(2)}) %collective-permute-start.9) | collective-permute-done | bytes 917536 | tf_op jit(solution)/shard_map/ppermute | solution.py:21
  139.1 7.1 %collective-permute-start.11 = (bf16[2,7,64,128]{3,2,1,0:T(8,128)(2,1)S(1)}, bf16[2,7,64,128]{3,2,1,0:T(8,128)(2,1)S(1)}, u32[]{:S(2)}, u32[]{:S(2)}) collective-permute-start(bf16[2,7,64,128]{3,2,1,0:T(8,128)(2,1)S(1)} %get-tuple-element.28), channel_id=1, source_target_pairs={{0,2},{1,3},{2,0},{3,1},{4,6},{5,7},{6,4},{7,5},{8,10},{9,11},{10,... | collective-permute-start | bytes 688136 | tf_op jit(solution)/shard_map/ppermute | solution.py:21
  146.5 6.1 %collective-permute-done.11.refs_2_ = bf16[2,7,64,128]{3,2,1,0:T(8,128)(2,1)S(1)} collective-permute-done((bf16[2,7,64,128]{3,2,1,0:T(8,128)(2,1)S(1)}, bf16[2,7,64,128]{3,2,1,0:T(8,128)(2,1)S(1)}, u32[]{:S(2)}, u32[]{:S(2)}) %collective-permute-start.11) | collective-permute-done | bytes 229408 | tf_op jit(solution)/shard_map/ppermute | solution.py:21
  155.1 3.3 %collective-permute-start.13 = (bf16[4,7,64,128]{3,2,1,0:T(8,128)(2,1)S(1)}, bf16[4,7,64,128]{3,2,1,0:T(8,128)(2,1)}, u32[]{:S(2)}, u32[]{:S(2)}) collective-permute-start(bf16[4,7,64,128]{3,2,1,0:T(8,128)(2,1)S(1)} %pad_maximum_fusion.2), channel_id=1, source_target_pairs={{0,4},{1,5},{2,6},{3,7},{4,0},{5,1},{6,2},{7,3},{8,12},{9,13},{10,... | collective-permute-start | bytes 1376264 | tf_op jit(solution)/shard_map/ppermute | solution.py:21
  161.3 5.6 %collective-permute-done.20.refs_4_ = bf16[2,10,64,128]{3,2,1,0:T(8,128)(2,1)S(1)} collective-permute-done((bf16[2,10,64,128]{3,2,1,0:T(8,128)(2,1)S(1)}, bf16[2,10,64,128]{3,2,1,0:T(8,128)(2,1)S(1)}, u32[]{:S(2)}, u32[]{:S(2)}) %collective-permute-start.20) | collective-permute-done | bytes 327712 | tf_op jit(solution)/shard_map/ppermute | solution.py:21
  169.3 2.2 %join.5.refs_5_ = bf16[16,64,2048]{2,1,0:T(8,128)(2,1)} custom-call(s32[1]{0:T(128)} %bitcast.me_ref, bf16[4,10,64,128]{3,2,1,0:T(8,128)(2,1)} %get-tuple-element.21.refs_0_, bf16[4,10,64,128]{3,2,1,0:T(8,128)(2,1)} %copy-done, bf16[2,10,64,128]{3,2,1,0:T(8,128)(2,1)} %copy-done.1, bf16[2,10,64,128]{3,2,1,0:T(8,128)(2,1)} %copy-done.2, ...), custom_call_target="tpu_custom_call" | custom-call | flops 6000000 | bytes 1572864 | tf_op jit(solution)/shard_map/join/pallas_call | solution.py:197
  171.5 2.3 %join.6.refs_5_ = bf16[16,64,2048]{2,1,0:T(8,128)(2,1)} custom-call(s32[1]{0:T(128)} %bitcast.me_ref, bf16[2,10,64,128]{3,2,1,0:T(8,128)(2,1)} %get-tuple-element.23.refs_0_, bf16[2,10,64,128]{3,2,1,0:T(8,128)(2,1)} %copy-done.7, bf16[2,10,64,128]{3,2,1,0:T(8,128)(2,1)} %copy-done.8, ...), custom_call_target="tpu_custom_call", output_to_operand_aliasing={{}: (6, {})} | custom-call | flops 10000000 | bytes 2621440 | tf_op jit(solution)/shard_map/join/pallas_call | solution.py:197
  175.6 2.3 %join.8.refs_1_ = bf16[16,64,2048]{2,1,0:T(8,128)(2,1)} custom-call(s32[1]{0:T(128)} %bitcast.me_ref, bf16[2,7,64,128]{3,2,1,0:T(8,128)(2,1)} %get-tuple-element.30.refs_0_, bf16[2,7,64,128]{3,2,1,0:T(8,128)(2,1)} %copy-done.10, bf16[2,7,64,128]{3,2,1,0:T(8,128)(2,1)} %copy-done.11, ...), custom_call_target="tpu_custom_call", output_to_operand_aliasing={{}: (6, {})} | custom-call | flops 7000000 | bytes 1835008 | tf_op jit(solution)/shard_map/join/pallas_call | solution.py:197
  177.9 2.3 %join.9 = bf16[16,64,2048]{2,1,0:T(8,128)(2,1)} custom-call(s32[1]{0:T(128)} %bitcast.me_ref, bf16[8,7,64,128]{3,2,1,0:T(8,128)(2,1)} %collective-permute-done.8.refs_0_, bf16[16,64,2048]{2,1,0:T(8,128)(2,1)} %join.8.refs_1_), custom_call_target="tpu_custom_call", output_to_operand_aliasing={{}: (2, {})} | custom-call | flops 7000000 | bytes 1835008 | tf_op jit(solution)/shard_map/join/pallas_call | solution.py:197
  (102 shorter events, 32.1 us)
Async XLA Ops:
  6.3 4.4 %collective-permute-start = (f32[16,8,128]{2,1,0:T(8,128)S(1)}, f32[16,8,128]{2,1,0:T(8,128)S(1)}, u32[]{:S(2)}, u32[]{:S(2)}) collective-permute-start(f32[16,8,128]{2,1,0:T(8,128)S(1)} %bitcast.12), channel_id=1, source_target_pairs={{0,1},{1,0},{2,3},{3,2},{4,5},{5,4},{6,7},{7,6},{8,9},{9,8},{10,11... | collective-permute-start | bytes 196616 | tf_op jit(solution)/shard_map/ppermute | solution.py:21
  10.7 5.9 %collective-permute-start.1 = (f32[16,8,128]{2,1,0:T(8,128)S(1)}, f32[16,8,128]{2,1,0:T(8,128)S(1)}, u32[]{:S(2)}, u32[]{:S(2)}) collective-permute-start(f32[16,8,128]{2,1,0:T(8,128)S(1)} %bitcast_add_fusion), channel_id=1, source_target_pairs={{0,2},{1,3},{2,0},{3,1},{4,6},{5,7},{6,4},{7,5},{8,10},{9,11},{10,... | collective-permute-start | bytes 196616 | tf_op jit(solution)/shard_map/ppermute | solution.py:21
  16.5 5.9 %collective-permute-start.2 = (f32[16,8,128]{2,1,0:T(8,128)S(1)}, f32[16,8,128]{2,1,0:T(8,128)S(1)}, u32[]{:S(2)}, u32[]{:S(2)}) collective-permute-start(f32[16,8,128]{2,1,0:T(8,128)S(1)} %add.16), channel_id=1, source_target_pairs={{0,4},{1,5},{2,6},{3,7},{4,0},{5,1},{6,2},{7,3},{8,12},{9,13},{10,... | collective-permute-start | bytes 196616 | tf_op jit(solution)/shard_map/ppermute | solution.py:21
  22.4 19.5 %collective-permute-start.3 = (f32[16,8,128]{2,1,0:T(8,128)S(1)}, f32[16,8,128]{2,1,0:T(8,128)S(1)}, u32[]{:S(2)}, u32[]{:S(2)}) collective-permute-start(f32[16,8,128]{2,1,0:T(8,128)S(1)} %add.17), channel_id=1, source_target_pairs={{0,8},{1,9},{2,10},{3,11},{4,12},{5,13},{6,14},{7,15},{8,0},{9,1},... | collective-permute-start | bytes 196616 | tf_op jit(solution)/shard_map/ppermute | solution.py:21
  27.6 12.9 %all-to-all-start = ((bf16[4,16,128]{2,1,0:T(8,128)(2,1)}), bf16[4,16,128]{2,1,0:T(8,128)(2,1)S(1)}, u32[]{:S(2)}, u32[]{:S(2)}) async-start(bf16[4,16,128]{2,1,0:T(8,128)(2,1)} %broadcast_in_dim.2), calls=%async_computation | async-start | bytes 32768 | tf_op jit(solution)/shard_map/all_to_all | solution.py:278
  34.6 56.6 %collective-permute-start.15 = (f32[8,1,64,128]{3,2,1,0:T(8,128)}, f32[8,1,64,128]{3,2,1,0:T(8,128)S(1)}, u32[]{:S(2)}, u32[]{:S(2)}) collective-permute-start(f32[8,1,64,128]{3,2,1,0:T(8,128)} %get-tuple-element.19), channel_id=1, source_target_pairs={{0,8},{1,9},{2,10},{3,11},{4,12},{5,13},{6,14},{7,15},{8,0},{9,1},... | collective-permute-start | bytes 786440 | tf_op jit(solution)/shard_map/ppermute | solution.py:21
  36.0 58.1 %collective-permute-start.16 = (f32[8,1,64,128]{3,2,1,0:T(8,128)}, f32[8,1,64,128]{3,2,1,0:T(8,128)}, u32[]{:S(2)}, u32[]{:S(2)}) collective-permute-start(f32[8,1,64,128]{3,2,1,0:T(8,128)} %get-tuple-element.20), channel_id=1, source_target_pairs={{0,8},{1,9},{2,10},{3,11},{4,12},{5,13},{6,14},{7,15},{8,0},{9,1},... | collective-permute-start | bytes 786440 | tf_op jit(solution)/shard_map/ppermute | solution.py:21
  40.5 47.4 %collective-permute-start.14 = (bf16[64,128]{1,0:T(8,128)(2,1)S(1)}, bf16[64,128]{1,0:T(8,128)(2,1)S(1)}, u32[]{:S(2)}, u32[]{:S(2)}) collective-permute-start(bf16[64,128]{1,0:T(8,128)(2,1)S(1)} %bitcast.14), channel_id=1, source_target_pairs={{0,8},{1,9},{2,10},{3,11},{4,12},{5,13},{6,14},{7,15},{8,0},{9,1},... | collective-permute-start | bytes 49160 | tf_op jit(solution)/shard_map/ppermute | solution.py:21
  50.7 30.9 %copy-start.5 = (bf16[8,7,64,128]{3,2,1,0:T(8,128)(2,1)S(1)}, bf16[8,7,64,128]{3,2,1,0:T(8,128)(2,1)}, u32[]{:S(2)}) copy-start(bf16[8,7,64,128]{3,2,1,0:T(8,128)(2,1)} %spread.4) | copy-start | bytes 2752516
  50.7 44.4 %copy-start.4 = (f32[16,8,128]{2,1,0:T(8,128)S(1)}, f32[16,8,128]{2,1,0:T(8,128)}, u32[]{:S(2)}) copy-start(f32[16,8,128]{2,1,0:T(8,128)} %add.18.refs_0_.s_ref) | copy-start | bytes 196612
  50.7 45.1 %copy-start.6 = (bf16[2,10,64,128]{3,2,1,0:T(8,128)(2,1)S(1)}, bf16[2,10,64,128]{3,2,1,0:T(8,128)(2,1)}, u32[]{:S(2)}) copy-start(bf16[2,10,64,128]{3,2,1,0:T(8,128)(2,1)} %get-tuple-element.23.refs_0_) | copy-start | bytes 983044
  54.6 45.8 %collective-permute-start.21 = (bf16[2,10,64,128]{3,2,1,0:T(8,128)(2,1)}, bf16[2,10,64,128]{3,2,1,0:T(8,128)(2,1)S(1)}, u32[]{:S(2)}, u32[]{:S(2)}) collective-permute-start(bf16[2,10,64,128]{3,2,1,0:T(8,128)(2,1)} %get-tuple-element.24), channel_id=1, source_target_pairs={{0,1},{1,0},{2,3},{3,2},{4,5},{5,4},{6,7},{7,6},{8,9},{9,8},{10,11... | collective-permute-start | bytes 983048 | tf_op jit(solution)/shard_map/ppermute | solution.py:21
  56.1 9.9 %collective-permute-start.4 = (bf16[2,7,64,128]{3,2,1,0:T(8,128)(2,1)}, bf16[2,7,64,128]{3,2,1,0:T(8,128)(2,1)S(1)}, u32[]{:S(2)}, u32[]{:S(2)}) collective-permute-start(bf16[2,7,64,128]{3,2,1,0:T(8,128)(2,1)} %get-tuple-element.16), channel_id=1, source_target_pairs={{0,1},{1,0},{2,3},{3,2},{4,5},{5,4},{6,7},{7,6},{8,9},{9,8},{10,11... | collective-permute-start | bytes 688136 | tf_op jit(solution)/shard_map/ppermute | solution.py:21
  66.0 8.1 %collective-permute-start.5 = (bf16[2,7,64,128]{3,2,1,0:T(8,128)(2,1)}, bf16[2,7,64,128]{3,2,1,0:T(8,128)(2,1)S(1)}, u32[]{:S(2)}, u32[]{:S(2)}) collective-permute-start(bf16[2,7,64,128]{3,2,1,0:T(8,128)(2,1)} %get-tuple-element.17), channel_id=1, source_target_pairs={{0,2},{1,3},{2,0},{3,1},{4,6},{5,7},{6,4},{7,5},{8,10},{9,11},{10,... | collective-permute-start | bytes 688136 | tf_op jit(solution)/shard_map/ppermute | solution.py:21
  74.1 7.5 %collective-permute-start.6 = (bf16[2,7,64,128]{3,2,1,0:T(8,128)(2,1)}, bf16[2,7,64,128]{3,2,1,0:T(8,128)(2,1)S(1)}, u32[]{:S(2)}, u32[]{:S(2)}) collective-permute-start(bf16[2,7,64,128]{3,2,1,0:T(8,128)(2,1)} %get-tuple-element.18), channel_id=1, source_target_pairs={{0,3},{1,2},{2,1},{3,0},{4,7},{5,6},{6,5},{7,4},{8,11},{9,10},{10,... | collective-permute-start | bytes 688136 | tf_op jit(solution)/shard_map/ppermute | solution.py:21
  81.6 56.6 %collective-permute-start.9 = (bf16[8,7,64,128]{3,2,1,0:T(8,128)(2,1)S(1)}, bf16[8,7,64,128]{3,2,1,0:T(8,128)(2,1)S(1)}, u32[]{:S(2)}, u32[]{:S(2)}) collective-permute-start(bf16[8,7,64,128]{3,2,1,0:T(8,128)(2,1)S(1)} %copy-done.5), channel_id=1, source_target_pairs={{0,8},{1,9},{2,10},{3,11},{4,12},{5,13},{6,14},{7,15},{8,0},{9,1},... | collective-permute-start | bytes 2752520 | tf_op jit(solution)/shard_map/ppermute | solution.py:21
  88.0 19.2 %collective-permute-start.7 = (bf16[4,7,64,128]{3,2,1,0:T(8,128)(2,1)}, bf16[4,7,64,128]{3,2,1,0:T(8,128)(2,1)}, u32[]{:S(2)}, u32[]{:S(2)}) collective-permute-start(bf16[4,7,64,128]{3,2,1,0:T(8,128)(2,1)} %pad_maximum_fusion.1), channel_id=1, source_target_pairs={{0,4},{1,5},{2,6},{3,7},{4,0},{5,1},{6,2},{7,3},{8,12},{9,13},{10,... | collective-permute-start | bytes 1376264 | tf_op jit(solution)/shard_map/ppermute | solution.py:21
  91.9 10.1 %collective-permute-start.22 = (bf16[2,10,64,128]{3,2,1,0:T(8,128)(2,1)}, bf16[2,10,64,128]{3,2,1,0:T(8,128)(2,1)S(1)}, u32[]{:S(2)}, u32[]{:S(2)}) collective-permute-start(bf16[2,10,64,128]{3,2,1,0:T(8,128)(2,1)} %get-tuple-element.25), channel_id=1, source_target_pairs={{0,2},{1,3},{2,0},{3,1},{4,6},{5,7},{6,4},{7,5},{8,10},{9,11},{10,... | collective-permute-start | bytes 983048 | tf_op jit(solution)/shard_map/ppermute | solution.py:21
  94.1 10.2 %collective-permute-start.23 = (bf16[2,10,64,128]{3,2,1,0:T(8,128)(2,1)}, bf16[2,10,64,128]{3,2,1,0:T(8,128)(2,1)}, u32[]{:S(2)}, u32[]{:S(2)}) collective-permute-start(bf16[2,10,64,128]{3,2,1,0:T(8,128)(2,1)} %get-tuple-element.26), channel_id=1, source_target_pairs={{0,3},{1,2},{2,1},{3,0},{4,7},{5,6},{6,5},{7,4},{8,11},{9,10},{10,... | collective-permute-start | bytes 983048 | tf_op jit(solution)/shard_map/ppermute | solution.py:21
  100.4 46.1 %copy-start.7 = (bf16[2,10,64,128]{3,2,1,0:T(8,128)(2,1)}, bf16[2,10,64,128]{3,2,1,0:T(8,128)(2,1)S(1)}, u32[]{:S(2)}) copy-start(bf16[2,10,64,128]{3,2,1,0:T(8,128)(2,1)S(1)} %collective-permute-done.21.refs_1_) | copy-start | bytes 983044
  100.4 38.7 %collective-permute-start.17 = (bf16[4,10,64,128]{3,2,1,0:T(8,128)(2,1)}, bf16[4,10,64,128]{3,2,1,0:T(8,128)(2,1)S(1)}, u32[]{:S(2)}, u32[]{:S(2)}) collective-permute-start(bf16[4,10,64,128]{3,2,1,0:T(8,128)(2,1)} %get-tuple-element.22), channel_id=1, source_target_pairs={{0,4},{1,5},{2,6},{3,7},{4,0},{5,1},{6,2},{7,3},{8,12},{9,13},{10,... | collective-permute-start | bytes 1966088 | tf_op jit(solution)/shard_map/ppermute | solution.py:21
  101.9 44.3 %copy-start.8 = (bf16[2,10,64,128]{3,2,1,0:T(8,128)(2,1)}, bf16[2,10,64,128]{3,2,1,0:T(8,128)(2,1)S(1)}, u32[]{:S(2)}) copy-start(bf16[2,10,64,128]{3,2,1,0:T(8,128)(2,1)S(1)} %collective-permute-done.22.refs_2_) | copy-start | bytes 983044
  106.1 65.4 %collective-permute-start.24 = (bf16[4,10,64,128]{3,2,1,0:T(8,128)(2,1)}, bf16[4,10,64,128]{3,2,1,0:T(8,128)(2,1)}, u32[]{:S(2)}, u32[]{:S(2)}) collective-permute-start(bf16[4,10,64,128]{3,2,1,0:T(8,128)(2,1)} %pad_maximum_fusion), channel_id=1, source_target_pairs={{0,4},{1,5},{2,6},{3,7},{4,0},{5,1},{6,2},{7,3},{8,12},{9,13},{10,... | collective-permute-start | bytes 1966088 | tf_op jit(solution)/shard_map/ppermute | solution.py:21
  109.0 68.9 %collective-permute-start.8 = (bf16[8,7,64,128]{3,2,1,0:T(8,128)(2,1)}, bf16[8,7,64,128]{3,2,1,0:T(8,128)(2,1)}, u32[]{:S(2)}, u32[]{:S(2)}) collective-permute-start(bf16[8,7,64,128]{3,2,1,0:T(8,128)(2,1)} %constant_dynamic-update-slice_fusion), channel_id=1, source_target_pairs={{0,8},{1,9},{2,10},{3,11},{4,12},{5,13},{6,14},{7,15},{8,0},{9,1},... | collective-permute-start | bytes 2752520 | tf_op jit(solution)/shard_map/ppermute | solution.py:21
  138.9 7.4 %collective-permute-start.10 = (bf16[2,7,64,128]{3,2,1,0:T(8,128)(2,1)S(1)}, bf16[2,7,64,128]{3,2,1,0:T(8,128)(2,1)S(1)}, u32[]{:S(2)}, u32[]{:S(2)}) collective-permute-start(bf16[2,7,64,128]{3,2,1,0:T(8,128)(2,1)S(1)} %get-tuple-element.29), channel_id=1, source_target_pairs={{0,1},{1,0},{2,3},{3,2},{4,5},{5,4},{6,7},{7,6},{8,9},{9,8},{10,11... | collective-permute-start | bytes 688136 | tf_op jit(solution)/shard_map/ppermute | solution.py:21
  139.1 27.8 %copy-start = (bf16[4,10,64,128]{3,2,1,0:T(8,128)(2,1)}, bf16[4,10,64,128]{3,2,1,0:T(8,128)(2,1)S(1)}, u32[]{:S(2)}) copy-start(bf16[4,10,64,128]{3,2,1,0:T(8,128)(2,1)S(1)} %collective-permute-done.17.refs_1_) | copy-start | bytes 1966084
  139.1 13.6 %collective-permute-start.11 = (bf16[2,7,64,128]{3,2,1,0:T(8,128)(2,1)S(1)}, bf16[2,7,64,128]{3,2,1,0:T(8,128)(2,1)S(1)}, u32[]{:S(2)}, u32[]{:S(2)}) collective-permute-start(bf16[2,7,64,128]{3,2,1,0:T(8,128)(2,1)S(1)} %get-tuple-element.28), channel_id=1, source_target_pairs={{0,2},{1,3},{2,0},{3,1},{4,6},{5,7},{6,4},{7,5},{8,10},{9,11},{10,... | collective-permute-start | bytes 688136 | tf_op jit(solution)/shard_map/ppermute | solution.py:21
  146.2 8.8 %collective-permute-start.12 = (bf16[2,7,64,128]{3,2,1,0:T(8,128)(2,1)S(1)}, bf16[2,7,64,128]{3,2,1,0:T(8,128)(2,1)S(1)}, u32[]{:S(2)}, u32[]{:S(2)}) collective-permute-start(bf16[2,7,64,128]{3,2,1,0:T(8,128)(2,1)S(1)} %get-tuple-element.27), channel_id=1, source_target_pairs={{0,3},{1,2},{2,1},{3,0},{4,7},{5,6},{6,5},{7,4},{8,11},{9,10},{10,... | collective-permute-start | bytes 688136 | tf_op jit(solution)/shard_map/ppermute | solution.py:21
  146.3 12.1 %collective-permute-start.18 = (bf16[2,10,64,128]{3,2,1,0:T(8,128)(2,1)S(1)}, bf16[2,10,64,128]{3,2,1,0:T(8,128)(2,1)S(1)}, u32[]{:S(2)}, u32[]{:S(2)}) collective-permute-start(bf16[2,10,64,128]{3,2,1,0:T(8,128)(2,1)S(1)} %pad_maximum_fusion.3), channel_id=1, source_target_pairs={{0,1},{1,0},{2,3},{3,2},{4,5},{5,4},{6,7},{7,6},{8,9},{9,8},{10,11... | collective-permute-start | bytes 983048 | tf_op jit(solution)/shard_map/ppermute | solution.py:21
  152.7 8.6 %collective-permute-start.19 = (bf16[2,10,64,128]{3,2,1,0:T(8,128)(2,1)S(1)}, bf16[2,10,64,128]{3,2,1,0:T(8,128)(2,1)S(1)}, u32[]{:S(2)}, u32[]{:S(2)}) collective-permute-start(bf16[2,10,64,128]{3,2,1,0:T(8,128)(2,1)S(1)} %pad_maximum_fusion.4), channel_id=1, source_target_pairs={{0,2},{1,3},{2,0},{3,1},{4,6},{5,7},{6,4},{7,5},{8,10},{9,11},{10,... | collective-permute-start | bytes 983048 | tf_op jit(solution)/shard_map/ppermute | solution.py:21
  155.1 20.5 %collective-permute-start.13 = (bf16[4,7,64,128]{3,2,1,0:T(8,128)(2,1)S(1)}, bf16[4,7,64,128]{3,2,1,0:T(8,128)(2,1)}, u32[]{:S(2)}, u32[]{:S(2)}) collective-permute-start(bf16[4,7,64,128]{3,2,1,0:T(8,128)(2,1)S(1)} %pad_maximum_fusion.2), channel_id=1, source_target_pairs={{0,4},{1,5},{2,6},{3,7},{4,0},{5,1},{6,2},{7,3},{8,12},{9,13},{10,... | collective-permute-start | bytes 1376264 | tf_op jit(solution)/shard_map/ppermute | solution.py:21
  158.4 8.4 %collective-permute-start.20 = (bf16[2,10,64,128]{3,2,1,0:T(8,128)(2,1)S(1)}, bf16[2,10,64,128]{3,2,1,0:T(8,128)(2,1)S(1)}, u32[]{:S(2)}, u32[]{:S(2)}) collective-permute-start(bf16[2,10,64,128]{3,2,1,0:T(8,128)(2,1)S(1)} %pad_maximum_fusion.5), channel_id=1, source_target_pairs={{0,3},{1,2},{2,1},{3,0},{4,7},{5,6},{6,5},{7,4},{8,11},{9,10},{10,... | collective-permute-start | bytes 983048 | tf_op jit(solution)/shard_map/ppermute | solution.py:21
  (13 other events, 153.2 us)

commit v4 on v3

--- a/solution.py
+++ b/solution.py
@@ -14,6 +14,7 @@
 HALF = 512
 
 F, L, E = (0, 7), (7, 7), (14, 2)
+RAW = (1, 1)
 A, B = (0, 10), (10, 6)
 
 
@@ -46,10 +47,12 @@
                 h = (r & 1) * ROWS
                 block = block * inverse[h : h + ROWS, r >> 1 : (r >> 1) + 1]
             y, x = r >> 2, r & 3
-            if len(outs) == w_ref.shape[0] and not scaled:
-                outs[i][2 * x + y, 0] = block.astype(outs[i].dtype)
+            if not scaled:
+                outs[int(i >= RAW[0])][2 * x + y, i % RAW[0]] = block
             elif len(outs) == 4:
                 outs[x][y, i] = block.astype(outs[x].dtype)
+            elif len(outs) == 2:
+                outs[y][x, i] = block.astype(outs[y].dtype)
             else:
                 outs[0][2 * x + y, i] = block.astype(outs[0].dtype)
 
@@ -102,9 +105,9 @@
             at = pl.multiple_of(((m & 7) ^ r) * ROWS, ROWS)
             column = inverse[(r & 1) * ROWS : (r & 1) * ROWS + ROWS, r >> 1 : (r >> 1) + 1]
             outs[r >> 2][r & 3, i] = (w_ref[i, pl.ds(at, ROWS), :] * column).astype(jnp.bfloat16)
-            raw = i - (count - len(raws))
+            raw = i - (count - E[1])
             if raw >= 0:
-                block = raws[raw][2 * (r & 3) + (r >> 2), 0] * column
+                block = raws[int(raw >= RAW[0])][2 * (r & 3) + (r >> 2), raw % RAW[0]] * column
                 outs[r >> 2][r & 3, count + 2 + raw] = block.astype(jnp.bfloat16)
     for out in outs:
         for x in range(4):
@@ -114,7 +117,7 @@
 
 def spread_own(w, sums, router, raws, me, which):
     first, count = which
-    slots = count + 2 + len(raws)
+    slots = count + 2 + E[1]
 
     def whole(*shape):
         return pl.BlockSpec(shape, lambda e, m: (0,) * len(shape))
@@ -136,7 +139,7 @@
                 whole(ROWS, LANES),
                 whole(ROWS, LANES),
             ]
-            + [whole(8, 1, ROWS, LANES)] * len(raws),
+            + [whole(8, n, ROWS, LANES) for n in RAW],
             out_specs=[whole(4, slots, ROWS, LANES)] * 2,
         ),
         out_shape=[jax.ShapeDtypeStruct((4, slots, ROWS, LANES), jnp.bfloat16)] * 2,
@@ -160,9 +163,9 @@
                     lambda e, m: (first, ((m[0] >> 3) ^ 1) * HALF, 0),
                 )
             ],
-            out_specs=[pl.BlockSpec((8, 1, ROWS, LANES), lambda e, m: (0, 0, 0, 0))] * count,
-        ),
-        out_shape=[jax.ShapeDtypeStruct((8, 1, ROWS, LANES), jnp.float32)] * count,
+            out_specs=[pl.BlockSpec((8, n, ROWS, LANES), lambda e, m: (0, 0, 0, 0)) for n in RAW],
+        ),
+        out_shape=[jax.ShapeDtypeStruct((8, n, ROWS, LANES), jnp.float32) for n in RAW],
         name="spread_raw",
         cost_estimate=pl.CostEstimate(
             flops=count * 1_000_000, bytes_accessed=count * 524_288, transcendentals=0
@@ -182,11 +185,11 @@
 
 def join(out, pieces, me, which, other, step, slot=0):
     first, count = which
-    assert count % step == 0 and slot % step == 0
-    base = slot // step
+    assert count % step == 0
     in_specs, args, where = [], [], []
     for array, taken, rs in pieces:
-        in_specs.append(pl.BlockSpec((taken, step, ROWS, LANES), lambda e, m: (0, base + e, 0, 0)))
+        shape = tuple(pl.Element(n) for n in (taken, step, ROWS, LANES))
+        in_specs.append(pl.BlockSpec(shape, lambda e, m: (0, slot + e * step, 0, 0)))
         args.append(array)
         where.append([(i, r) for i, r in enumerate(rs)])
     alias = {}
@@ -282,27 +285,27 @@
     raws = spread_raw(w_down, me, E)
     raws = [swap(raw, 8) for raw in raws]
 
-    (oth_f,) = spread(w_down, sums, me, F, 1, 1, 7)
+    (oth_f,) = spread(w_down, sums, me, F, 1, 1, F[1])
     came_f = swap(oth_f, 8)
-    oth_l = spread(w_down, sums, me, L, 1, 4, 7)
+    oth_l = spread(w_down, sums, me, L, 1, 4, L[1])
     own_b = spread_own(w_down, sums, router, raws, me, B)
-    own_a = spread(w_down, sums, me, A, 0, 4, 5)
+    own_a = spread(w_down, sums, me, A, 0, 2, 5)
 
     plane_l = plane(oth_l)
     last = pack([(a, 0, 1) for a in plane_l[0]] + [(plane_l[1], 0, 4)])
     came_l = swap(last, 8)
     plane_b = plane_y(own_b)
-    plane_a = plane(own_a)
+    plane_a = plane_y(own_a)
     plane_f = plane(by_x(came_f))
 
     scale = lax.dynamic_slice_in_dim(sums.reshape(EXPERTS, 16, ROWS), index, 1, 1)[:, 0] / D_MODEL
 
     out = join(None, plane_b, me, B, 0, B[1])
-    out = join(out, pieces_of(*plane_a), me, A, 0, 5)
     serve_router = router_join(plane_b, me, B[1]).T
-    out = join(out, plane_b, me, E, 1, 2, B[1] + 2)
-    out = join(out, pieces_of(*plane_f), me, F, 1, 7)
-    out = join(out, [(came_l, 8, list(range(8)))], me, L, 1, 7)
+    out = join(out, plane_b, me, E, 1, E[1], B[1] + 2)
+    out = join(out, plane_a, me, A, 0, 5)
+    out = join(out, pieces_of(*plane_f), me, F, 1, F[1])
+    out = join(out, [(came_l, 8, list(range(8)))], me, L, 1, L[1])
     return (out, scale, serve_router)
 
 

time: 181 us -> 177 us (0.978)
  the two profiles are of different devices: /device:TPU:96 before, /device:TPU:34 now
where the time goes in v4:
time: 177 us; the launch traced here: 174 us
  waiting for transfers between devices  56.5 us (32%)
  starting transfers between devices  51 us (29%)
  Pallas kernels  30.1 us (17%)
  blocking collectives  18.1 us (10%)
  other arithmetic  8.75 us (5%)
  local copies, waits for them, and re-layouts  8.34 us (5%)
    ppermute x25, waiting for transfers between devices, swap(): lax.ppermute(shard, 'fsdp', [(i, i ^ k) for i in range(lax.axis_size('fsd...  56.5 us
    ppermute x25, starting transfers between devices, swap(): lax.ppermute(shard, 'fsdp', [(i, i ^ k) for i in range(lax.axis_size('fsd...  51 us
    all_to_all x1, blocking collectives, on_device(): lax.all_to_all(jnp.broadcast_to(part[None], (4, 16, LANES)), 'ep', 0, 0,...  18.1 us
    pallas_call x3, Pallas kernels, spread(): pl.pallas_call(functools.partial(spread_kernel, other, scaled), grid_spec...  11.8 us
    pallas_call x5, Pallas kernels, join(): pl.pallas_call(functools.partial(join_kernel, where), grid_spec=pltpu.Pre...  10.9 us
    reduce_sum x1, other arithmetic, on_device(): sums = jnp.sum(jnp.abs(w_down), axis=2).reshape(EXPERTS, 8, LANES)  5.61 us
    slice x12, local copies, waits for them, and re-layouts, pack(): return jnp.concatenate([array[first:end] for array, first, end in parts], 0)  3.89 us
    pallas_call x1, Pallas kernels, spread_own(): pl.pallas_call(own_kernel, grid_spec=pltpu.PrefetchScalarGridSpec(num_sca...  3.81 us
  transfers between devices with their start and end apart: 25, of which 14 were waited for; matrix products, arithmetic and copies ran while one was open for 5% of the time, Pallas kernels for 14%

profile of v4, /device:TPU:34, one launch (start us, length us, event | category | flops | bytes accessed | tf_op | source)
XLA Modules:
  0.0 173.6 jit_solution(1567703894782947341)
XLA Ops:
  0.6 5.6 %abs_reduce_fusion = f32[16,1024]{1,0:T(8,128)S(1)} fusion(f32[16,1024,128]{2,1,0:T(8,128)} %w_ref.9), kind=kLoop, calls=%fused_computation | loop fusion | flops 4177920 | bytes 8454144 | tf_op jit(solution)/shard_map/reduce_sum | solution.py:276
  6.9 3.7 %collective-permute-done = f32[16,8,128]{2,1,0:T(8,128)S(1)} collective-permute-done((f32[16,8,128]{2,1,0:T(8,128)S(1)}, f32[16,8,128]{2,1,0:T(8,128)S(1)}, u32[]{:S(2)}, u32[]{:S(2)}) %collective-permute-start) | collective-permute-done | bytes 65568 | tf_op jit(solution)/shard_map/ppermute | solution.py:22
  10.6 2.2 %collective-permute-start.1 = (f32[16,8,128]{2,1,0:T(8,128)S(1)}, f32[16,8,128]{2,1,0:T(8,128)S(1)}, u32[]{:S(2)}, u32[]{:S(2)}) collective-permute-start(f32[16,8,128]{2,1,0:T(8,128)S(1)} %bitcast_add_fusion), channel_id=1, source_target_pairs={{0,2},{1,3},{2,0},{3,1},{4,6},{5,7},{6,4},{7,5},{8,10},{9,11},{10,... | collective-permute-start | bytes 196616 | tf_op jit(solution)/shard_map/ppermute | solution.py:22
  12.9 3.6 %collective-permute-done.1 = f32[16,8,128]{2,1,0:T(8,128)S(1)} collective-permute-done((f32[16,8,128]{2,1,0:T(8,128)S(1)}, f32[16,8,128]{2,1,0:T(8,128)S(1)}, u32[]{:S(2)}, u32[]{:S(2)}) %collective-permute-start.1) | collective-permute-done | bytes 65568 | tf_op jit(solution)/shard_map/ppermute | solution.py:22
  16.5 3.3 %collective-permute-start.2 = (f32[16,8,128]{2,1,0:T(8,128)S(1)}, f32[16,8,128]{2,1,0:T(8,128)S(1)}, u32[]{:S(2)}, u32[]{:S(2)}) collective-permute-start(f32[16,8,128]{2,1,0:T(8,128)S(1)} %add.16), channel_id=1, source_target_pairs={{0,4},{1,5},{2,6},{3,7},{4,0},{5,1},{6,2},{7,3},{8,12},{9,13},{10,... | collective-permute-start | bytes 196616 | tf_op jit(solution)/shard_map/ppermute | solution.py:22
  19.8 1.9 %spread_raw.1 = (f32[8,1,64,128]{3,2,1,0:T(8,128)}, f32[8,1,64,128]{3,2,1,0:T(8,128)}) custom-call(s32[1]{0:T(128)} %bitcast.me_ref, f32[16,1024,128]{2,1,0:T(8,128)} %w_ref.9), custom_call_target="tpu_custom_call" | custom-call | flops 2000000 | bytes 1048576 | tf_op jit(solution)/shard_map/spread_raw/pallas_call | solution.py:155
  21.7 6.3 %collective-permute-start.19 = (f32[8,1,64,128]{3,2,1,0:T(8,128)}, f32[8,1,64,128]{3,2,1,0:T(8,128)S(1)}, u32[]{:S(2)}, u32[]{:S(2)}) collective-permute-start(f32[8,1,64,128]{3,2,1,0:T(8,128)} %get-tuple-element.19), channel_id=1, source_target_pairs={{0,8},{1,9},{2,10},{3,11},{4,12},{5,13},{6,14},{7,15},{8,0},{9,1},... | collective-permute-start | bytes 786440 | tf_op jit(solution)/shard_map/ppermute | solution.py:22
  28.0 6.0 %collective-permute-start.3 = (f32[16,8,128]{2,1,0:T(8,128)S(1)}, f32[16,8,128]{2,1,0:T(8,128)S(1)}, u32[]{:S(2)}, u32[]{:S(2)}) collective-permute-start(f32[16,8,128]{2,1,0:T(8,128)S(1)} %add.17), channel_id=1, source_target_pairs={{0,8},{1,9},{2,10},{3,11},{4,12},{5,13},{6,14},{7,15},{8,0},{9,1},... | collective-permute-start | bytes 196616 | tf_op jit(solution)/shard_map/ppermute | solution.py:22
  34.0 18.1 %all_to_all.5 = bf16[4,16,128]{2,1,0:T(8,128)(2,1)S(1)} all-to-all(bf16[4,16,128]{2,1,0:T(8,128)(2,1)S(1)} %broadcast_in_dim.2), channel_id=1, replica_groups=mesh['unit'=4,'ep'=4,'fsdp'=16] {'ep'}, dimensions={0} | all-to-all | bytes 32768 | tf_op jit(solution)/shard_map/all_to_all | solution.py:281
  52.7 3.8 %spread.4 = bf16[8,7,64,128]{3,2,1,0:T(8,128)(2,1)} custom-call(s32[1]{0:T(128)} %bitcast.me_ref, f32[16,1024,128]{2,1,0:T(8,128)} %w_ref.9, f32[16,8,128]{2,1,0:T(8,128)} %copy-done.4), custom_call_target="tpu_custom_call" | custom-call | flops 7000000 | bytes 2752512 | tf_op jit(solution)/shard_map/spread/pallas_call | solution.py:81
  56.5 3.7 %spread.3 = (bf16[2,7,64,128]{3,2,1,0:T(8,128)(2,1)}, bf16[2,7,64,128]{3,2,1,0:T(8,128)(2,1)}, bf16[2,7,64,128]{3,2,1,0:T(8,128)(2,1)}, bf16[2,7,64,128]{3,2,1,0:T(8,128)(2,1)}) custom-call(s32[1]{0:T(128)} %bitcast.me_ref, f32[16,1024,128]{2,1,0:T(8,128)} %w_ref.9, f32[16,8,128]{2,1,0:T(8,128)} %copy-done.4), custom_call_target="tpu_custom_call" | custom-call | flops 7000000 | bytes 2752512 | tf_op jit(solution)/shard_map/spread/pallas_call | solution.py:81
  60.2 4.3 %spread.5 = (bf16[4,10,64,128]{3,2,1,0:T(8,128)(2,1)}, bf16[4,10,64,128]{3,2,1,0:T(8,128)(2,1)}) custom-call(s32[1]{0:T(128)} %bitcast.me_ref, f32[16,1024,128]{2,1,0:T(8,128)} %w_ref.9, f32[16,8,128]{2,1,0:T(8,128)} %copy-done.4), custom_call_target="tpu_custom_call" | custom-call | flops 10000000 | bytes 3932160 | tf_op jit(solution)/shard_map/spread/pallas_call | solution.py:81
  66.0 3.8 %spread_own.1 = (bf16[4,10,64,128]{3,2,1,0:T(8,128)(2,1)}, bf16[4,10,64,128]{3,2,1,0:T(8,128)(2,1)}) custom-call(s32[1]{0:T(128)} %bitcast.me_ref, f32[16,1024,128]{2,1,0:T(8,128)} %w_ref.9, f32[16,8,128]{2,1,0:T(8,128)} %copy-done.4, bf16[64,128]{1,0:T(8,128)(2,1)} %bitcast.15, bf16[64,128]{1,0:T(8,128)(2,1)} %copy-done.15, f32[8,1,64,128]{3,2,1,0:T(8,128)} %copy-done.11, ...), custom_call_target="tpu_custom_call" | custom-call | flops 10000000 | bytes 3932160 | tf_op jit(solution)/shard_map/spread_own/pallas_call | solution.py:125
  71.3 3.3 %collective-permute-start.14 = (bf16[4,10,64,128]{3,2,1,0:T(8,128)(2,1)S(1)}, bf16[4,10,64,128]{3,2,1,0:T(8,128)(2,1)S(1)}, u32[]{:S(2)}, u32[]{:S(2)}) collective-permute-start(bf16[4,10,64,128]{3,2,1,0:T(8,128)(2,1)S(1)} %copy-done.18), channel_id=1, source_target_pairs={{0,4},{1,5},{2,6},{3,7},{4,0},{5,1},{6,2},{7,3},{8,12},{9,13},{10,... | collective-permute-start | bytes 1966088 | tf_op jit(solution)/shard_map/ppermute | solution.py:22
  74.6 6.0 %collective-permute-start.9 = (bf16[8,7,64,128]{3,2,1,0:T(8,128)(2,1)}, bf16[8,7,64,128]{3,2,1,0:T(8,128)(2,1)S(1)}, u32[]{:S(2)}, u32[]{:S(2)}) collective-permute-start(bf16[8,7,64,128]{3,2,1,0:T(8,128)(2,1)} %spread.4), channel_id=1, source_target_pairs={{0,8},{1,9},{2,10},{3,11},{4,12},{5,13},{6,14},{7,15},{8,0},{9,1},... | collective-permute-start | bytes 2752520 | tf_op jit(solution)/shard_map/ppermute | solution.py:22
  81.2 2.4 %collective-permute-start.5 = (bf16[2,7,64,128]{3,2,1,0:T(8,128)(2,1)S(1)}, bf16[2,7,64,128]{3,2,1,0:T(8,128)(2,1)S(1)}, u32[]{:S(2)}, u32[]{:S(2)}) collective-permute-start(bf16[2,7,64,128]{3,2,1,0:T(8,128)(2,1)S(1)} %copy-done.20), channel_id=1, source_target_pairs={{0,2},{1,3},{2,0},{3,1},{4,6},{5,7},{6,4},{7,5},{8,10},{9,11},{10,... | collective-permute-start | bytes 688136 | tf_op jit(solution)/shard_map/ppermute | solution.py:22
  84.3 2.4 %collective-permute-done.4 = bf16[2,7,64,128]{3,2,1,0:T(8,128)(2,1)S(1)} collective-permute-done((bf16[2,7,64,128]{3,2,1,0:T(8,128)(2,1)S(1)}, bf16[2,7,64,128]{3,2,1,0:T(8,128)(2,1)S(1)}, u32[]{:S(2)}, u32[]{:S(2)}) %collective-permute-start.4) | collective-permute-done | bytes 229408 | tf_op jit(solution)/shard_map/ppermute | solution.py:22
  90.7 2.0 %collective-permute-done.6 = bf16[2,7,64,128]{3,2,1,0:T(8,128)(2,1)S(1)} collective-permute-done((bf16[2,7,64,128]{3,2,1,0:T(8,128)(2,1)S(1)}, bf16[2,7,64,128]{3,2,1,0:T(8,128)(2,1)S(1)}, u32[]{:S(2)}, u32[]{:S(2)}) %collective-permute-start.6) | collective-permute-done | bytes 229408 | tf_op jit(solution)/shard_map/ppermute | solution.py:22
  93.9 1.8 %collective-permute-start.22 = (bf16[2,10,64,128]{3,2,1,0:T(8,128)(2,1)S(1)}, bf16[2,10,64,128]{3,2,1,0:T(8,128)(2,1)S(1)}, u32[]{:S(2)}, u32[]{:S(2)}) collective-permute-start(bf16[2,10,64,128]{3,2,1,0:T(8,128)(2,1)S(1)} %pad_maximum_fusion.5), channel_id=1, source_target_pairs={{0,1},{1,0},{2,3},{3,2},{4,5},{5,4},{6,7},{7,6},{8,9},{9,8},{10,11... | collective-permute-start | bytes 983048 | tf_op jit(solution)/shard_map/ppermute | solution.py:22
  95.7 7.5 %collective-permute-done.14.refs_1_ = bf16[4,10,64,128]{3,2,1,0:T(8,128)(2,1)S(1)} collective-permute-done((bf16[4,10,64,128]{3,2,1,0:T(8,128)(2,1)S(1)}, bf16[4,10,64,128]{3,2,1,0:T(8,128)(2,1)S(1)}, u32[]{:S(2)}, u32[]{:S(2)}) %collective-permute-start.14) | collective-permute-done | bytes 655392 | tf_op jit(solution)/shard_map/ppermute | solution.py:22
  103.2 5.0 %collective-permute-done.7 = bf16[4,7,64,128]{3,2,1,0:T(8,128)(2,1)S(1)} collective-permute-done((bf16[4,7,64,128]{3,2,1,0:T(8,128)(2,1)S(1)}, bf16[4,7,64,128]{3,2,1,0:T(8,128)(2,1)S(1)}, u32[]{:S(2)}, u32[]{:S(2)}) %collective-permute-start.7) | collective-permute-done | bytes 458784 | tf_op jit(solution)/shard_map/ppermute | solution.py:22
  109.0 5.7 %collective-permute-start.8 = (bf16[8,7,64,128]{3,2,1,0:T(8,128)(2,1)}, bf16[8,7,64,128]{3,2,1,0:T(8,128)(2,1)}, u32[]{:S(2)}, u32[]{:S(2)}) collective-permute-start(bf16[8,7,64,128]{3,2,1,0:T(8,128)(2,1)} %constant_dynamic-update-slice_fusion), channel_id=1, source_target_pairs={{0,8},{1,9},{2,10},{3,11},{4,12},{5,13},{6,14},{7,15},{8,0},{9,1},... | collective-permute-start | bytes 2752520 | tf_op jit(solution)/shard_map/ppermute | solution.py:22
  114.7 20.9 %collective-permute-done.9 = bf16[8,7,64,128]{3,2,1,0:T(8,128)(2,1)S(1)} collective-permute-done((bf16[8,7,64,128]{3,2,1,0:T(8,128)(2,1)}, bf16[8,7,64,128]{3,2,1,0:T(8,128)(2,1)S(1)}, u32[]{:S(2)}, u32[]{:S(2)}) %collective-permute-start.9) | collective-permute-done | bytes 917536 | tf_op jit(solution)/shard_map/ppermute | solution.py:22
  136.9 2.4 %collective-permute-start.11 = (bf16[2,7,64,128]{3,2,1,0:T(8,128)(2,1)S(1)}, bf16[2,7,64,128]{3,2,1,0:T(8,128)(2,1)S(1)}, u32[]{:S(2)}, u32[]{:S(2)}) collective-permute-start(bf16[2,7,64,128]{3,2,1,0:T(8,128)(2,1)S(1)} %get-tuple-element.24), channel_id=1, source_target_pairs={{0,2},{1,3},{2,0},{3,1},{4,6},{5,7},{6,4},{7,5},{8,10},{9,11},{10,... | collective-permute-start | bytes 688136 | tf_op jit(solution)/shard_map/ppermute | solution.py:22
  142.4 2.1 %collective-permute-start.23 = (bf16[2,10,64,128]{3,2,1,0:T(8,128)(2,1)S(1)}, bf16[2,10,64,128]{3,2,1,0:T(8,128)(2,1)S(1)}, u32[]{:S(2)}, u32[]{:S(2)}) collective-permute-start(bf16[2,10,64,128]{3,2,1,0:T(8,128)(2,1)S(1)} %pad_maximum_fusion.6), channel_id=1, source_target_pairs={{0,2},{1,3},{2,0},{3,1},{4,6},{5,7},{6,4},{7,5},{8,10},{9,11},{10,... | collective-permute-start | bytes 983048 | tf_op jit(solution)/shard_map/ppermute | solution.py:22
  147.5 3.9 %collective-permute-done.12.refs_3_ = bf16[2,7,64,128]{3,2,1,0:T(8,128)(2,1)S(1)} collective-permute-done((bf16[2,7,64,128]{3,2,1,0:T(8,128)(2,1)S(1)}, bf16[2,7,64,128]{3,2,1,0:T(8,128)(2,1)S(1)}, u32[]{:S(2)}, u32[]{:S(2)}) %collective-permute-start.12) | collective-permute-done | bytes 229408 | tf_op jit(solution)/shard_map/ppermute | solution.py:22
  152.7 2.1 %collective-permute-start.15 = (bf16[2,10,64,128]{3,2,1,0:T(8,128)(2,1)}, bf16[2,10,64,128]{3,2,1,0:T(8,128)(2,1)}, u32[]{:S(2)}, u32[]{:S(2)}) collective-permute-start(bf16[2,10,64,128]{3,2,1,0:T(8,128)(2,1)} %pad_maximum_fusion.2), channel_id=1, source_target_pairs={{0,1},{1,0},{2,3},{3,2},{4,5},{5,4},{6,7},{7,6},{8,9},{9,8},{10,11... | collective-permute-start | bytes 983048 | tf_op jit(solution)/shard_map/ppermute | solution.py:22
  158.8 2.2 %join.5.refs_5_ = bf16[16,64,2048]{2,1,0:T(8,128)(2,1)} custom-call(s32[1]{0:T(128)} %bitcast.me_ref, bf16[4,10,64,128]{3,2,1,0:T(8,128)(2,1)} %get-tuple-element.21.refs_0_, bf16[4,10,64,128]{3,2,1,0:T(8,128)(2,1)} %copy-done, bf16[2,10,64,128]{3,2,1,0:T(8,128)(2,1)} %copy-done.1, bf16[2,10,64,128]{3,2,1,0:T(8,128)(2,1)} %copy-done.2, ...), custom_call_target="tpu_custom_call" | custom-call | flops 6000000 | bytes 1572864 | tf_op jit(solution)/shard_map/join/pallas_call | solution.py:200
  163.8 2.0 %collective-permute-done.17.refs_4_ = bf16[2,10,64,128]{3,2,1,0:T(8,128)(2,1)} collective-permute-done((bf16[2,10,64,128]{3,2,1,0:T(8,128)(2,1)}, bf16[2,10,64,128]{3,2,1,0:T(8,128)(2,1)}, u32[]{:S(2)}, u32[]{:S(2)}) %collective-permute-start.17) | collective-permute-done | bytes 327712 | tf_op jit(solution)/shard_map/ppermute | solution.py:22
  165.9 2.4 %join.7.refs_5_ = bf16[16,64,2048]{2,1,0:T(8,128)(2,1)} custom-call(s32[1]{0:T(128)} %bitcast.me_ref, bf16[4,10,64,128]{3,2,1,0:T(8,128)(2,1)} %get-tuple-element.17.refs_0_, bf16[4,10,64,128]{3,2,1,0:T(8,128)(2,1)} %copy-done.6, bf16[2,10,64,128]{3,2,1,0:T(8,128)(2,1)} %collective-permute-done.15.refs_2_, ...), custom_call_target="tpu_custom_call", output_to_operand_aliasing={{}: (6, {})} | custom-call | flops 10000000 | bytes 2621440 | tf_op jit(solution)/shard_map/join/pallas_call | solution.py:200
  169.0 2.3 %join.8.refs_1_ = bf16[16,64,2048]{2,1,0:T(8,128)(2,1)} custom-call(s32[1]{0:T(128)} %bitcast.me_ref, bf16[2,7,64,128]{3,2,1,0:T(8,128)(2,1)} %get-tuple-element.26.refs_0_, bf16[2,7,64,128]{3,2,1,0:T(8,128)(2,1)} %copy-done.7, bf16[2,7,64,128]{3,2,1,0:T(8,128)(2,1)} %copy-done.8, bf16[2,7,64,128]{3,2,1,0:T(8,128)(2,1)} %copy-done.9, ...), custom_call_target="tpu_custom_call", output_to_operand_aliasing={{}: (6, {})} | custom-call | flops 7000000 | bytes 1835008 | tf_op jit(solution)/shard_map/join/pallas_call | solution.py:200
  171.4 2.3 %join.9 = bf16[16,64,2048]{2,1,0:T(8,128)(2,1)} custom-call(s32[1]{0:T(128)} %bitcast.me_ref, bf16[8,7,64,128]{3,2,1,0:T(8,128)(2,1)} %collective-permute-done.8.refs_0_, bf16[16,64,2048]{2,1,0:T(8,128)(2,1)} %join.8.refs_1_), custom_call_target="tpu_custom_call", output_to_operand_aliasing={{}: (2, {})} | custom-call | flops 7000000 | bytes 1835008 | tf_op jit(solution)/shard_map/join/pallas_call | solution.py:200
  (107 shorter events, 27.7 us)
Async XLA Ops:
  6.3 4.4 %collective-permute-start = (f32[16,8,128]{2,1,0:T(8,128)S(1)}, f32[16,8,128]{2,1,0:T(8,128)S(1)}, u32[]{:S(2)}, u32[]{:S(2)}) collective-permute-start(f32[16,8,128]{2,1,0:T(8,128)S(1)} %bitcast.12), channel_id=1, source_target_pairs={{0,1},{1,0},{2,3},{3,2},{4,5},{5,4},{6,7},{7,6},{8,9},{9,8},{10,11... | collective-permute-start | bytes 196616 | tf_op jit(solution)/shard_map/ppermute | solution.py:22
  10.6 5.9 %collective-permute-start.1 = (f32[16,8,128]{2,1,0:T(8,128)S(1)}, f32[16,8,128]{2,1,0:T(8,128)S(1)}, u32[]{:S(2)}, u32[]{:S(2)}) collective-permute-start(f32[16,8,128]{2,1,0:T(8,128)S(1)} %bitcast_add_fusion), channel_id=1, source_target_pairs={{0,2},{1,3},{2,0},{3,1},{4,6},{5,7},{6,4},{7,5},{8,10},{9,11},{10,... | collective-permute-start | bytes 196616 | tf_op jit(solution)/shard_map/ppermute | solution.py:22
  16.5 11.5 %collective-permute-start.2 = (f32[16,8,128]{2,1,0:T(8,128)S(1)}, f32[16,8,128]{2,1,0:T(8,128)S(1)}, u32[]{:S(2)}, u32[]{:S(2)}) collective-permute-start(f32[16,8,128]{2,1,0:T(8,128)S(1)} %add.16), channel_id=1, source_target_pairs={{0,4},{1,5},{2,6},{3,7},{4,0},{5,1},{6,2},{7,3},{8,12},{9,13},{10,... | collective-permute-start | bytes 196616 | tf_op jit(solution)/shard_map/ppermute | solution.py:22
  21.7 42.9 %collective-permute-start.19 = (f32[8,1,64,128]{3,2,1,0:T(8,128)}, f32[8,1,64,128]{3,2,1,0:T(8,128)S(1)}, u32[]{:S(2)}, u32[]{:S(2)}) collective-permute-start(f32[8,1,64,128]{3,2,1,0:T(8,128)} %get-tuple-element.19), channel_id=1, source_target_pairs={{0,8},{1,9},{2,10},{3,11},{4,12},{5,13},{6,14},{7,15},{8,0},{9,1},... | collective-permute-start | bytes 786440 | tf_op jit(solution)/shard_map/ppermute | solution.py:22
  28.0 36.7 %collective-permute-start.20 = (f32[8,1,64,128]{3,2,1,0:T(8,128)}, f32[8,1,64,128]{3,2,1,0:T(8,128)S(1)}, u32[]{:S(2)}, u32[]{:S(2)}) collective-permute-start(f32[8,1,64,128]{3,2,1,0:T(8,128)} %get-tuple-element.20), channel_id=1, source_target_pairs={{0,8},{1,9},{2,10},{3,11},{4,12},{5,13},{6,14},{7,15},{8,0},{9,1},... | collective-permute-start | bytes 786440 | tf_op jit(solution)/shard_map/ppermute | solution.py:22
  28.0 24.1 %collective-permute-start.3 = (f32[16,8,128]{2,1,0:T(8,128)S(1)}, f32[16,8,128]{2,1,0:T(8,128)S(1)}, u32[]{:S(2)}, u32[]{:S(2)}) collective-permute-start(f32[16,8,128]{2,1,0:T(8,128)S(1)} %add.17), channel_id=1, source_target_pairs={{0,8},{1,9},{2,10},{3,11},{4,12},{5,13},{6,14},{7,15},{8,0},{9,1},... | collective-permute-start | bytes 196616 | tf_op jit(solution)/shard_map/ppermute | solution.py:22
  52.1 12.5 %collective-permute-start.18 = (bf16[64,128]{1,0:T(8,128)(2,1)S(1)}, bf16[64,128]{1,0:T(8,128)(2,1)S(1)}, u32[]{:S(2)}, u32[]{:S(2)}) collective-permute-start(bf16[64,128]{1,0:T(8,128)(2,1)S(1)} %bitcast.14), channel_id=1, source_target_pairs={{0,8},{1,9},{2,10},{3,11},{4,12},{5,13},{6,14},{7,15},{8,0},{9,1},... | collective-permute-start | bytes 49160 | tf_op jit(solution)/shard_map/ppermute | solution.py:22
  64.6 16.1 %copy-start.21 = (bf16[2,7,64,128]{3,2,1,0:T(8,128)(2,1)S(1)}, bf16[2,7,64,128]{3,2,1,0:T(8,128)(2,1)}, u32[]{:S(2)}) copy-start(bf16[2,7,64,128]{3,2,1,0:T(8,128)(2,1)} %get-tuple-element.14) | copy-start | bytes 688132
  64.6 16.6 %copy-start.20 = (bf16[2,7,64,128]{3,2,1,0:T(8,128)(2,1)S(1)}, bf16[2,7,64,128]{3,2,1,0:T(8,128)(2,1)}, u32[]{:S(2)}) copy-start(bf16[2,7,64,128]{3,2,1,0:T(8,128)(2,1)} %get-tuple-element.15) | copy-start | bytes 688132
  64.6 19.0 %copy-start.13 = (bf16[2,7,64,128]{3,2,1,0:T(8,128)(2,1)S(1)}, bf16[2,7,64,128]{3,2,1,0:T(8,128)(2,1)}, u32[]{:S(2)}) copy-start(bf16[2,7,64,128]{3,2,1,0:T(8,128)(2,1)} %get-tuple-element.13) | copy-start | bytes 688132
  64.6 22.1 %copy-start.19 = (bf16[2,7,64,128]{3,2,1,0:T(8,128)(2,1)S(1)}, bf16[2,7,64,128]{3,2,1,0:T(8,128)(2,1)}, u32[]{:S(2)}) copy-start(bf16[2,7,64,128]{3,2,1,0:T(8,128)(2,1)} %get-tuple-element.16) | copy-start | bytes 688132
  69.8 24.0 %collective-permute-start.21 = (bf16[4,10,64,128]{3,2,1,0:T(8,128)(2,1)}, bf16[4,10,64,128]{3,2,1,0:T(8,128)(2,1)S(1)}, u32[]{:S(2)}, u32[]{:S(2)}) collective-permute-start(bf16[4,10,64,128]{3,2,1,0:T(8,128)(2,1)} %get-tuple-element.22), channel_id=1, source_target_pairs={{0,4},{1,5},{2,6},{3,7},{4,0},{5,1},{6,2},{7,3},{8,12},{9,13},{10,... | collective-permute-start | bytes 1966088 | tf_op jit(solution)/shard_map/ppermute | solution.py:22
  71.3 31.9 %collective-permute-start.14 = (bf16[4,10,64,128]{3,2,1,0:T(8,128)(2,1)S(1)}, bf16[4,10,64,128]{3,2,1,0:T(8,128)(2,1)S(1)}, u32[]{:S(2)}, u32[]{:S(2)}) collective-permute-start(bf16[4,10,64,128]{3,2,1,0:T(8,128)(2,1)S(1)} %copy-done.18), channel_id=1, source_target_pairs={{0,4},{1,5},{2,6},{3,7},{4,0},{5,1},{6,2},{7,3},{8,12},{9,13},{10,... | collective-permute-start | bytes 1966088 | tf_op jit(solution)/shard_map/ppermute | solution.py:22
  74.6 61.0 %collective-permute-start.9 = (bf16[8,7,64,128]{3,2,1,0:T(8,128)(2,1)}, bf16[8,7,64,128]{3,2,1,0:T(8,128)(2,1)S(1)}, u32[]{:S(2)}, u32[]{:S(2)}) collective-permute-start(bf16[8,7,64,128]{3,2,1,0:T(8,128)(2,1)} %spread.4), channel_id=1, source_target_pairs={{0,8},{1,9},{2,10},{3,11},{4,12},{5,13},{6,14},{7,15},{8,0},{9,1},... | collective-permute-start | bytes 2752520 | tf_op jit(solution)/shard_map/ppermute | solution.py:22
  80.6 6.0 %collective-permute-start.4 = (bf16[2,7,64,128]{3,2,1,0:T(8,128)(2,1)S(1)}, bf16[2,7,64,128]{3,2,1,0:T(8,128)(2,1)S(1)}, u32[]{:S(2)}, u32[]{:S(2)}) collective-permute-start(bf16[2,7,64,128]{3,2,1,0:T(8,128)(2,1)S(1)} %copy-done.21), channel_id=1, source_target_pairs={{0,1},{1,0},{2,3},{3,2},{4,5},{5,4},{6,7},{7,6},{8,9},{9,8},{10,11... | collective-permute-start | bytes 688136 | tf_op jit(solution)/shard_map/ppermute | solution.py:22
  81.2 8.9 %collective-permute-start.5 = (bf16[2,7,64,128]{3,2,1,0:T(8,128)(2,1)S(1)}, bf16[2,7,64,128]{3,2,1,0:T(8,128)(2,1)S(1)}, u32[]{:S(2)}, u32[]{:S(2)}) collective-permute-start(bf16[2,7,64,128]{3,2,1,0:T(8,128)(2,1)S(1)} %copy-done.20), channel_id=1, source_target_pairs={{0,2},{1,3},{2,0},{3,1},{4,6},{5,7},{6,4},{7,5},{8,10},{9,11},{10,... | collective-permute-start | bytes 688136 | tf_op jit(solution)/shard_map/ppermute | solution.py:22
  86.7 6.0 %collective-permute-start.6 = (bf16[2,7,64,128]{3,2,1,0:T(8,128)(2,1)S(1)}, bf16[2,7,64,128]{3,2,1,0:T(8,128)(2,1)S(1)}, u32[]{:S(2)}, u32[]{:S(2)}) collective-permute-start(bf16[2,7,64,128]{3,2,1,0:T(8,128)(2,1)S(1)} %copy-done.19), channel_id=1, source_target_pairs={{0,3},{1,2},{2,1},{3,0},{4,7},{5,6},{6,5},{7,4},{8,11},{9,10},{10,... | collective-permute-start | bytes 688136 | tf_op jit(solution)/shard_map/ppermute | solution.py:22
  93.4 14.8 %collective-permute-start.7 = (bf16[4,7,64,128]{3,2,1,0:T(8,128)(2,1)S(1)}, bf16[4,7,64,128]{3,2,1,0:T(8,128)(2,1)S(1)}, u32[]{:S(2)}, u32[]{:S(2)}) collective-permute-start(bf16[4,7,64,128]{3,2,1,0:T(8,128)(2,1)S(1)} %pad_maximum_fusion), channel_id=1, source_target_pairs={{0,4},{1,5},{2,6},{3,7},{4,0},{5,1},{6,2},{7,3},{8,12},{9,13},{10,... | collective-permute-start | bytes 1376264 | tf_op jit(solution)/shard_map/ppermute | solution.py:22
  93.8 53.7 %copy-start = (bf16[4,10,64,128]{3,2,1,0:T(8,128)(2,1)}, bf16[4,10,64,128]{3,2,1,0:T(8,128)(2,1)S(1)}, u32[]{:S(2)}) copy-start(bf16[4,10,64,128]{3,2,1,0:T(8,128)(2,1)S(1)} %collective-permute-done.21.refs_1_) | copy-start | bytes 1966084
  93.9 58.8 %collective-permute-start.22 = (bf16[2,10,64,128]{3,2,1,0:T(8,128)(2,1)S(1)}, bf16[2,10,64,128]{3,2,1,0:T(8,128)(2,1)S(1)}, u32[]{:S(2)}, u32[]{:S(2)}) collective-permute-start(bf16[2,10,64,128]{3,2,1,0:T(8,128)(2,1)S(1)} %pad_maximum_fusion.5), channel_id=1, source_target_pairs={{0,1},{1,0},{2,3},{3,2},{4,5},{5,4},{6,7},{7,6},{8,9},{9,8},{10,11... | collective-permute-start | bytes 983048 | tf_op jit(solution)/shard_map/ppermute | solution.py:22
  103.2 55.6 %copy-start.6 = (bf16[4,10,64,128]{3,2,1,0:T(8,128)(2,1)}, bf16[4,10,64,128]{3,2,1,0:T(8,128)(2,1)S(1)}, u32[]{:S(2)}) copy-start(bf16[4,10,64,128]{3,2,1,0:T(8,128)(2,1)S(1)} %collective-permute-done.14.refs_1_) | copy-start | bytes 1966084
  109.0 62.3 %collective-permute-start.8 = (bf16[8,7,64,128]{3,2,1,0:T(8,128)(2,1)}, bf16[8,7,64,128]{3,2,1,0:T(8,128)(2,1)}, u32[]{:S(2)}, u32[]{:S(2)}) collective-permute-start(bf16[8,7,64,128]{3,2,1,0:T(8,128)(2,1)} %constant_dynamic-update-slice_fusion), channel_id=1, source_target_pairs={{0,8},{1,9},{2,10},{3,11},{4,12},{5,13},{6,14},{7,15},{8,0},{9,1},... | collective-permute-start | bytes 2752520 | tf_op jit(solution)/shard_map/ppermute | solution.py:22
  136.4 6.0 %collective-permute-start.10 = (bf16[2,7,64,128]{3,2,1,0:T(8,128)(2,1)S(1)}, bf16[2,7,64,128]{3,2,1,0:T(8,128)(2,1)S(1)}, u32[]{:S(2)}, u32[]{:S(2)}) collective-permute-start(bf16[2,7,64,128]{3,2,1,0:T(8,128)(2,1)S(1)} %get-tuple-element.25), channel_id=1, source_target_pairs={{0,1},{1,0},{2,3},{3,2},{4,5},{5,4},{6,7},{7,6},{8,9},{9,8},{10,11... | collective-permute-start | bytes 688136 | tf_op jit(solution)/shard_map/ppermute | solution.py:22
  136.9 9.0 %collective-permute-start.11 = (bf16[2,7,64,128]{3,2,1,0:T(8,128)(2,1)S(1)}, bf16[2,7,64,128]{3,2,1,0:T(8,128)(2,1)S(1)}, u32[]{:S(2)}, u32[]{:S(2)}) collective-permute-start(bf16[2,7,64,128]{3,2,1,0:T(8,128)(2,1)S(1)} %get-tuple-element.24), channel_id=1, source_target_pairs={{0,2},{1,3},{2,0},{3,1},{4,6},{5,7},{6,4},{7,5},{8,10},{9,11},{10,... | collective-permute-start | bytes 688136 | tf_op jit(solution)/shard_map/ppermute | solution.py:22
  139.4 12.1 %collective-permute-start.12 = (bf16[2,7,64,128]{3,2,1,0:T(8,128)(2,1)S(1)}, bf16[2,7,64,128]{3,2,1,0:T(8,128)(2,1)S(1)}, u32[]{:S(2)}, u32[]{:S(2)}) collective-permute-start(bf16[2,7,64,128]{3,2,1,0:T(8,128)(2,1)S(1)} %get-tuple-element.23), channel_id=1, source_target_pairs={{0,3},{1,2},{2,1},{3,0},{4,7},{5,6},{6,5},{7,4},{8,11},{9,10},{10,... | collective-permute-start | bytes 688136 | tf_op jit(solution)/shard_map/ppermute | solution.py:22
  142.4 18.7 %copy-start.7 = (bf16[2,7,64,128]{3,2,1,0:T(8,128)(2,1)}, bf16[2,7,64,128]{3,2,1,0:T(8,128)(2,1)S(1)}, u32[]{:S(2)}) copy-start(bf16[2,7,64,128]{3,2,1,0:T(8,128)(2,1)S(1)} %collective-permute-done.10.refs_1_) | copy-start | bytes 688132
  142.4 12.4 %collective-permute-start.23 = (bf16[2,10,64,128]{3,2,1,0:T(8,128)(2,1)S(1)}, bf16[2,10,64,128]{3,2,1,0:T(8,128)(2,1)S(1)}, u32[]{:S(2)}, u32[]{:S(2)}) collective-permute-start(bf16[2,10,64,128]{3,2,1,0:T(8,128)(2,1)S(1)} %pad_maximum_fusion.6), channel_id=1, source_target_pairs={{0,2},{1,3},{2,0},{3,1},{4,6},{5,7},{6,4},{7,5},{8,10},{9,11},{10,... | collective-permute-start | bytes 983048 | tf_op jit(solution)/shard_map/ppermute | solution.py:22
  145.9 9.1 %collective-permute-start.24 = (bf16[2,10,64,128]{3,2,1,0:T(8,128)(2,1)S(1)}, bf16[2,10,64,128]{3,2,1,0:T(8,128)(2,1)S(1)}, u32[]{:S(2)}, u32[]{:S(2)}) collective-permute-start(bf16[2,10,64,128]{3,2,1,0:T(8,128)(2,1)S(1)} %pad_maximum_fusion.7), channel_id=1, source_target_pairs={{0,3},{1,2},{2,1},{3,0},{4,7},{5,6},{6,5},{7,4},{8,11},{9,10},{10,... | collective-permute-start | bytes 983048 | tf_op jit(solution)/shard_map/ppermute | solution.py:22
  151.5 16.7 %collective-permute-start.13 = (bf16[4,7,64,128]{3,2,1,0:T(8,128)(2,1)S(1)}, bf16[4,7,64,128]{3,2,1,0:T(8,128)(2,1)S(1)}, u32[]{:S(2)}, u32[]{:S(2)}) collective-permute-start(bf16[4,7,64,128]{3,2,1,0:T(8,128)(2,1)S(1)} %pad_maximum_fusion.1), channel_id=1, source_target_pairs={{0,4},{1,5},{2,6},{3,7},{4,0},{5,1},{6,2},{7,3},{8,12},{9,13},{10,... | collective-permute-start | bytes 1376264 | tf_op jit(solution)/shard_map/ppermute | solution.py:22
  152.7 10.1 %collective-permute-start.15 = (bf16[2,10,64,128]{3,2,1,0:T(8,128)(2,1)}, bf16[2,10,64,128]{3,2,1,0:T(8,128)(2,1)}, u32[]{:S(2)}, u32[]{:S(2)}) collective-permute-start(bf16[2,10,64,128]{3,2,1,0:T(8,128)(2,1)} %pad_maximum_fusion.2), channel_id=1, source_target_pairs={{0,1},{1,0},{2,3},{3,2},{4,5},{5,4},{6,7},{7,6},{8,9},{9,8},{10,11... | collective-permute-start | bytes 983048 | tf_op jit(solution)/shard_map/ppermute | solution.py:22
  154.8 9.0 %collective-permute-start.16 = (bf16[2,10,64,128]{3,2,1,0:T(8,128)(2,1)}, bf16[2,10,64,128]{3,2,1,0:T(8,128)(2,1)}, u32[]{:S(2)}, u32[]{:S(2)}) collective-permute-start(bf16[2,10,64,128]{3,2,1,0:T(8,128)(2,1)} %pad_maximum_fusion.3), channel_id=1, source_target_pairs={{0,2},{1,3},{2,0},{3,1},{4,6},{5,7},{6,4},{7,5},{8,10},{9,11},{10,... | collective-permute-start | bytes 983048 | tf_op jit(solution)/shard_map/ppermute | solution.py:22
  155.0 10.9 %collective-permute-start.17 = (bf16[2,10,64,128]{3,2,1,0:T(8,128)(2,1)}, bf16[2,10,64,128]{3,2,1,0:T(8,128)(2,1)}, u32[]{:S(2)}, u32[]{:S(2)}) collective-permute-start(bf16[2,10,64,128]{3,2,1,0:T(8,128)(2,1)} %pad_maximum_fusion.4), channel_id=1, source_target_pairs={{0,3},{1,2},{2,1},{3,0},{4,7},{5,6},{6,5},{7,4},{8,11},{9,10},{10,... | collective-permute-start | bytes 983048 | tf_op jit(solution)/shard_map/ppermute | solution.py:22
  (15 other events, 80.6 us)

commit v5 on v4

--- a/solution.py
+++ b/solution.py
@@ -13,9 +13,11 @@
 LANES = 128
 HALF = 512
 
-F, L, E = (0, 7), (7, 7), (14, 2)
-RAW = (1, 1)
+F, L, E = (0, 6), (6, 7), (13, 3)
+RAW = (2, 1)
 A, B = (0, 10), (10, 6)
+
+SMALL = pltpu.CompilerParams(vmem_limit_bytes=12 * 2**20)
 
 
 def swap(shard, k):
@@ -89,6 +91,7 @@
         ),
         out_shape=[jax.ShapeDtypeStruct((blocks, count, ROWS, LANES), kind)] * arrays,
         name="spread",
+        compiler_params=SMALL,
         cost_estimate=pl.CostEstimate(
             flops=count * 1_000_000, bytes_accessed=count * 393_216, transcendentals=0
         ),
@@ -144,6 +147,7 @@
         ),
         out_shape=[jax.ShapeDtypeStruct((4, slots, ROWS, LANES), jnp.bfloat16)] * 2,
         name="spread_own",
+        compiler_params=SMALL,
         cost_estimate=pl.CostEstimate(
             flops=slots * 1_000_000, bytes_accessed=slots * 393_216, transcendentals=0
         ),
@@ -211,6 +215,7 @@
         out_shape=jax.ShapeDtypeStruct((EXPERTS, ROWS, D_MODEL), jnp.bfloat16),
         input_output_aliases=alias,
         name="join",
+        compiler_params=SMALL,
         cost_estimate=pl.CostEstimate(
             flops=count * 1_000_000, bytes_accessed=count * 262_144, transcendentals=0
         ),
@@ -240,33 +245,54 @@
     return [(have[k], 1, [k]) for k in range(4)] + [(over_y, 4, [4, 5, 6, 7])]
 
 
-def router_kernel(where, me_ref, *refs):
+def join_b_kernel(where, me_ref, *refs):
     me = me_ref[0]
+    out_ref, router_ref = refs[-2:]
+    count = out_ref.shape[0]
     for ref, places in zip(refs, where):
         for place, r in places:
-            for z in range(2):
-                at = pl.multiple_of((me ^ (8 * z + r)) * LANES, LANES)
-                refs[-1][:, pl.ds(at, LANES)] = ref[place, z]
-
-
-def router_join(pieces, me, slot):
+            near = pl.ds(pl.multiple_of((me ^ r) * LANES, LANES), LANES)
+            far = pl.ds(pl.multiple_of((me ^ r ^ 8) * LANES, LANES), LANES)
+            for i in range(count):
+                out_ref[i, :, near] = ref[place, i]
+            router_ref[:, near] = ref[place, count]
+            router_ref[:, far] = ref[place, count + 1]
+            for i in range(E[1]):
+                out_ref[count - E[1] + i, :, far] = ref[place, count + 2 + i]
+
+
+def join_b(out, pieces, me):
+    first, count = B
+    assert first + count == E[0] + E[1] == EXPERTS and E[0] >= first
+    slots = count + 2 + E[1]
     where = [list(enumerate(rs)) for _, _, rs in pieces]
-    assert slot % 2 == 0
-    return pl.pallas_call(
-        functools.partial(router_kernel, where),
+    return pl.pallas_call(
+        functools.partial(join_b_kernel, where),
         grid_spec=pltpu.PrefetchScalarGridSpec(
             num_scalar_prefetch=1,
             grid=(1,),
             in_specs=[
-                pl.BlockSpec((taken, 2, ROWS, LANES), lambda e, m: (0, slot // 2, 0, 0))
+                pl.BlockSpec((taken, slots, ROWS, LANES), lambda e, m: (0, 0, 0, 0))
                 for _, taken, _ in pieces
+            ]
+            + [pl.BlockSpec(memory_space=pl.ANY)],
+            out_specs=[
+                pl.BlockSpec(
+                    (pl.Element(count), pl.Element(ROWS), pl.Element(D_MODEL)),
+                    lambda e, m: (first, 0, 0),
+                ),
+                pl.BlockSpec((ROWS, D_MODEL), lambda e, m: (0, 0)),
             ],
-            out_specs=pl.BlockSpec((ROWS, D_MODEL), lambda e, m: (0, 0)),
-        ),
-        out_shape=jax.ShapeDtypeStruct((ROWS, D_MODEL), jnp.bfloat16),
-        name="router",
-        cost_estimate=pl.CostEstimate(flops=2_000_000, bytes_accessed=524_288, transcendentals=0),
-    )(me, *[array for array, _, _ in pieces])
+        ),
+        out_shape=[
+            jax.ShapeDtypeStruct((EXPERTS, ROWS, D_MODEL), jnp.bfloat16),
+            jax.ShapeDtypeStruct((ROWS, D_MODEL), jnp.bfloat16),
+        ],
+        input_output_aliases={len(pieces) + 1: 0},
+        name="join_b",
+        compiler_params=SMALL,
+        cost_estimate=pl.CostEstimate(flops=8_000_000, bytes_accessed=2_097_152, transcendentals=0),
+    )(me, *[array for array, _, _ in pieces], out)
 
 
 def on_device(w_down, router_weight, router_gain):
@@ -300,13 +326,11 @@
 
     scale = lax.dynamic_slice_in_dim(sums.reshape(EXPERTS, 16, ROWS), index, 1, 1)[:, 0] / D_MODEL
 
-    out = join(None, plane_b, me, B, 0, B[1])
-    serve_router = router_join(plane_b, me, B[1]).T
-    out = join(out, plane_b, me, E, 1, E[1], B[1] + 2)
-    out = join(out, plane_a, me, A, 0, 5)
+    out = join(None, plane_a, me, A, 0, 5)
+    out, router = join_b(out, plane_b, me)
     out = join(out, pieces_of(*plane_f), me, F, 1, F[1])
     out = join(out, [(came_l, 8, list(range(8)))], me, L, 1, L[1])
-    return (out, scale, serve_router)
+    return (out, scale, router.T)
 
 
 def solution(mesh):

time: 177 us -> 167 us (0.944)
  blocking collectives: 18.1 us -> 0 us
  Pallas kernels: 30.1 us -> 16.7 us
  waiting for transfers between devices: 56.5 us -> 67.5 us
  starting transfers between devices: 51 us -> 56.4 us
  local copies, waits for them, and re-layouts: 8.34 us -> 12.9 us
    all_to_all x1 -> x0, blocking collectives: 18.1 us -> none  [on_device(): lax.all_to_all(jnp.broadcast_to(part[None], (4, 16, LANES)), 'ep', 0, 0,...]
    ppermute x25, waiting for transfers between devices: 56.5 us -> 67.5 us  [swap(): lax.ppermute(shard, 'fsdp', [(i, i ^ k) for i in range(lax.axis_size('fsd...]
    pallas_call x3, Pallas kernels: 11.8 us -> 5.01 us  [spread(): pl.pallas_call(functools.partial(spread_kernel, other, scaled), grid_spec...]
    unnamed x45 -> x27, local copies, waits for them, and re-layouts: 2.77 us -> 8.54 us
    pallas_call x5 -> x3, Pallas kernels: 10.9 us -> 5.58 us  [join(): pl.pallas_call(functools.partial(join_kernel, where), grid_spec=pltpu.Pre...]
    all_to_all x0 -> x1, starting transfers between devices: none -> 4.22 us  [on_device(): lax.all_to_all(jnp.broadcast_to(part[None], (4, 16, LANES)), 'ep', 0, 0,...]
    pallas_call x1, Pallas kernels: 3.81 us -> 1.25 us  [spread_own(): pl.pallas_call(own_kernel, grid_spec=pltpu.PrefetchScalarGridSpec(num_sca...]
  transfers between devices with their start and end apart: 25 -> 26, of which waited for: 14 -> 13; matrix products, arithmetic and copies ran while one was open for 5% -> 5% of each run, Pallas kernels for 14% -> 9%
where the time goes in v5:
time: 167 us; the launch traced here: 164 us
  waiting for transfers between devices  67.5 us (40%)
  starting transfers between devices  56.4 us (34%)
  Pallas kernels  16.7 us (10%)
  local copies, waits for them, and re-layouts  12.9 us (8%)
  other arithmetic  9.55 us (6%)
    ppermute x25, waiting for transfers between devices, swap(): lax.ppermute(shard, 'fsdp', [(i, i ^ k) for i in range(lax.axis_size('fsd...  67.5 us
    ppermute x25, starting transfers between devices, swap(): lax.ppermute(shard, 'fsdp', [(i, i ^ k) for i in range(lax.axis_size('fsd...  52.1 us
    unnamed x27, local copies, waits for them, and re-layouts  8.54 us
    reduce_sum x1, other arithmetic, on_device(): sums = jnp.sum(jnp.abs(w_down), axis=2).reshape(EXPERTS, 8, LANES)  5.62 us
    pallas_call x3, Pallas kernels, join(): pl.pallas_call(functools.partial(join_kernel, where), grid_spec=pltpu.Pre...  5.58 us
    pallas_call x3, Pallas kernels, spread(): pl.pallas_call(functools.partial(spread_kernel, other, scaled), grid_spec...  5.01 us
    all_to_all x1, starting transfers between devices, on_device(): lax.all_to_all(jnp.broadcast_to(part[None], (4, 16, LANES)), 'ep', 0, 0,...  4.22 us
  transfers between devices with their start and end apart: 26, of which 13 were waited for; matrix products, arithmetic and copies ran while one was open for 5% of the time, Pallas kernels for 9%

profile of v5, /device:TPU:34, one launch (start us, length us, event | category | flops | bytes accessed | tf_op | source)
XLA Modules:
  0.0 164.0 jit_solution(7590309270897076655)
XLA Ops:
  0.7 5.6 %abs_reduce_fusion = f32[16,1024]{1,0:T(8,128)S(1)} fusion(f32[16,1024,128]{2,1,0:T(8,128)} %w_ref.9), kind=kLoop, calls=%fused_computation | loop fusion | flops 4177920 | bytes 8454144 | tf_op jit(solution)/shard_map/reduce_sum | solution.py:302
  6.9 3.7 %collective-permute-done = f32[16,8,128]{2,1,0:T(8,128)S(1)} collective-permute-done((f32[16,8,128]{2,1,0:T(8,128)S(1)}, f32[16,8,128]{2,1,0:T(8,128)S(1)}, u32[]{:S(2)}, u32[]{:S(2)}) %collective-permute-start) | collective-permute-done | bytes 65568 | tf_op jit(solution)/shard_map/ppermute | solution.py:24
  10.7 2.2 %collective-permute-start.1 = (f32[16,8,128]{2,1,0:T(8,128)S(1)}, f32[16,8,128]{2,1,0:T(8,128)S(1)}, u32[]{:S(2)}, u32[]{:S(2)}) collective-permute-start(f32[16,8,128]{2,1,0:T(8,128)S(1)} %bitcast_add_fusion), channel_id=1, source_target_pairs={{0,2},{1,3},{2,0},{3,1},{4,6},{5,7},{6,4},{7,5},{8,10},{9,11},{10,... | collective-permute-start | bytes 196616 | tf_op jit(solution)/shard_map/ppermute | solution.py:24
  12.9 3.6 %collective-permute-done.1 = f32[16,8,128]{2,1,0:T(8,128)S(1)} collective-permute-done((f32[16,8,128]{2,1,0:T(8,128)S(1)}, f32[16,8,128]{2,1,0:T(8,128)S(1)}, u32[]{:S(2)}, u32[]{:S(2)}) %collective-permute-start.1) | collective-permute-done | bytes 65568 | tf_op jit(solution)/shard_map/ppermute | solution.py:24
  16.5 3.3 %collective-permute-start.2 = (f32[16,8,128]{2,1,0:T(8,128)S(1)}, f32[16,8,128]{2,1,0:T(8,128)S(1)}, u32[]{:S(2)}, u32[]{:S(2)}) collective-permute-start(f32[16,8,128]{2,1,0:T(8,128)S(1)} %add.16), channel_id=1, source_target_pairs={{0,4},{1,5},{2,6},{3,7},{4,0},{5,1},{6,2},{7,3},{8,12},{9,13},{10,... | collective-permute-start | bytes 196616 | tf_op jit(solution)/shard_map/ppermute | solution.py:24
  19.8 2.6 %collective-permute-done.2 = f32[16,8,128]{2,1,0:T(8,128)S(1)} collective-permute-done((f32[16,8,128]{2,1,0:T(8,128)S(1)}, f32[16,8,128]{2,1,0:T(8,128)S(1)}, u32[]{:S(2)}, u32[]{:S(2)}) %collective-permute-start.2) | collective-permute-done | bytes 65568 | tf_op jit(solution)/shard_map/ppermute | solution.py:24
  22.4 6.4 %collective-permute-start.3 = (f32[16,8,128]{2,1,0:T(8,128)S(1)}, f32[16,8,128]{2,1,0:T(8,128)S(1)}, u32[]{:S(2)}, u32[]{:S(2)}) collective-permute-start(f32[16,8,128]{2,1,0:T(8,128)S(1)} %add.17), channel_id=1, source_target_pairs={{0,8},{1,9},{2,10},{3,11},{4,12},{5,13},{6,14},{7,15},{8,0},{9,1},... | collective-permute-start | bytes 196616 | tf_op jit(solution)/shard_map/ppermute | solution.py:24
  29.4 4.2 %all-to-all-start = ((bf16[4,16,128]{2,1,0:T(8,128)(2,1)}), bf16[4,16,128]{2,1,0:T(8,128)(2,1)S(1)}, u32[]{:S(2)}, u32[]{:S(2)}) async-start(bf16[4,16,128]{2,1,0:T(8,128)(2,1)} %broadcast_in_dim.2), calls=%async_computation | async-start | bytes 32768 | tf_op jit(solution)/shard_map/all_to_all | solution.py:307
  33.6 2.1 %spread_raw.1 = (f32[8,2,64,128]{3,2,1,0:T(8,128)}, f32[8,1,64,128]{3,2,1,0:T(8,128)}) custom-call(s32[1]{0:T(128)} %bitcast.me_ref, f32[16,1024,128]{2,1,0:T(8,128)} %w_ref.9), custom_call_target="tpu_custom_call" | custom-call | flops 3000000 | bytes 1572864 | tf_op jit(solution)/shard_map/spread_raw/pallas_call | solution.py:159
  37.1 4.5 %collective-permute-start.16 = (f32[8,1,64,128]{3,2,1,0:T(8,128)}, f32[8,1,64,128]{3,2,1,0:T(8,128)S(1)}, u32[]{:S(2)}, u32[]{:S(2)}) collective-permute-start(f32[8,1,64,128]{3,2,1,0:T(8,128)} %get-tuple-element.20), channel_id=1, source_target_pairs={{0,8},{1,9},{2,10},{3,11},{4,12},{5,13},{6,14},{7,15},{8,0},{9,1},... | collective-permute-start | bytes 786440 | tf_op jit(solution)/shard_map/ppermute | solution.py:24
  43.1 3.4 %copy-done = f32[16,1024,128]{2,1,0:T(8,128)S(1)} copy-done((f32[16,1024,128]{2,1,0:T(8,128)S(1)}, f32[16,1024,128]{2,1,0:T(8,128)}, u32[]{:S(2)}) %copy-start) | copy-done | bytes 8388632
  46.4 2.4 %spread.5 = (bf16[4,10,64,128]{3,2,1,0:T(8,128)(2,1)S(1)}, bf16[4,10,64,128]{3,2,1,0:T(8,128)(2,1)S(1)}) custom-call(s32[1]{0:T(128)} %bitcast.me_ref, f32[16,1024,128]{2,1,0:T(8,128)S(1)} %copy-done, f32[16,8,128]{2,1,0:T(8,128)S(1)} %add.18.refs_0_.s_ref), custom_call_target="tpu_custom_call" | custom-call | flops 10000000 | bytes 3932160 | tf_op jit(solution)/shard_map/spread/pallas_call | solution.py:83
  51.5 3.3 %collective-permute-start.21 = (bf16[4,10,64,128]{3,2,1,0:T(8,128)(2,1)S(1)}, bf16[4,10,64,128]{3,2,1,0:T(8,128)(2,1)S(1)}, u32[]{:S(2)}, u32[]{:S(2)}) collective-permute-start(bf16[4,10,64,128]{3,2,1,0:T(8,128)(2,1)S(1)} %get-tuple-element.24), channel_id=1, source_target_pairs={{0,4},{1,5},{2,6},{3,7},{4,0},{5,1},{6,2},{7,3},{8,12},{9,13},{10,... | collective-permute-start | bytes 1966088 | tf_op jit(solution)/shard_map/ppermute | solution.py:24
  56.1 7.1 %collective-permute-done.4 = bf16[2,7,64,128]{3,2,1,0:T(8,128)(2,1)S(1)} collective-permute-done((bf16[2,7,64,128]{3,2,1,0:T(8,128)(2,1)S(1)}, bf16[2,7,64,128]{3,2,1,0:T(8,128)(2,1)S(1)}, u32[]{:S(2)}, u32[]{:S(2)}) %collective-permute-start.4) | collective-permute-done | bytes 229408 | tf_op jit(solution)/shard_map/ppermute | solution.py:24
  64.1 6.6 %collective-permute-done.5 = bf16[2,7,64,128]{3,2,1,0:T(8,128)(2,1)S(1)} collective-permute-done((bf16[2,7,64,128]{3,2,1,0:T(8,128)(2,1)S(1)}, bf16[2,7,64,128]{3,2,1,0:T(8,128)(2,1)S(1)}, u32[]{:S(2)}, u32[]{:S(2)}) %collective-permute-start.5) | collective-permute-done | bytes 229408 | tf_op jit(solution)/shard_map/ppermute | solution.py:24
  72.3 4.4 %collective-permute-done.6 = bf16[2,7,64,128]{3,2,1,0:T(8,128)(2,1)S(1)} collective-permute-done((bf16[2,7,64,128]{3,2,1,0:T(8,128)(2,1)S(1)}, bf16[2,7,64,128]{3,2,1,0:T(8,128)(2,1)S(1)}, u32[]{:S(2)}, u32[]{:S(2)}) %collective-permute-start.6) | collective-permute-done | bytes 229408 | tf_op jit(solution)/shard_map/ppermute | solution.py:24
  76.8 4.3 %collective-permute-start.9 = (bf16[8,6,64,128]{3,2,1,0:T(8,128)(2,1)S(1)}, bf16[8,6,64,128]{3,2,1,0:T(8,128)(2,1)S(1)}, u32[]{:S(2)}, u32[]{:S(2)}) collective-permute-start(bf16[8,6,64,128]{3,2,1,0:T(8,128)(2,1)S(1)} %spread.4), channel_id=1, source_target_pairs={{0,8},{1,9},{2,10},{3,11},{4,12},{5,13},{6,14},{7,15},{8,0},{9,1},... | collective-permute-start | bytes 2359304 | tf_op jit(solution)/shard_map/ppermute | solution.py:24
  83.7 3.3 %collective-permute-start.17 = (bf16[4,11,64,128]{3,2,1,0:T(8,128)(2,1)S(1)}, bf16[4,11,64,128]{3,2,1,0:T(8,128)(2,1)S(1)}, u32[]{:S(2)}, u32[]{:S(2)}) collective-permute-start(bf16[4,11,64,128]{3,2,1,0:T(8,128)(2,1)S(1)} %get-tuple-element.22), channel_id=1, source_target_pairs={{0,4},{1,5},{2,6},{3,7},{4,0},{5,1},{6,2},{7,3},{8,12},{9,13},{10,... | collective-permute-start | bytes 2162696 | tf_op jit(solution)/shard_map/ppermute | solution.py:24
  87.2 23.4 %collective-permute-done.9 = bf16[8,6,64,128]{3,2,1,0:T(8,128)(2,1)S(1)} collective-permute-done((bf16[8,6,64,128]{3,2,1,0:T(8,128)(2,1)S(1)}, bf16[8,6,64,128]{3,2,1,0:T(8,128)(2,1)S(1)}, u32[]{:S(2)}, u32[]{:S(2)}) %collective-permute-start.9) | collective-permute-done | bytes 786464 | tf_op jit(solution)/shard_map/ppermute | solution.py:24
  110.8 3.4 %collective-permute-start.12 = (bf16[2,6,64,128]{3,2,1,0:T(8,128)(2,1)S(1)}, bf16[2,6,64,128]{3,2,1,0:T(8,128)(2,1)S(1)}, u32[]{:S(2)}, u32[]{:S(2)}) collective-permute-start(bf16[2,6,64,128]{3,2,1,0:T(8,128)(2,1)S(1)} %get-tuple-element.27), channel_id=1, source_target_pairs={{0,3},{1,2},{2,1},{3,0},{4,7},{5,6},{6,5},{7,4},{8,11},{9,10},{10,... | collective-permute-start | bytes 589832 | tf_op jit(solution)/shard_map/ppermute | solution.py:24
  116.5 2.0 %collective-permute-done.10.refs_1_ = bf16[2,6,64,128]{3,2,1,0:T(8,128)(2,1)S(1)} collective-permute-done((bf16[2,6,64,128]{3,2,1,0:T(8,128)(2,1)S(1)}, bf16[2,6,64,128]{3,2,1,0:T(8,128)(2,1)S(1)}, u32[]{:S(2)}, u32[]{:S(2)}) %collective-permute-start.10) | collective-permute-done | bytes 196640 | tf_op jit(solution)/shard_map/ppermute | solution.py:24
  118.5 1.7 %collective-permute-done.11.refs_2_ = bf16[2,6,64,128]{3,2,1,0:T(8,128)(2,1)S(1)} collective-permute-done((bf16[2,6,64,128]{3,2,1,0:T(8,128)(2,1)S(1)}, bf16[2,6,64,128]{3,2,1,0:T(8,128)(2,1)S(1)}, u32[]{:S(2)}, u32[]{:S(2)}) %collective-permute-start.11) | collective-permute-done | bytes 196640 | tf_op jit(solution)/shard_map/ppermute | solution.py:24
  120.2 3.5 %collective-permute-start.24 = (bf16[2,10,64,128]{3,2,1,0:T(8,128)(2,1)S(1)}, bf16[2,10,64,128]{3,2,1,0:T(8,128)(2,1)S(1)}, u32[]{:S(2)}, u32[]{:S(2)}) collective-permute-start(bf16[2,10,64,128]{3,2,1,0:T(8,128)(2,1)S(1)} %pad_maximum_fusion.7), channel_id=1, source_target_pairs={{0,3},{1,2},{2,1},{3,0},{4,7},{5,6},{6,5},{7,4},{8,11},{9,10},{10,... | collective-permute-start | bytes 983048 | tf_op jit(solution)/shard_map/ppermute | solution.py:24
  124.4 6.1 %collective-permute-start.8 = (bf16[8,7,64,128]{3,2,1,0:T(8,128)(2,1)}, bf16[8,7,64,128]{3,2,1,0:T(8,128)(2,1)}, u32[]{:S(2)}, u32[]{:S(2)}) collective-permute-start(bf16[8,7,64,128]{3,2,1,0:T(8,128)(2,1)} %constant_dynamic-update-slice_fusion), channel_id=1, source_target_pairs={{0,8},{1,9},{2,10},{3,11},{4,12},{5,13},{6,14},{7,15},{8,0},{9,1},... | collective-permute-start | bytes 2752520 | tf_op jit(solution)/shard_map/ppermute | solution.py:24
  134.9 1.8 %collective-permute-start.18 = (bf16[2,11,64,128]{3,2,1,0:T(8,128)(2,1)}, bf16[2,11,64,128]{3,2,1,0:T(8,128)(2,1)}, u32[]{:S(2)}, u32[]{:S(2)}) collective-permute-start(bf16[2,11,64,128]{3,2,1,0:T(8,128)(2,1)} %pad_maximum_fusion.2), channel_id=1, source_target_pairs={{0,1},{1,0},{2,3},{3,2},{4,5},{5,4},{6,7},{7,6},{8,9},{9,8},{10,11... | collective-permute-start | bytes 1081352 | tf_op jit(solution)/shard_map/ppermute | solution.py:24
  138.9 1.5 collective-permute-start.20
  145.3 1.8 %collective-permute-done.19.refs_3_ = bf16[2,11,64,128]{3,2,1,0:T(8,128)(2,1)} collective-permute-done((bf16[2,11,64,128]{3,2,1,0:T(8,128)(2,1)}, bf16[2,11,64,128]{3,2,1,0:T(8,128)(2,1)}, u32[]{:S(2)}, u32[]{:S(2)}) %collective-permute-start.19) | collective-permute-done | bytes 360480 | tf_op jit(solution)/shard_map/ppermute | solution.py:24
  147.1 3.4 %collective-permute-done.20.refs_4_ = bf16[2,11,64,128]{3,2,1,0:T(8,128)(2,1)} collective-permute-done((bf16[2,11,64,128]{3,2,1,0:T(8,128)(2,1)}, bf16[2,11,64,128]{3,2,1,0:T(8,128)(2,1)}, u32[]{:S(2)}, u32[]{:S(2)}) %collective-permute-start.20) | collective-permute-done | bytes 360480 | tf_op jit(solution)/shard_map/ppermute | solution.py:24
  150.5 2.8 %join_b.1 = (bf16[16,64,2048]{2,1,0:T(8,128)(2,1)}, bf16[64,2048]{1,0:T(8,128)(2,1)}) custom-call(s32[1]{0:T(128)} %bitcast.me_ref, bf16[4,11,64,128]{3,2,1,0:T(8,128)(2,1)S(1)} %get-tuple-element.21.refs_0_, bf16[4,11,64,128]{3,2,1,0:T(8,128)(2,1)S(1)} %collective-permute-done.17.refs_1_, ...), custom_call_target="tpu_custom_call", output_to_operand_aliasing={{0}: (6, {})} | custom-call | flops 8000000 | bytes 2097152 | tf_op jit(solution)/shard_map/join_b/pallas_call | solution.py:269
  153.3 2.0 %join.4.refs_1_ = bf16[16,64,2048]{2,1,0:T(8,128)(2,1)} custom-call(s32[1]{0:T(128)} %bitcast.me_ref, bf16[2,6,64,128]{3,2,1,0:T(8,128)(2,1)S(1)} %get-tuple-element.30.refs_0_, bf16[2,6,64,128]{3,2,1,0:T(8,128)(2,1)S(1)} %collective-permute-done.10.refs_1_, ...), custom_call_target="tpu_custom_call", output_to_operand_aliasing={{}: (6, {})} | custom-call | flops 6000000 | bytes 1572864 | tf_op jit(solution)/shard_map/join/pallas_call | solution.py:204
  155.4 6.3 %collective-permute-done.8.refs_0_ = bf16[8,7,64,128]{3,2,1,0:T(8,128)(2,1)} collective-permute-done((bf16[8,7,64,128]{3,2,1,0:T(8,128)(2,1)}, bf16[8,7,64,128]{3,2,1,0:T(8,128)(2,1)}, u32[]{:S(2)}, u32[]{:S(2)}) %collective-permute-start.8) | collective-permute-done | bytes 917536 | tf_op jit(solution)/shard_map/ppermute | solution.py:24
  161.7 2.3 %join.5 = bf16[16,64,2048]{2,1,0:T(8,128)(2,1)} custom-call(s32[1]{0:T(128)} %bitcast.me_ref, bf16[8,7,64,128]{3,2,1,0:T(8,128)(2,1)} %collective-permute-done.8.refs_0_, bf16[16,64,2048]{2,1,0:T(8,128)(2,1)} %join.4.refs_1_), custom_call_target="tpu_custom_call", output_to_operand_aliasing={{}: (2, {})} | custom-call | flops 7000000 | bytes 1835008 | tf_op jit(solution)/shard_map/join/pallas_call | solution.py:204
  (89 shorter events, 28.0 us)
Async XLA Ops:
  0.6 28.2 %copy-start.9 = (f32[128,16]{0,1:T(8,128)S(1)}, f32[128,16]{0,1:T(8,128)}, u32[]{:S(2)}) copy-start(f32[128,16]{0,1:T(8,128)} %param.4) | copy-start | bytes 24580
  0.6 28.1 %copy-start.10 = (f32[128]{0:T(128)S(1)}, f32[128]{0:T(128)}, u32[]{:S(2)}) copy-start(f32[128]{0:T(128)} %param.5) | copy-start | bytes 1540
  6.3 4.4 %collective-permute-start = (f32[16,8,128]{2,1,0:T(8,128)S(1)}, f32[16,8,128]{2,1,0:T(8,128)S(1)}, u32[]{:S(2)}, u32[]{:S(2)}) collective-permute-start(f32[16,8,128]{2,1,0:T(8,128)S(1)} %bitcast.16), channel_id=1, source_target_pairs={{0,1},{1,0},{2,3},{3,2},{4,5},{5,4},{6,7},{7,6},{8,9},{9,8},{10,11... | collective-permute-start | bytes 196616 | tf_op jit(solution)/shard_map/ppermute | solution.py:24
  10.7 5.9 %collective-permute-start.1 = (f32[16,8,128]{2,1,0:T(8,128)S(1)}, f32[16,8,128]{2,1,0:T(8,128)S(1)}, u32[]{:S(2)}, u32[]{:S(2)}) collective-permute-start(f32[16,8,128]{2,1,0:T(8,128)S(1)} %bitcast_add_fusion), channel_id=1, source_target_pairs={{0,2},{1,3},{2,0},{3,1},{4,6},{5,7},{6,4},{7,5},{8,10},{9,11},{10,... | collective-permute-start | bytes 196616 | tf_op jit(solution)/shard_map/ppermute | solution.py:24
  16.5 5.9 %collective-permute-start.2 = (f32[16,8,128]{2,1,0:T(8,128)S(1)}, f32[16,8,128]{2,1,0:T(8,128)S(1)}, u32[]{:S(2)}, u32[]{:S(2)}) collective-permute-start(f32[16,8,128]{2,1,0:T(8,128)S(1)} %add.16), channel_id=1, source_target_pairs={{0,4},{1,5},{2,6},{3,7},{4,0},{5,1},{6,2},{7,3},{8,12},{9,13},{10,... | collective-permute-start | bytes 196616 | tf_op jit(solution)/shard_map/ppermute | solution.py:24
  22.4 20.6 %collective-permute-start.3 = (f32[16,8,128]{2,1,0:T(8,128)S(1)}, f32[16,8,128]{2,1,0:T(8,128)S(1)}, u32[]{:S(2)}, u32[]{:S(2)}) collective-permute-start(f32[16,8,128]{2,1,0:T(8,128)S(1)} %add.17), channel_id=1, source_target_pairs={{0,8},{1,9},{2,10},{3,11},{4,12},{5,13},{6,14},{7,15},{8,0},{9,1},... | collective-permute-start | bytes 196616 | tf_op jit(solution)/shard_map/ppermute | solution.py:24
  29.4 12.2 %all-to-all-start = ((bf16[4,16,128]{2,1,0:T(8,128)(2,1)}), bf16[4,16,128]{2,1,0:T(8,128)(2,1)S(1)}, u32[]{:S(2)}, u32[]{:S(2)}) async-start(bf16[4,16,128]{2,1,0:T(8,128)(2,1)} %broadcast_in_dim.2), calls=%async_computation | async-start | bytes 32768 | tf_op jit(solution)/shard_map/all_to_all | solution.py:307
  35.7 46.8 %collective-permute-start.15 = (f32[8,2,64,128]{3,2,1,0:T(8,128)}, f32[8,2,64,128]{3,2,1,0:T(8,128)S(1)}, u32[]{:S(2)}, u32[]{:S(2)}) collective-permute-start(f32[8,2,64,128]{3,2,1,0:T(8,128)} %get-tuple-element.19), channel_id=1, source_target_pairs={{0,8},{1,9},{2,10},{3,11},{4,12},{5,13},{6,14},{7,15},{8,0},{9,1},... | collective-permute-start | bytes 1572872 | tf_op jit(solution)/shard_map/ppermute | solution.py:24
  37.1 45.3 %collective-permute-start.16 = (f32[8,1,64,128]{3,2,1,0:T(8,128)}, f32[8,1,64,128]{3,2,1,0:T(8,128)S(1)}, u32[]{:S(2)}, u32[]{:S(2)}) collective-permute-start(f32[8,1,64,128]{3,2,1,0:T(8,128)} %get-tuple-element.20), channel_id=1, source_target_pairs={{0,8},{1,9},{2,10},{3,11},{4,12},{5,13},{6,14},{7,15},{8,0},{9,1},... | collective-permute-start | bytes 786440 | tf_op jit(solution)/shard_map/ppermute | solution.py:24
  41.6 40.2 %collective-permute-start.14 = (bf16[64,128]{1,0:T(8,128)(2,1)S(1)}, bf16[64,128]{1,0:T(8,128)(2,1)S(1)}, u32[]{:S(2)}, u32[]{:S(2)}) collective-permute-start(bf16[64,128]{1,0:T(8,128)(2,1)S(1)} %bitcast.13), channel_id=1, source_target_pairs={{0,8},{1,9},{2,10},{3,11},{4,12},{5,13},{6,14},{7,15},{8,0},{9,1},... | collective-permute-start | bytes 49160 | tf_op jit(solution)/shard_map/ppermute | solution.py:24
  48.8 33.6 %slice-start = ((s8[8388608]{0:T(1024)(128)(4,1)}), s8[4194304]{0:T(1024)(128)(4,1)S(1)}, s32[]{:S(2)}) async-start(s8[8388608]{0:T(1024)(128)(4,1)} %bitcast.11), calls=%async_computation.1 | async-start | bytes 8388608
  50.1 32.4 %slice-start.1 = ((s8[8388608]{0:T(1024)(128)(4,1)}), s8[4194304]{0:T(1024)(128)(4,1)S(1)}, s32[]{:S(2)}) async-start(s8[8388608]{0:T(1024)(128)(4,1)} %bitcast.11), calls=%async_computation.2 | async-start | bytes 8388608
  51.5 35.6 %collective-permute-start.21 = (bf16[4,10,64,128]{3,2,1,0:T(8,128)(2,1)S(1)}, bf16[4,10,64,128]{3,2,1,0:T(8,128)(2,1)S(1)}, u32[]{:S(2)}, u32[]{:S(2)}) collective-permute-start(bf16[4,10,64,128]{3,2,1,0:T(8,128)(2,1)S(1)} %get-tuple-element.24), channel_id=1, source_target_pairs={{0,4},{1,5},{2,6},{3,7},{4,0},{5,1},{6,2},{7,3},{8,12},{9,13},{10,... | collective-permute-start | bytes 1966088 | tf_op jit(solution)/shard_map/ppermute | solution.py:24
  54.8 8.4 %collective-permute-start.4 = (bf16[2,7,64,128]{3,2,1,0:T(8,128)(2,1)S(1)}, bf16[2,7,64,128]{3,2,1,0:T(8,128)(2,1)S(1)}, u32[]{:S(2)}, u32[]{:S(2)}) collective-permute-start(bf16[2,7,64,128]{3,2,1,0:T(8,128)(2,1)S(1)} %get-tuple-element.16), channel_id=1, source_target_pairs={{0,1},{1,0},{2,3},{3,2},{4,5},{5,4},{6,7},{7,6},{8,9},{9,8},{10,11... | collective-permute-start | bytes 688136 | tf_op jit(solution)/shard_map/ppermute | solution.py:24
  63.2 7.5 %collective-permute-start.5 = (bf16[2,7,64,128]{3,2,1,0:T(8,128)(2,1)S(1)}, bf16[2,7,64,128]{3,2,1,0:T(8,128)(2,1)S(1)}, u32[]{:S(2)}, u32[]{:S(2)}) collective-permute-start(bf16[2,7,64,128]{3,2,1,0:T(8,128)(2,1)S(1)} %get-tuple-element.17), channel_id=1, source_target_pairs={{0,2},{1,3},{2,0},{3,1},{4,6},{5,7},{6,4},{7,5},{8,10},{9,11},{10,... | collective-permute-start | bytes 688136 | tf_op jit(solution)/shard_map/ppermute | solution.py:24
  70.7 6.0 %collective-permute-start.6 = (bf16[2,7,64,128]{3,2,1,0:T(8,128)(2,1)S(1)}, bf16[2,7,64,128]{3,2,1,0:T(8,128)(2,1)S(1)}, u32[]{:S(2)}, u32[]{:S(2)}) collective-permute-start(bf16[2,7,64,128]{3,2,1,0:T(8,128)(2,1)S(1)} %get-tuple-element.18), channel_id=1, source_target_pairs={{0,3},{1,2},{2,1},{3,0},{4,7},{5,6},{6,5},{7,4},{8,11},{9,10},{10,... | collective-permute-start | bytes 688136 | tf_op jit(solution)/shard_map/ppermute | solution.py:24
  76.8 33.8 %collective-permute-start.9 = (bf16[8,6,64,128]{3,2,1,0:T(8,128)(2,1)S(1)}, bf16[8,6,64,128]{3,2,1,0:T(8,128)(2,1)S(1)}, u32[]{:S(2)}, u32[]{:S(2)}) collective-permute-start(bf16[8,6,64,128]{3,2,1,0:T(8,128)(2,1)S(1)} %spread.4), channel_id=1, source_target_pairs={{0,8},{1,9},{2,10},{3,11},{4,12},{5,13},{6,14},{7,15},{8,0},{9,1},... | collective-permute-start | bytes 2359304 | tf_op jit(solution)/shard_map/ppermute | solution.py:24
  81.8 32.4 %collective-permute-start.7 = (bf16[4,7,64,128]{3,2,1,0:T(8,128)(2,1)S(1)}, bf16[4,7,64,128]{3,2,1,0:T(8,128)(2,1)S(1)}, u32[]{:S(2)}, u32[]{:S(2)}) collective-permute-start(bf16[4,7,64,128]{3,2,1,0:T(8,128)(2,1)S(1)} %pad_maximum_fusion), channel_id=1, source_target_pairs={{0,4},{1,5},{2,6},{3,7},{4,0},{5,1},{6,2},{7,3},{8,12},{9,13},{10,... | collective-permute-start | bytes 1376264 | tf_op jit(solution)/shard_map/ppermute | solution.py:24
  83.7 47.6 %collective-permute-start.17 = (bf16[4,11,64,128]{3,2,1,0:T(8,128)(2,1)S(1)}, bf16[4,11,64,128]{3,2,1,0:T(8,128)(2,1)S(1)}, u32[]{:S(2)}, u32[]{:S(2)}) collective-permute-start(bf16[4,11,64,128]{3,2,1,0:T(8,128)(2,1)S(1)} %get-tuple-element.22), channel_id=1, source_target_pairs={{0,4},{1,5},{2,6},{3,7},{4,0},{5,1},{6,2},{7,3},{8,12},{9,13},{10,... | collective-permute-start | bytes 2162696 | tf_op jit(solution)/shard_map/ppermute | solution.py:24
  110.6 7.9 %collective-permute-start.10 = (bf16[2,6,64,128]{3,2,1,0:T(8,128)(2,1)S(1)}, bf16[2,6,64,128]{3,2,1,0:T(8,128)(2,1)S(1)}, u32[]{:S(2)}, u32[]{:S(2)}) collective-permute-start(bf16[2,6,64,128]{3,2,1,0:T(8,128)(2,1)S(1)} %get-tuple-element.29), channel_id=1, source_target_pairs={{0,1},{1,0},{2,3},{3,2},{4,5},{5,4},{6,7},{7,6},{8,9},{9,8},{10,11... | collective-permute-start | bytes 589832 | tf_op jit(solution)/shard_map/ppermute | solution.py:24
  110.7 9.5 %collective-permute-start.11 = (bf16[2,6,64,128]{3,2,1,0:T(8,128)(2,1)S(1)}, bf16[2,6,64,128]{3,2,1,0:T(8,128)(2,1)S(1)}, u32[]{:S(2)}, u32[]{:S(2)}) collective-permute-start(bf16[2,6,64,128]{3,2,1,0:T(8,128)(2,1)S(1)} %get-tuple-element.28), channel_id=1, source_target_pairs={{0,2},{1,3},{2,0},{3,1},{4,6},{5,7},{6,4},{7,5},{8,10},{9,11},{10,... | collective-permute-start | bytes 589832 | tf_op jit(solution)/shard_map/ppermute | solution.py:24
  110.8 13.6 %collective-permute-start.12 = (bf16[2,6,64,128]{3,2,1,0:T(8,128)(2,1)S(1)}, bf16[2,6,64,128]{3,2,1,0:T(8,128)(2,1)S(1)}, u32[]{:S(2)}, u32[]{:S(2)}) collective-permute-start(bf16[2,6,64,128]{3,2,1,0:T(8,128)(2,1)S(1)} %get-tuple-element.27), channel_id=1, source_target_pairs={{0,3},{1,2},{2,1},{3,0},{4,7},{5,6},{6,5},{7,4},{8,11},{9,10},{10,... | collective-permute-start | bytes 589832 | tf_op jit(solution)/shard_map/ppermute | solution.py:24
  114.3 19.9 %collective-permute-start.22 = (bf16[2,10,64,128]{3,2,1,0:T(8,128)(2,1)S(1)}, bf16[2,10,64,128]{3,2,1,0:T(8,128)(2,1)S(1)}, u32[]{:S(2)}, u32[]{:S(2)}) collective-permute-start(bf16[2,10,64,128]{3,2,1,0:T(8,128)(2,1)S(1)} %pad_maximum_fusion.5), channel_id=1, source_target_pairs={{0,1},{1,0},{2,3},{3,2},{4,5},{5,4},{6,7},{7,6},{8,9},{9,8},{10,11... | collective-permute-start | bytes 983048 | tf_op jit(solution)/shard_map/ppermute | solution.py:24
  118.5 18.2 %collective-permute-start.23 = (bf16[2,10,64,128]{3,2,1,0:T(8,128)(2,1)S(1)}, bf16[2,10,64,128]{3,2,1,0:T(8,128)(2,1)S(1)}, u32[]{:S(2)}, u32[]{:S(2)}) collective-permute-start(bf16[2,10,64,128]{3,2,1,0:T(8,128)(2,1)S(1)} %pad_maximum_fusion.6), channel_id=1, source_target_pairs={{0,2},{1,3},{2,0},{3,1},{4,6},{5,7},{6,4},{7,5},{8,10},{9,11},{10,... | collective-permute-start | bytes 983048 | tf_op jit(solution)/shard_map/ppermute | solution.py:24
  120.2 17.9 %collective-permute-start.24 = (bf16[2,10,64,128]{3,2,1,0:T(8,128)(2,1)S(1)}, bf16[2,10,64,128]{3,2,1,0:T(8,128)(2,1)S(1)}, u32[]{:S(2)}, u32[]{:S(2)}) collective-permute-start(bf16[2,10,64,128]{3,2,1,0:T(8,128)(2,1)S(1)} %pad_maximum_fusion.7), channel_id=1, source_target_pairs={{0,3},{1,2},{2,1},{3,0},{4,7},{5,6},{6,5},{7,4},{8,11},{9,10},{10,... | collective-permute-start | bytes 983048 | tf_op jit(solution)/shard_map/ppermute | solution.py:24
  124.4 6.9 %copy-start.1 = (bf16[2,6,64,128]{3,2,1,0:T(8,128)(2,1)}, bf16[2,6,64,128]{3,2,1,0:T(8,128)(2,1)S(1)}, u32[]{:S(2)}) copy-start(bf16[2,6,64,128]{3,2,1,0:T(8,128)(2,1)S(1)} %collective-permute-done.12.refs_3_) | copy-start | bytes 589828
  124.4 37.3 %collective-permute-start.8 = (bf16[8,7,64,128]{3,2,1,0:T(8,128)(2,1)}, bf16[8,7,64,128]{3,2,1,0:T(8,128)(2,1)}, u32[]{:S(2)}, u32[]{:S(2)}) collective-permute-start(bf16[8,7,64,128]{3,2,1,0:T(8,128)(2,1)} %constant_dynamic-update-slice_fusion), channel_id=1, source_target_pairs={{0,8},{1,9},{2,10},{3,11},{4,12},{5,13},{6,14},{7,15},{8,0},{9,1},... | collective-permute-start | bytes 2752520 | tf_op jit(solution)/shard_map/ppermute | solution.py:24
  131.3 22.1 %collective-permute-start.13 = (bf16[4,6,64,128]{3,2,1,0:T(8,128)(2,1)}, bf16[4,6,64,128]{3,2,1,0:T(8,128)(2,1)}, u32[]{:S(2)}, u32[]{:S(2)}) collective-permute-start(bf16[4,6,64,128]{3,2,1,0:T(8,128)(2,1)} %pad_maximum_fusion.1), channel_id=1, source_target_pairs={{0,4},{1,5},{2,6},{3,7},{4,0},{5,1},{6,2},{7,3},{8,12},{9,13},{10,... | collective-permute-start | bytes 1179656 | tf_op jit(solution)/shard_map/ppermute | solution.py:24
  134.9 10.4 %collective-permute-start.18 = (bf16[2,11,64,128]{3,2,1,0:T(8,128)(2,1)}, bf16[2,11,64,128]{3,2,1,0:T(8,128)(2,1)}, u32[]{:S(2)}, u32[]{:S(2)}) collective-permute-start(bf16[2,11,64,128]{3,2,1,0:T(8,128)(2,1)} %pad_maximum_fusion.2), channel_id=1, source_target_pairs={{0,1},{1,0},{2,3},{3,2},{4,5},{5,4},{6,7},{7,6},{8,9},{9,8},{10,11... | collective-permute-start | bytes 1081352 | tf_op jit(solution)/shard_map/ppermute | solution.py:24
  137.4 9.6 %collective-permute-start.19 = (bf16[2,11,64,128]{3,2,1,0:T(8,128)(2,1)}, bf16[2,11,64,128]{3,2,1,0:T(8,128)(2,1)}, u32[]{:S(2)}, u32[]{:S(2)}) collective-permute-start(bf16[2,11,64,128]{3,2,1,0:T(8,128)(2,1)} %pad_maximum_fusion.3), channel_id=1, source_target_pairs={{0,2},{1,3},{2,0},{3,1},{4,6},{5,7},{6,4},{7,5},{8,10},{9,11},{10,... | collective-permute-start | bytes 1081352 | tf_op jit(solution)/shard_map/ppermute | solution.py:24
  138.9 11.6 %collective-permute-start.20 = (bf16[2,11,64,128]{3,2,1,0:T(8,128)(2,1)}, bf16[2,11,64,128]{3,2,1,0:T(8,128)(2,1)}, u32[]{:S(2)}, u32[]{:S(2)}) collective-permute-start(bf16[2,11,64,128]{3,2,1,0:T(8,128)(2,1)} %pad_maximum_fusion.4), channel_id=1, source_target_pairs={{0,3},{1,2},{2,1},{3,0},{4,7},{5,6},{6,5},{7,4},{8,11},{9,10},{10,... | collective-permute-start | bytes 1081352 | tf_op jit(solution)/shard_map/ppermute | solution.py:24
  145.3 8.1 %copy-start.2 = (bf16[2,6,64,128]{3,2,1,0:T(8,128)(2,1)S(1)}, bf16[2,6,64,128]{3,2,1,0:T(8,128)(2,1)}, u32[]{:S(2)}) copy-start(bf16[2,6,64,128]{3,2,1,0:T(8,128)(2,1)} %copy-done.1) | copy-start | bytes 589828
  (7 other events, 8.5 us)
